TPU v7x, 8 devices: a whole 2x2x1 slice. The times are simulated.
8 devices in a mesh: w: 2 (over z, y), h: 4 (over x, core).
Axes of the slice: x: 2, y: 2, z: 1, core: 2. Of those that a mesh axis runs over, the one named last changes fastest.
Arguments:
- x: bfloat16 [1, 64, 512, 640], P(None, 'h', 'w')
- w1: bfloat16 [3, 3, 640, 640], replicated
- gamma: float32 [640], replicated
- beta: float32 [640], replicated
- w2: bfloat16 [3, 3, 640, 640], replicated
- g: bfloat16 [1, 64, 512, 640], P(None, 'h', 'w')
Outputs:
- output 1: bfloat16 [1, 64, 512, 640], P(None, 'h', 'w')
- output 2: bfloat16 [1, 64, 512, 640], P(None, 'h', 'w')
- output 3: float32 [3, 3, 640, 640], replicated
- output 4: float32 [3, 3, 640, 640], replicated
- output 5: float32 [640], replicated
- output 6: float32 [640], replicated
All inputs are finite; a program needn't handle non-finite values.
Results may differ from a plain program's by a relative error of at most 0.00136865.
Values are sent between devices in bfloat16 or wider.
A program may use at most 1 GiB of HBM per device.

v0:
```python
import jax
import jax.numpy as jnp
from jax import lax
from jax.sharding import PartitionSpec as P

GROUPS = 32
EPS = 1e-5
DN = ('NHWC', 'HWIO', 'NHWC')


def _conv(up, w):
    return lax.conv_general_dilated(up, w, (1, 1), 'VALID', dimension_numbers=DN, preferred_element_type=jnp.float32)


def _flip_t(w):
    return jnp.flip(w, (0, 1)).transpose(0, 1, 3, 2)


def _wgrad(up, v):
    th, tw = v.shape[1], v.shape[2]
    return jnp.stack([jnp.stack([jnp.einsum('bhwc,bhwo->co', up[:, a:a + th, b:b + tw], v, preferred_element_type=jnp.float32) for b in range(3)]) for a in range(3)])


def _edge(u, axis, name, n):
    lo = lax.slice_in_dim(u, 0, 1, axis=axis)
    hi = lax.slice_in_dim(u, u.shape[axis] - 1, u.shape[axis], axis=axis)
    if n == 1:
        prev = jnp.zeros_like(lo)
        nxt = jnp.zeros_like(lo)
    else:
        prev = lax.ppermute(hi, name, [(i, i + 1) for i in range(n - 1)])
        nxt = lax.ppermute(lo, name, [(i + 1, i) for i in range(n - 1)])
    return jnp.concatenate([prev, u, nxt], axis=axis)


def solution(mesh):
    nh, nw = mesh.shape['h'], mesh.shape['w']
    tile = P(None, 'h', 'w', None)

    def halo(u):
        return _edge(_edge(u, 1, 'h', nh), 2, 'w', nw)

    def body(x, w1, gamma, beta, w2, g):
        nb, th, tw, c = x.shape
        cg = c // GROUPS
        cnt = th * nh * tw * nw * cg
        xp = halo(x)
        a = _conv(xp, w1).astype(jnp.bfloat16).astype(jnp.float32)
        s = jnp.stack([a.sum((1, 2)), (a * a).sum((1, 2))])
        s = lax.psum(s.reshape(2, nb, GROUPS, cg).sum(-1), ('h', 'w')) / cnt
        rstd_g = lax.rsqrt(s[1] - s[0] * s[0] + EPS)
        mean = jnp.repeat(s[0], cg, axis=-1)[:, None, None, :]
        rstd = jnp.repeat(rstd_g, cg, axis=-1)[:, None, None, :]
        xhatv = (a - mean) * rstd
        zf, gelu_vjp = jax.vjp(lambda n: jax.nn.gelu(n, approximate=True), xhatv * gamma + beta)
        z = zf.astype(jnp.bfloat16)
        zp = halo(z)
        y = (_conv(zp, w2) + x.astype(jnp.float32)).astype(jnp.bfloat16)
        gp = halo(g)
        dz = _conv(gp, _flip_t(w2))
        dw2 = lax.psum(_wgrad(zp, g), ('h', 'w'))
        (dn,) = gelu_vjp(dz)
        t = lax.psum(jnp.stack([(dn * xhatv).sum((1, 2)), dn.sum((1, 2))]), ('h', 'w'))
        dgamma = t[0].sum(0)
        dbeta = t[1].sum(0)
        u = jnp.repeat((t * gamma).reshape(2, nb, GROUPS, cg).sum(-1) / cnt, cg, axis=-1)[:, :, None, None, :]
        da = (rstd * (dn * gamma - u[1] - xhatv * u[0])).astype(jnp.bfloat16)
        dap = halo(da)
        dx = (_conv(dap, _flip_t(w1)) + g.astype(jnp.float32)).astype(jnp.bfloat16)
        dw1 = lax.psum(_wgrad(xp, da), ('h', 'w'))
        return y, dx, dw1, dw2, dgamma, dbeta

    return jax.shard_map(body, mesh=mesh, in_specs=(tile, P(), P(), P(), P(), tile), out_specs=(tile, tile, P(), P(), P(), P()), check_vma=False)
```

profile of v0, /device:TPU:0, one launch (start us, length us, event | category | flops | bytes accessed | tf_op | source)
XLA Modules:
  0.0 921.4 jit_solution(8114820154502949133)
XLA Ops:
  7.2 7.8 copy.52
  22.8 5.2 collective-permute-start.8
  44.2 5.1 collective-permute-start.2
  56.4 4.5 collective-permute-start.10
  66.6 11.1 %maximum_bitcast_fusion = bf16[18,1,258,640]{2,3,0,1:T(8,128)(2,1)} fusion(bf16[1,18,1,640]{2,3,1,0:T(8,128)(2,1)S(1)} %copy.58, bf16[1,1,256,640]{2,3,1,0:T(8,128)(2,1)} %copy-done.9, bf16[1,16,256,640]{2,3,1,0:T(8,128)(2,1)} %copy.52, bf16[1,1,256,640]{2,3,1,0:T(8,128)(2,1)S(1)} %collective-permute-done, bf16[1,18,1,640]{2,3,1,0:T(8,128)(2,1)} %copy.57), kind=kLoop, calls=%fused_computation.44 | loop fusion | flops 29721600 | bytes 11888640 | tf_op jit(solution)/shard_map/concatenate | solution.py:33
  77.7 10.2 %copy.104 = bf16[18,1,258,640]{3,2,0,1:T(8,128)(2,1)} copy(bf16[18,1,258,640]{2,3,0,1:T(8,128)(2,1)} %maximum_bitcast_fusion) | data formatting | bytes 11888640
  87.9 5.8 pad.clone
  93.7 9.1 reshape.184
  102.7 3.9 copy.61
  106.8 44.9 %fusion.10 = (f32[640]{0:T(1024)S(1)}, f32[640]{0:T(1024)S(1)}, bf16[16,8,33,640]{3,1,2,0:T(8,128)(2,1)}) fusion(pred[8,33]{0,1:T(8,128)(4,1)S(1)} %copy-done.26, bf16[3,3,640,640]{3,2,1,0:T(8,128)(2,1)} %param.7, bf16[18,1,7,2,640]{4,2,3,0,1:T(8,128)(2,1)S(1)} %slice.200, bf16[18,1,8,33,640]{4,2,3,0,1:T(8,128)(2,1)S(1)} %copy.61), kind=kOutput, calls=%fused_computation.18 | convolution fusion | flops 31183687680 | bytes 19190024 | tf_op jit(solution)/shard_map/conv_general_dilated | solution.py:12
  152.0 22.3 %psum.28 = f32[2,1,32]{2,0,1:T(2,128)S(1)} all-reduce(f32[2,1,32]{2,0,1:T(2,128)S(1)} %bitcast.349), channel_id=1, replica_groups=mesh['w'=2,'h'=4] {'h','w'}, use_global_device_ids=true, to_apply=%region_3.0 | all-reduce | flops 64 | bytes 512 | tf_op jit(solution)/shard_map/psum | solution.py:50
  174.6 4.5 maximum_bitcast_fusion.2
  182.2 9.1 reshape.202
  191.3 3.9 copy.78
  195.3 57.3 %fusion.27 = (f32[640]{0:T(1024)S(1)}, f32[640]{0:T(1024)S(1)}, f32[16,8,33,640]{3,1,2,0:T(8,128)}) fusion(bf16[16,8,33,640]{3,1,2,0:T(8,128)(2,1)} %get-tuple-element.50, f32[640]{0:T(1024)S(1)} %broadcast_in_dim.26, f32[640]{0:T(1024)S(1)} %broadcast_in_dim.24, pred[8,33]{0,1:T(8,128)(4,1)S(1)} %copy-done.26, f32[640]{0:T(1024)S(1)} %copy-done.25, ...), kind=kOutput, calls=%fused_computation.35 | convolution fusion | flops 31243161600 | bytes 30013704 | tf_op jit(solution)/shard_map/conv_general_dilated | solution.py:12
  252.6 24.8 %psum.29 = f32[2,1,640]{2,0,1:T(2,128)S(1)} all-reduce(f32[2,1,640]{2,0,1:T(2,128)S(1)} %pad_maximum_fusion.13), channel_id=1, replica_groups=mesh['w'=2,'h'=4] {'h','w'}, use_global_device_ids=true, to_apply=%region_6.7 | all-reduce | flops 1280 | bytes 10240 | tf_op jit(solution)/shard_map/psum | solution.py:63
  278.0 10.0 %fusion.25 = (bf16[16,8,33,640]{3,1,2,0:T(8,128)(2,1)S(1)}, bf16[16,8,33,640]{3,1,2,0:T(8,128)(2,1)S(1)}) fusion(bf16[16,8,33,640]{3,1,2,0:T(8,128)(2,1)} %get-tuple-element.50, f32[16,8,33,640]{3,1,2,0:T(8,128)} %get-tuple-element.51, f32[640]{0:T(1024)S(1)} %broadcast_in_dim.28, f32[640]{0:T(1024)S(1)} %broadcast_in_dim.30, f32[640]{0:T(1024)S(1)} %copy-done.24, ...), kind=kLoop, calls=%fused_computation.33 | loop fusion | flops 54067200 | bytes 27048960 | tf_op jit(solution)/shard_map/convert_element_type | solution.py:67
  296.6 9.8 %maximum_maximum_fusion = (bf16[1,18,257,640]{2,3,1,0:T(8,128)(2,1)}, bf16[1,18,257,640]{2,3,1,0:T(8,128)(2,1)}) fusion(bf16[1,1,256,640]{2,3,1,0:T(8,128)(2,1)S(1)} %copy-done.10, bf16[1,16,256,640]{2,3,1,0:T(8,128)(2,1)S(1)} %bitcast.323, bf16[1,1,256,640]{2,3,1,0:T(8,128)(2,1)S(1)} %copy-done.8, bf16[1,18,1,640]{2,3,1,0:T(8,128)(2,1)S(1)} %copy-done.2, ...), kind=kLoop, calls=%fused_computation.46 | loop fusion | flops 47370240 | bytes 17786880 | tf_op jit(solution)/shard_map/concatenate | solution.py:33
  306.4 9.4 %fusion.167 = f32[1,640,640]{2,1,0:T(8,128)} fusion(bf16[1,18,257,640]{2,3,1,0:T(8,128)(2,1)} %get-tuple-element.29, bf16[16,1,256,640]{3,0,2,1:T(8,128)(2,1)S(1)} %slice.215), kind=kOutput, calls=%fused_computation.163 | convolution fusion | flops 3355443200 | bytes 12124160 | tf_op jit(solution)/shard_map/bhwc,bhwo->co/dot_general | solution.py:21
  315.8 8.5 fusion.155
  324.3 5.4 fusion.164
  329.8 5.4 fusion.152
  335.2 9.3 %fusion.161 = f32[1,640,640]{2,1,0:T(8,128)} fusion(bf16[1,18,257,640]{2,3,1,0:T(8,128)(2,1)} %get-tuple-element.29, bf16[16,1,256,640]{3,0,2,1:T(8,128)(2,1)S(1)} %slice.215), kind=kOutput, calls=%fused_computation.161 | convolution fusion | flops 3355443200 | bytes 12124160 | tf_op jit(solution)/shard_map/bhwc,bhwo->co/dot_general | solution.py:21
  344.5 6.3 fusion.142
  350.8 5.4 fusion.158
  357.9 5.3 slice.203
  363.2 8.3 copy.101
  387.5 9.5 %fusion.147 = f32[1,640,640]{2,1,0:T(8,128)} fusion(bf16[1,16,256,640]{3,2,1,0:T(8,128)(2,1)} %param.11, bf16[16,1,256,640]{2,3,0,1:T(8,128)(2,1)} %copy.101), kind=kOutput, calls=%fused_computation.157 | convolution fusion | flops 3355443200 | bytes 12124160 | tf_op jit(solution)/shard_map/bhwc,bhwo->co/dot_general | solution.py:21
  397.1 4.3 fusion.127
  403.9 4.3 fusion.122
  408.2 4.6 maximum_bitcast_fusion.4
  412.8 11.7 %pad_maximum_fusion = f32[3,3,640,640]{3,2,1,0:T(8,128)} fusion(f32[1,3,640,640]{3,2,1,0:T(8,128)} %maximum_bitcast_fusion.6, f32[1,3,640,640]{3,2,1,0:T(8,128)} %get-tuple-element.55, f32[1,3,640,640]{3,2,1,0:T(8,128)} %get-tuple-element.54), kind=kLoop, calls=%fused_computation.5 | loop fusion | flops 7372800 | bytes 29491200 | tf_op jit(solution)/shard_map/stack | solution.py:21
  424.6 6.1 copy.145
  431.6 5.2 collective-permute-start.12
  451.7 4.5 collective-permute-start.6
  459.3 6.0 collective-permute-start.14
  465.3 9.3 %fusion.137 = f32[1,640,640]{2,1,0:T(8,128)} fusion(bf16[1,16,256,640]{3,2,1,0:T(8,128)(2,1)} %param.11, bf16[1,1,256,640]{2,3,1,0:T(8,128)(2,1)S(1)} %collective-permute-done.5, bf16[1,16,256,640]{2,3,1,0:T(8,128)(2,1)} %bitcast.327), kind=kOutput, calls=%fused_computation.155 | convolution fusion | flops 3358064640 | bytes 12451840 | tf_op jit(solution)/shard_map/bhwc,bhwo->co/dot_general | solution.py:21
  474.7 5.4 fusion.132
  485.0 10.8 %maximum_maximum_fusion.1 = (bf16[1,18,257,640]{2,3,1,0:T(8,128)(2,1)S(1)}, bf16[1,18,257,640]{2,3,1,0:T(8,128)(2,1)S(1)}) fusion(bf16[1,1,256,640]{2,3,1,0:T(8,128)(2,1)S(1)} %collective-permute-done.5, bf16[1,16,256,640]{2,3,1,0:T(8,128)(2,1)} %bitcast.328, bf16[1,1,256,640]{2,3,1,0:T(8,128)(2,1)} %copy-done.11, bf16[1,18,1,640]{2,3,1,0:T(8,128)(2,1)} %copy.70, ...), kind=kLoop, calls=%fused_computation.48 | loop fusion | flops 47370240 | bytes 17786880 | tf_op jit(solution)/shard_map/concatenate | solution.py:33
  495.7 7.1 fusion.185
  502.9 7.1 fusion.179
  510.0 5.4 fusion.182
  515.3 4.6 fusion.176
  520.0 4.4 fusion.173
  524.4 4.2 fusion.170
  536.5 11.7 %pad_maximum_fusion.1 = f32[3,3,640,640]{3,2,1,0:T(8,128)} fusion(f32[1,3,640,640]{3,2,1,0:T(8,128)} %maximum_bitcast_fusion.9, f32[1,3,640,640]{3,2,1,0:T(8,128)} %maximum_bitcast_fusion.8, f32[1,3,640,640]{3,2,1,0:T(8,128)} %maximum_bitcast_fusion.7), kind=kLoop, calls=%fused_computation.6 | loop fusion | flops 7372800 | bytes 29491200 | tf_op jit(solution)/shard_map/stack | solution.py:21
  548.2 11.1 %maximum_bitcast_fusion.1 = bf16[18,1,258,640]{2,3,0,1:T(8,128)(2,1)} fusion(bf16[1,18,1,640]{2,3,1,0:T(8,128)(2,1)S(1)} %copy.71, bf16[1,1,256,640]{2,3,1,0:T(8,128)(2,1)S(1)} %collective-permute-done.5, bf16[1,16,256,640]{2,3,1,0:T(8,128)(2,1)} %bitcast.329, bf16[1,1,256,640]{2,3,1,0:T(8,128)(2,1)} %copy-done.11, bf16[1,18,1,640]{2,3,1,0:T(8,128)(2,1)} %copy.70), kind=kLoop, calls=%fused_computation.45 | loop fusion | flops 29721600 | bytes 11888640 | tf_op jit(solution)/shard_map/concatenate | solution.py:33
  559.3 10.2 %copy.105 = bf16[18,1,258,640]{3,2,0,1:T(8,128)(2,1)} copy(bf16[18,1,258,640]{2,3,0,1:T(8,128)(2,1)} %maximum_bitcast_fusion.1) | data formatting | bytes 11888640
  569.5 5.9 pad.2.clone
  575.4 9.1 reshape.197
  584.4 3.9 copy.74
  591.1 44.4 %broadcast_select_fusion.1 = f32[16,8,33,640]{3,1,2,0:T(8,128)S(1)} fusion(pred[8,33]{0,1:T(8,128)(4,1)S(1)} %copy-done.27, bf16[3,3,640,640]{3,2,1,0:T(8,128)(2,1)} %param.10, bf16[18,1,7,2,640]{4,2,3,0,1:T(8,128)(2,1)S(1)} %slice.208, bf16[18,1,8,33,640]{4,2,3,0,1:T(8,128)(2,1)} %copy-done.5), kind=kOutput, calls=%fused_computation.79 | convolution fusion | flops 31164764160 | bytes 24591624 | tf_op jit(solution)/shard_map/conv_general_dilated | solution.py:12
  635.5 6.0 copy.75
  641.5 11.2 %fusion.31 = bf16[1,16,256,640]{3,1,2,0:T(8,128)(2,1)} fusion(f32[16,1,264,640]{3,0,2,1:T(8,128)} %bitcast.335, bf16[1,16,256,640]{3,2,1,0:T(8,128)(2,1)} %param.6), kind=kLoop, calls=%fused_computation.43 | loop fusion | flops 7864320 | bytes 20971520 | tf_op jit(solution)/shard_map/convert_element_type | solution.py:58
  652.6 6.0 copy.95
  658.7 9.2 maximum_bitcast_fusion.3
  671.0 9.1 reshape.215
  686.6 44.3 %broadcast_select_fusion = f32[16,8,33,640]{3,1,2,0:T(8,128)S(1)} fusion(pred[8,33]{0,1:T(8,128)(4,1)S(1)} %copy-done.27, bf16[3,3,640,640]{3,2,1,0:T(8,128)(2,1)} %param.7, bf16[18,1,7,2,640]{4,2,3,0,1:T(8,128)(2,1)S(1)} %slice.218, bf16[18,1,8,33,640]{4,2,3,0,1:T(8,128)(2,1)} %copy-done.4), kind=kOutput, calls=%fused_computation.78 | convolution fusion | flops 31164764160 | bytes 24591624 | tf_op jit(solution)/shard_map/conv_general_dilated | solution.py:12
  730.8 5.9 copy.85
  736.7 11.1 %fusion.29 = bf16[1,16,256,640]{3,1,2,0:T(8,128)(2,1)} fusion(f32[16,1,264,640]{3,0,2,1:T(8,128)} %bitcast.336, bf16[1,16,256,640]{3,2,1,0:T(8,128)(2,1)} %param.11), kind=kLoop, calls=%fused_computation.40 | loop fusion | flops 7864320 | bytes 20971520 | tf_op jit(solution)/shard_map/convert_element_type | solution.py:69
  747.9 6.0 copy.96
  753.9 136.9 %all-reduce.3.cloned.1.call-done = (f32[3,3,640,640]{3,2,1,0:T(8,128)}, f32[3,3,640,640]{3,2,1,0:T(8,128)}) async-done(((f32[3,3,640,640]{3,2,1,0:T(8,128)}, f32[3,3,640,640]{3,2,1,0:T(8,128)}), (f32[3,3,640,640]{3,2,1,0:T(8,128)}, f32[3,3,640,640]{3,2,1,0:T(8,128)})) %all-reduce.3.cloned.1.call-update) | async-done | bytes 29491216 | tf_op jit(solution)/shard_map/psum | solution.py:70
  890.9 11.6 %copy.150 = f32[3,3,640,640]{3,2,1,0:T(8,128)} copy(f32[3,3,640,640]{3,2,1,0:T(8,128)} %get-tuple-element.58) | data formatting | bytes 29491200
  902.5 11.6 %copy.151 = f32[3,3,640,640]{3,2,1,0:T(8,128)} copy(f32[3,3,640,640]{3,2,1,0:T(8,128)} %get-tuple-element.59) | data formatting | bytes 29491200
  (197 shorter events, 113.7 us)
Async XLA Ops:
  7.2 883.7 %all-reduce.3.cloned.1.call-start = ((), (), s32[]{:S(2)}) async-start(), calls=%async_computation | async-start | bytes 58982400 | tf_op jit(solution)/shard_map/psum | solution.py:70
  16.1 13.2 %collective-permute-start.1 = (bf16[1,1,256,640]{2,3,1,0:T(8,128)(2,1)S(1)}, bf16[1,1,256,640]{2,3,1,0:T(8,128)(2,1)S(1)}, u32[]{:S(2)}, u32[]{:S(2)}) collective-permute-start(bf16[1,1,256,640]{2,3,1,0:T(8,128)(2,1)S(1)} %get-tuple-element.47), channel_id=1, source_target_pairs={{1,0},{2,1},{3,2},{5,4},{6,5},{7,6}} | collective-permute-start | bytes 983048 | tf_op jit(solution)/shard_map/ppermute | solution.py:32
  17.4 11.9 %collective-permute-start = (bf16[1,1,256,640]{2,3,1,0:T(8,128)(2,1)S(1)}, bf16[1,1,256,640]{2,3,1,0:T(8,128)(2,1)S(1)}, u32[]{:S(2)}, u32[]{:S(2)}) collective-permute-start(bf16[1,1,256,640]{2,3,1,0:T(8,128)(2,1)S(1)} %get-tuple-element.46), channel_id=1, source_target_pairs={{0,1},{1,2},{2,3},{4,5},{5,6},{6,7}} | collective-permute-start | bytes 983048 | tf_op jit(solution)/shard_map/ppermute | solution.py:31
  22.8 26.6 %collective-permute-start.8 = (bf16[1,1,256,640]{3,2,1,0:T(8,128)(2,1)}, bf16[1,1,256,640]{3,2,1,0:T(8,128)(2,1)}, u32[]{:S(2)}, u32[]{:S(2)}) collective-permute-start(bf16[1,1,256,640]{3,2,1,0:T(8,128)(2,1)} %get-tuple-element.45), channel_id=1, source_target_pairs={{0,1},{1,2},{2,3},{4,5},{5,6},{6,7}} | collective-permute-start | bytes 983048 | tf_op jit(solution)/shard_map/ppermute | solution.py:31
  28.0 26.0 %collective-permute-start.9 = (bf16[1,1,256,640]{3,2,1,0:T(8,128)(2,1)}, bf16[1,1,256,640]{3,2,1,0:T(8,128)(2,1)}, u32[]{:S(2)}, u32[]{:S(2)}) collective-permute-start(bf16[1,1,256,640]{3,2,1,0:T(8,128)(2,1)} %get-tuple-element.44), channel_id=1, source_target_pairs={{1,0},{2,1},{3,2},{5,4},{6,5},{7,6}} | collective-permute-start | bytes 983048 | tf_op jit(solution)/shard_map/ppermute | solution.py:32
  29.3 0.7 copy-start.9
  30.0 36.6 %copy-start.7 = (bf16[1,1,256,640]{2,3,1,0:T(8,128)(2,1)}, bf16[1,1,256,640]{2,3,1,0:T(8,128)(2,1)S(1)}, u32[]{:S(2)}) copy-start(bf16[1,1,256,640]{2,3,1,0:T(8,128)(2,1)S(1)} %collective-permute-done) | copy-start | bytes 983044
  40.1 20.8 %collective-permute-start.3 = (bf16[1,18,1,640]{3,1,2,0:T(8,128)(2,1)S(1)}, bf16[1,18,1,640]{3,1,2,0:T(8,128)(2,1)S(1)}, u32[]{:S(2)}, u32[]{:S(2)}) collective-permute-start(bf16[1,18,1,640]{3,1,2,0:T(8,128)(2,1)S(1)} %copy.56), channel_id=1, source_target_pairs={{4,0},{5,1},{6,2},{7,3}} | collective-permute-start | bytes 69128 | tf_op jit(solution)/shard_map/ppermute | solution.py:32
  44.2 18.9 %collective-permute-start.2 = (bf16[1,18,1,640]{3,1,2,0:T(8,128)(2,1)}, bf16[1,18,1,640]{3,1,2,0:T(8,128)(2,1)}, u32[]{:S(2)}, u32[]{:S(2)}) collective-permute-start(bf16[1,18,1,640]{3,1,2,0:T(8,128)(2,1)} %copy.55), channel_id=1, source_target_pairs={{0,4},{1,5},{2,6},{3,7}} | collective-permute-start | bytes 69128 | tf_op jit(solution)/shard_map/ppermute | solution.py:31
  55.0 6.0 copy-start.6
  55.1 119.5 %collective-permute-start.11 = (bf16[1,18,1,640]{3,2,1,0:T(2,128)(2,1)S(1)}, bf16[1,18,1,640]{3,2,1,0:T(2,128)(2,1)S(1)}, u32[]{:S(2)}, u32[]{:S(2)}) collective-permute-start(bf16[1,18,1,640]{3,2,1,0:T(2,128)(2,1)S(1)} %get-tuple-element.33), channel_id=1, source_target_pairs={{4,0},{5,1},{6,2},{7,3}} | collective-permute-start | bytes 69128 | tf_op jit(solution)/shard_map/ppermute | solution.py:32
  56.4 118.2 %collective-permute-start.10 = (bf16[1,18,1,640]{3,2,1,0:T(2,128)(2,1)S(1)}, bf16[1,18,1,640]{3,2,1,0:T(2,128)(2,1)S(1)}, u32[]{:S(2)}, u32[]{:S(2)}) collective-permute-start(bf16[1,18,1,640]{3,2,1,0:T(2,128)(2,1)S(1)} %get-tuple-element.32), channel_id=1, source_target_pairs={{0,4},{1,5},{2,6},{3,7}} | collective-permute-start | bytes 69128 | tf_op jit(solution)/shard_map/ppermute | solution.py:31
  63.1 14.6 %copy-start = (bf16[1,18,1,640]{2,3,1,0:T(8,128)(2,1)}, bf16[1,18,1,640]{2,3,1,0:T(8,128)(2,1)S(1)}, u32[]{:S(2)}) copy-start(bf16[1,18,1,640]{2,3,1,0:T(8,128)(2,1)S(1)} %copy.58) | copy-start | bytes 69124
  102.7 4.0 copy-start.26
  191.3 4.0 copy-start.24
  191.3 4.0 copy-start.25
  292.1 1.8 copy-start.2
  292.7 2.6 slice-start
  292.8 3.4 copy-start.1
  292.8 3.4 copy-start.8
  292.8 3.4 copy-start.10
  292.8 3.8 slice-start.1
  296.6 54.2 %copy-start.3 = (bf16[16,1,256,640]{3,0,2,1:T(8,128)(2,1)}, bf16[16,1,256,640]{3,0,2,1:T(8,128)(2,1)S(1)}, u32[]{:S(2)}) copy-start(bf16[16,1,256,640]{3,0,2,1:T(8,128)(2,1)S(1)} %slice.215) | copy-start | bytes 15728644
  306.4 17.9 %slice-start.14 = ((s8[8847360]{0:T(1024)(128)(4,1)}), s8[4194304]{0:T(1024)(128)(4,1)S(1)}, s32[]{:S(2)}) async-start(s8[8847360]{0:T(1024)(128)(4,1)} %bitcast.347), calls=%async_computation.15 | async-start | bytes 8388608
  306.4 17.9 %slice-start.15 = ((s8[8847360]{0:T(1024)(128)(4,1)}), s8[4194304]{0:T(1024)(128)(4,1)S(1)}, s32[]{:S(2)}) async-start(s8[8847360]{0:T(1024)(128)(4,1)} %bitcast.347), calls=%async_computation.16 | async-start | bytes 8388608
  315.8 8.6 slice-start.16
  329.8 14.7 %slice-start.10 = ((s8[5242880]{0:T(1024)(128)(4,1)}), s8[4194304]{0:T(1024)(128)(4,1)S(1)}, s32[]{:S(2)}) async-start(s8[5242880]{0:T(1024)(128)(4,1)} %bitcast.343), calls=%async_computation.11 | async-start | bytes 8388608
  335.2 9.3 %slice-start.11 = ((s8[5242880]{0:T(1024)(128)(4,1)}), s8[1048576]{0:T(1024)(128)(4,1)S(1)}, s32[]{:S(2)}) async-start(s8[5242880]{0:T(1024)(128)(4,1)} %bitcast.343), calls=%async_computation.12 | async-start | bytes 2097152
  356.6 80.7 %collective-permute-start.5 = (bf16[1,1,256,640]{2,3,1,0:T(8,128)(2,1)S(1)}, bf16[1,1,256,640]{2,3,1,0:T(8,128)(2,1)S(1)}, u32[]{:S(2)}, u32[]{:S(2)}) collective-permute-start(bf16[1,1,256,640]{2,3,1,0:T(8,128)(2,1)S(1)} %copy.102), channel_id=1, source_target_pairs={{1,0},{2,1},{3,2},{5,4},{6,5},{7,6}} | collective-permute-start | bytes 983048 | tf_op jit(solution)/shard_map/ppermute | solution.py:32
  377.1 60.3 %collective-permute-start.4 = (bf16[1,1,256,640]{2,3,1,0:T(8,128)(2,1)}, bf16[1,1,256,640]{2,3,1,0:T(8,128)(2,1)S(1)}, u32[]{:S(2)}, u32[]{:S(2)}) collective-permute-start(bf16[1,1,256,640]{2,3,1,0:T(8,128)(2,1)} %copy.100), channel_id=1, source_target_pairs={{0,1},{1,2},{2,3},{4,5},{5,6},{6,7}} | collective-permute-start | bytes 983048 | tf_op jit(solution)/shard_map/ppermute | solution.py:31
  383.8 13.2 %slice-start.2 = ((s8[5242880]{0:T(1024)(128)(4,1)}), s8[4194304]{0:T(1024)(128)(4,1)S(1)}, s32[]{:S(2)}) async-start(s8[5242880]{0:T(1024)(128)(4,1)} %bitcast.324), calls=%async_computation.3 | async-start | bytes 8388608
  383.8 13.2 %slice-start.12 = ((s8[5242880]{0:T(1024)(128)(4,1)}), s8[4194304]{0:T(1024)(128)(4,1)S(1)}, s32[]{:S(2)}) async-start(s8[5242880]{0:T(1024)(128)(4,1)} %bitcast.345), calls=%async_computation.13 | async-start | bytes 8388608
  385.7 11.3 %slice-start.3 = ((s8[5242880]{0:T(1024)(128)(4,1)}), s8[1048576]{0:T(1024)(128)(4,1)S(1)}, s32[]{:S(2)}) async-start(s8[5242880]{0:T(1024)(128)(4,1)} %bitcast.324), calls=%async_computation.4 | async-start | bytes 2097152
  385.7 11.3 %slice-start.13 = ((s8[5242880]{0:T(1024)(128)(4,1)}), s8[1048576]{0:T(1024)(128)(4,1)S(1)}, s32[]{:S(2)}) async-start(s8[5242880]{0:T(1024)(128)(4,1)} %bitcast.345), calls=%async_computation.14 | async-start | bytes 2097152
  385.7 70.5 %collective-permute-start.13 = (bf16[1,1,256,640]{3,2,1,0:T(8,128)(2,1)}, bf16[1,1,256,640]{3,2,1,0:T(8,128)(2,1)}, u32[]{:S(2)}, u32[]{:S(2)}) collective-permute-start(bf16[1,1,256,640]{3,2,1,0:T(8,128)(2,1)} %slice.217), channel_id=1, source_target_pairs={{1,0},{2,1},{3,2},{5,4},{6,5},{7,6}} | collective-permute-start | bytes 983048 | tf_op jit(solution)/shard_map/ppermute | solution.py:32
  397.0 4.3 copy-start.18
  397.0 4.3 copy-start.19
  403.9 4.3 copy-start.14
  403.9 4.3 copy-start.15
  403.9 4.3 copy-start.16
  403.9 4.3 copy-start.17
  424.6 6.1 copy-start.23
  431.6 24.7 %collective-permute-start.12 = (bf16[1,1,256,640]{3,2,1,0:T(8,128)(2,1)}, bf16[1,1,256,640]{3,2,1,0:T(8,128)(2,1)}, u32[]{:S(2)}, u32[]{:S(2)}) collective-permute-start(bf16[1,1,256,640]{3,2,1,0:T(8,128)(2,1)} %slice.214), channel_id=1, source_target_pairs={{0,1},{1,2},{2,3},{4,5},{5,6},{6,7}} | collective-permute-start | bytes 983048 | tf_op jit(solution)/shard_map/ppermute | solution.py:31
  437.4 0.7 copy-start.11
  448.1 32.0 %collective-permute-start.7 = (bf16[1,18,1,640]{3,1,2,0:T(8,128)(2,1)S(1)}, bf16[1,18,1,640]{3,1,2,0:T(8,128)(2,1)S(1)}, u32[]{:S(2)}, u32[]{:S(2)}) collective-permute-start(bf16[1,18,1,640]{3,1,2,0:T(8,128)(2,1)S(1)} %copy.69), channel_id=1, source_target_pairs={{4,0},{5,1},{6,2},{7,3}} | collective-permute-start | bytes 69128 | tf_op jit(solution)/shard_map/ppermute | solution.py:32
  451.7 30.5 %collective-permute-start.6 = (bf16[1,18,1,640]{3,1,2,0:T(8,128)(2,1)S(1)}, bf16[1,18,1,640]{3,1,2,0:T(8,128)(2,1)S(1)}, u32[]{:S(2)}, u32[]{:S(2)}) collective-permute-start(bf16[1,18,1,640]{3,1,2,0:T(8,128)(2,1)S(1)} %copy.68), channel_id=1, source_target_pairs={{0,4},{1,5},{2,6},{3,7}} | collective-permute-start | bytes 69128 | tf_op jit(solution)/shard_map/ppermute | solution.py:31
  458.0 200.7 %collective-permute-start.15 = (bf16[1,18,1,640]{3,2,1,0:T(2,128)(2,1)}, bf16[1,18,1,640]{3,2,1,0:T(2,128)(2,1)}, u32[]{:S(2)}, u32[]{:S(2)}) collective-permute-start(bf16[1,18,1,640]{3,2,1,0:T(2,128)(2,1)} %get-tuple-element.31), channel_id=1, source_target_pairs={{4,0},{5,1},{6,2},{7,3}} | collective-permute-start | bytes 69128 | tf_op jit(solution)/shard_map/ppermute | solution.py:32
  459.3 15.4 %slice-start.4 = ((s8[5242880]{0:T(1024)(128)(4,1)}), s8[4194304]{0:T(1024)(128)(4,1)S(1)}, s32[]{:S(2)}) async-start(s8[5242880]{0:T(1024)(128)(4,1)} %bitcast.330), calls=%async_computation.5 | async-start | bytes 8388608
  459.3 15.4 %slice-start.6 = ((s8[5242880]{0:T(1024)(128)(4,1)}), s8[4194304]{0:T(1024)(128)(4,1)S(1)}, s32[]{:S(2)}) async-start(s8[5242880]{0:T(1024)(128)(4,1)} %bitcast.337), calls=%async_computation.7 | async-start | bytes 8388608
  459.3 15.4 %slice-start.5 = ((s8[5242880]{0:T(1024)(128)(4,1)}), s8[1048576]{0:T(1024)(128)(4,1)S(1)}, s32[]{:S(2)}) async-start(s8[5242880]{0:T(1024)(128)(4,1)} %bitcast.330), calls=%async_computation.6 | async-start | bytes 2097152
  459.3 15.4 %slice-start.7 = ((s8[5242880]{0:T(1024)(128)(4,1)}), s8[1048576]{0:T(1024)(128)(4,1)S(1)}, s32[]{:S(2)}) async-start(s8[5242880]{0:T(1024)(128)(4,1)} %bitcast.337), calls=%async_computation.8 | async-start | bytes 2097152
  459.3 15.4 %copy-start.12 = (bf16[1,1,256,640]{2,3,1,0:T(8,128)(2,1)S(1)}, bf16[1,1,256,640]{2,3,1,0:T(8,128)(2,1)}, u32[]{:S(2)}) copy-start(bf16[1,1,256,640]{2,3,1,0:T(8,128)(2,1)} %copy-done.11) | copy-start | bytes 983044
  459.3 199.3 %collective-permute-start.14 = (bf16[1,18,1,640]{3,2,1,0:T(2,128)(2,1)}, bf16[1,18,1,640]{3,2,1,0:T(2,128)(2,1)}, u32[]{:S(2)}, u32[]{:S(2)}) collective-permute-start(bf16[1,18,1,640]{3,2,1,0:T(2,128)(2,1)} %get-tuple-element.30), channel_id=1, source_target_pairs={{0,4},{1,5},{2,6},{3,7}} | collective-permute-start | bytes 69128 | tf_op jit(solution)/shard_map/ppermute | solution.py:31
  495.7 14.2 %slice-start.8 = ((s8[5242880]{0:T(1024)(128)(4,1)}), s8[4194304]{0:T(1024)(128)(4,1)S(1)}, s32[]{:S(2)}) async-start(s8[5242880]{0:T(1024)(128)(4,1)} %bitcast.339), calls=%async_computation.9 | async-start | bytes 8388608
  502.9 7.1 slice-start.9
  524.4 4.2 copy-start.21
  524.4 4.2 copy-start.22
  528.7 2.6 copy-start.13
  531.3 2.6 copy-start.20
  584.4 6.7 copy-start.27
  588.3 2.7 copy-start.5
  683.9 2.5 copy-start.4
Sparse Core Ops, SparseCore 0:
  548.3 342.4 all-reduce.2
where the time goes:
time: 932 us; the launch traced here: 921 us
  matrix products  306 us (33%)
  local copies, waits for them, and re-layouts  232 us (25%)
  waiting for transfers between devices  137 us (15%)
  other arithmetic  136 us (15%)
  starting transfers between devices  47.9 us (5%)
  blocking collectives  47 us (5%)
  between operations  15.4 us (2%)
    conv_general_dilated x4, matrix products, _conv(): lax.conv_general_dilated(up, w, (1, 1), 'VALID', dimension_numbers=DN, pr...  191 us
    psum x1, waiting for transfers between devices, body(): dw1 = lax.psum(_wgrad(xp, da), ('h', 'w'))  137 us
    dot_general x18, matrix products, _wgrad(): jnp.einsum('bhwc,bhwo->co', up[:, a:a + th, b:b + tw], v, preferred_eleme...  115 us
    unnamed x103, local copies, waits for them, and re-layouts  93.6 us
    conv_general_dilated x14, local copies, waits for them, and re-layouts, _conv(): lax.conv_general_dilated(up, w, (1, 1), 'VALID', dimension_numbers=DN, pr...  64.1 us
    concatenate x8, other arithmetic, _edge(): return jnp.concatenate([prev, u, nxt], axis=axis)  63.7 us
    another operation x7, other arithmetic, _wgrad(): jnp.stack([jnp.stack([jnp.einsum('bhwc,bhwo->co', up[:, a:a + th, b:b + t...  38.4 us
    ppermute x8, starting transfers between devices, _edge(): prev = lax.ppermute(hi, name, [(i, i + 1) for i in range(n - 1)])  37.1 us
  transfers between devices with their start and end apart: 17, of which 1 were waited for; matrix products, arithmetic and copies ran while one was open for 52% of the time, Pallas kernels for 0%

commit v1 on v0

v1 whole, which is shorter than its diff:
```python
import functools

import jax
import jax.numpy as jnp
from jax import lax
from jax.experimental import pallas as pl
from jax.experimental.pallas import tpu as pltpu
from jax.sharding import Mesh
from jax.sharding import PartitionSpec as P


GROUPS = 32
EPS = 1e-5
F32 = jnp.float32
BF16 = jnp.bfloat16
MESH = pl.DeviceIdType.MESH
EB = 16
VMEM_LIMIT = 61 * 1024 * 1024
ANY = pl.BlockSpec(memory_space=pl.ANY)
VM = pl.BlockSpec(memory_space=pltpu.VMEM)
GELU_C = 0.7978845608028654
GELU_A = 0.044715


def _gelu_parts(n):
    n2 = n * n
    t = jnp.tanh(GELU_C * (n + GELU_A * n * n2))
    return n2, t


def _gelu(n):
    _, t = _gelu_parts(n)
    return 0.5 * n * (1.0 + t)


def _gelu_grad(n):
    n2, t = _gelu_parts(n)
    return 0.5 * (1.0 + t) + 0.5 * n * (1.0 - t * t) * (GELU_C * (1.0 + 3.0 * GELU_A * n2))


def _halo_kernel(nh, nw, n_arr, *refs):
    ins = refs[:n_arr]
    outs = refs[n_arr:4 * n_arr]
    send, recv = refs[4 * n_arr:]
    th, tw, c = ins[0].shape
    w = lax.axis_index("w")
    h = lax.axis_index("x") * 2 + lax.axis_index("c")

    def dev(dh, dw):
        hh = h + dh
        return (w + dw, hh // 2, hh % 2)

    def has(dh, dw):
        ok = None
        for cond in ([h > 0] if dh < 0 else [h < nh - 1] if dh > 0 else []) + ([w > 0] if dw < 0 else [w < nw - 1] if dw > 0 else []):
            ok = cond if ok is None else jnp.logical_and(ok, cond)
        return ok

    dirs = [(dh, dw) for dh in (-1, 0, 1) for dw in (-1, 0, 1) if (dh, dw) != (0, 0)]
    barrier = pltpu.get_barrier_semaphore()
    for d in dirs:
        @pl.when(has(*d))
        def _(d=d):
            pl.semaphore_signal(barrier, inc=1, device_id=dev(*d), device_id_type=MESH)
    one = jnp.int32(1)
    zero = jnp.int32(0)
    nv = one + jnp.where(h > 0, one, zero) + jnp.where(h < nh - 1, one, zero)
    nz = one + jnp.where(w > 0, one, zero) + jnp.where(w < nw - 1, one, zero)
    pl.semaphore_wait(barrier, nv * nz - 1)

    def parts(k, dh, dw):
        u = ins[k]
        rows, cl, cr = outs[3 * k:3 * k + 3]
        r = 0 if dh < 0 else th - 1
        to = 1 if dh < 0 else 0
        to18 = th + 1 if dh < 0 else 0
        cs = slice(0, EB) if dw < 0 else slice(tw - EB, tw)
        side = cr if dw < 0 else cl
        if dw == 0:
            return u.at[r], rows.at[to]
        if dh == 0:
            return u.at[:, cs, :], side.at[1:th + 1]
        return u.at[r, cs, :], side.at[to18]

    def copy(k, i, dh, dw):
        src, dst = parts(k, dh, dw)
        return pltpu.make_async_remote_copy(src_ref=src, dst_ref=dst, send_sem=send.at[k * 8 + i], recv_sem=recv.at[k * 8 + i],
                                            device_id=dev(dh, dw), device_id_type=MESH)

    for k in range(n_arr):
        for i, d in enumerate(dirs):
            @pl.when(has(*d))
            def _(k=k, i=i, d=d):
                copy(k, i, *d).start()
    for k in range(n_arr):
        rows, cl, cr = outs[3 * k:3 * k + 3]
        for dh, dw in dirs:
            @pl.when(jnp.logical_not(has(-dh, -dw)))
            def _(rows=rows, cl=cl, cr=cr, dh=dh, dw=dw):
                to = 1 if dh < 0 else 0
                to18 = th + 1 if dh < 0 else 0
                side = cr if dw < 0 else cl
                if dw == 0:
                    rows[to] = jnp.zeros((tw, c), BF16)
                elif dh == 0:
                    side[1:th + 1] = jnp.zeros((th, EB, c), BF16)
                else:
                    side[to18] = jnp.zeros((EB, c), BF16)
    for k in range(n_arr):
        for i, (dh, dw) in enumerate(dirs):
            @pl.when(has(dh, dw))
            def _(k=k, i=i, dh=dh, dw=dw):
                copy(k, i, dh, dw).wait_send()

            @pl.when(has(-dh, -dw))
            def _(k=k, i=i, dh=dh, dw=dw):
                copy(k, i, dh, dw).wait_recv()


def _halo(nh, nw, cid, *us):
    th, tw, c = us[0].shape
    n = len(us)
    out = []
    for _ in us:
        out += [jax.ShapeDtypeStruct((2, tw, c), BF16), jax.ShapeDtypeStruct((th + 2, EB, c), BF16), jax.ShapeDtypeStruct((th + 2, EB, c), BF16)]
    res = pl.pallas_call(
        functools.partial(_halo_kernel, nh, nw, n), out_shape=out, in_specs=[ANY] * n, out_specs=[VM] * (3 * n),
        scratch_shapes=[pltpu.SemaphoreType.DMA((8 * n,)), pltpu.SemaphoreType.DMA((8 * n,))],
        compiler_params=pltpu.CompilerParams(collective_id=cid, has_side_effects=True, vmem_limit_bytes=VMEM_LIMIT),
    )(*us)
    return [tuple(res[3 * k:3 * k + 3]) for k in range(n)]


def _allsum_kernel(nh, nw, cnt, mode, part_ref, par_ref, out_ref, mine, buf, lsem, send, recv):
    n = nh * nw
    w = lax.axis_index("w")
    h = lax.axis_index("x") * 2 + lax.axis_index("c")
    me = w * nh + h

    def dev(j):
        hh = j % nh
        return (j // nh, hh // 2, hh % 2)

    local = pltpu.make_async_copy(part_ref, mine, lsem)
    local.start()
    barrier = pltpu.get_barrier_semaphore()
    for k in range(1, n):
        pl.semaphore_signal(barrier, inc=1, device_id=dev(lax.rem(me + k, n)), device_id_type=MESH)
    local.wait()
    pl.semaphore_wait(barrier, n - 1)
    copies = []
    for k in range(1, n):
        cp = pltpu.make_async_remote_copy(src_ref=mine, dst_ref=buf.at[k - 1], send_sem=send.at[k - 1], recv_sem=recv.at[k - 1],
                                          device_id=dev(lax.rem(me + k, n)), device_id_type=MESH)
        cp.start()
        copies.append(cp)
    for cp in copies:
        cp.wait()
    total = None
    vals = [mine[...]] + [buf[k] for k in range(n - 1)]
    for j in range(n):
        t = jnp.zeros_like(vals[0])
        off = lax.rem(me - j + n, n)
        for k in range(n):
            t = t + jnp.where(off == k, vals[k], 0.0)
        total = t if total is None else total + t
    c = total.shape[-1]
    gi = jnp.floor((lax.broadcasted_iota(jnp.int32, (c, c), 0).astype(F32) + 0.5) * (GROUPS / c))
    gj = jnp.floor((lax.broadcasted_iota(jnp.int32, (c, c), 1).astype(F32) + 0.5) * (GROUPS / c))
    same = jnp.where(gi == gj, 1.0, 0.0).astype(F32)
    row = lax.broadcasted_iota(jnp.int32, (8, c), 0)
    if mode == 0:
        m = jnp.dot(total, same, precision=lax.Precision.HIGHEST, preferred_element_type=F32) / cnt
        mean, sq = m[0:1], m[1:2]
        rstd = lax.rsqrt(sq - mean * mean + EPS)
        out_ref[...] = jnp.where(row == 0, mean, jnp.where(row == 1, rstd, par_ref[...]))
    else:
        u = jnp.dot(total * par_ref[2:3], same, precision=lax.Precision.HIGHEST, preferred_element_type=F32) / cnt
        out_ref[...] = jnp.where(row == 0, total[0:1], jnp.where(row == 1, total[1:2], jnp.where(row == 2, u[0:1], u[1:2])))


def _allsum(nh, nw, cnt, mode, cid, part, par):
    c = part.shape[-1]
    n = nh * nw
    return pl.pallas_call(
        functools.partial(_allsum_kernel, nh, nw, cnt, mode), out_shape=jax.ShapeDtypeStruct((8, c), F32),
        in_specs=[ANY, VM], out_specs=VM,
        scratch_shapes=[pltpu.VMEM((8, c), F32), pltpu.VMEM((n - 1, 8, c), F32), pltpu.SemaphoreType.DMA,
                        pltpu.SemaphoreType.DMA((n - 1,)), pltpu.SemaphoreType.DMA((n - 1,))],
        compiler_params=pltpu.CompilerParams(collective_id=cid, has_side_effects=True, vmem_limit_bytes=VMEM_LIMIT),
    )(part, par)


def _load_patches(u_ref, rows_ref, p, sems):
    th, c = u_ref.shape[0], u_ref.shape[2]
    cps = [pltpu.make_async_copy(u_ref, p.at[1:th + 1, :, c:2 * c], sems.at[0]),
           pltpu.make_async_copy(rows_ref.at[0], p.at[0, :, c:2 * c], sems.at[1]),
           pltpu.make_async_copy(rows_ref.at[1], p.at[th + 1, :, c:2 * c], sems.at[2])]
    for cp in cps:
        cp.start()
    return cps


def _shift_patches(p, cl_ref, cr_ref):
    n, tw, c3 = p.shape
    c = c3 // 3
    ck = 128

    def row(r, _):
        idx = lax.broadcasted_iota(jnp.int32, (tw, ck), 0)
        for k in range(c // ck):
            f = p[r, :, c + k * ck:c + (k + 1) * ck].astype(F32)
            lo = cl_ref[r, :, k * ck:(k + 1) * ck].astype(F32)[EB - 1:EB]
            hi = cr_ref[r, :, k * ck:(k + 1) * ck].astype(F32)[0:1]
            p[r, :, k * ck:(k + 1) * ck] = jnp.where(idx == 0, lo, pltpu.roll(f, 1, 0)).astype(BF16)
            p[r, :, 2 * c + k * ck:2 * c + (k + 1) * ck] = jnp.where(idx == tw - 1, hi, pltpu.roll(f, tw - 1, 0)).astype(BF16)
        return 0

    lax.fori_loop(0, n, row, 0)


def _conv_kernel(transposed, rb, n_extra, epilogue, u_ref, rows_ref, cl_ref, cr_ref, w_ref, *refs):
    extra = refs[:n_extra]
    outs = refs[n_extra:-4]
    p, wb, psem, wsem = refs[-4:]
    c = u_ref.shape[2]
    i = pl.program_id(0)

    @pl.when(i == 0)
    def _():
        cps = _load_patches(u_ref, rows_ref, p, psem)
        ws = []
        for a in range(3):
            for b in range(3):
                if transposed:
                    ws.append(pltpu.make_async_copy(w_ref.at[2 - a, 2 - b], wb.at[a, :, b * c:(b + 1) * c], wsem.at[a * 3 + b]))
                else:
                    ws.append(pltpu.make_async_copy(w_ref.at[a, b], wb.at[a, b * c:(b + 1) * c, :], wsem.at[a * 3 + b]))
        for cp in ws:
            cp.start()
        for cp in cps:
            cp.wait()
        _shift_patches(p, cl_ref, cr_ref)
        for cp in ws:
            cp.wait()

    tw = p.shape[1]
    acc = None
    for a in range(3):
        lhs = p[pl.ds(i * rb + a, rb)].reshape(rb * tw, 3 * c)
        dims = (((1,), (1,)), ((), ())) if transposed else (((1,), (0,)), ((), ()))
        d = lax.dot_general(lhs, wb[a], dims, preferred_element_type=F32)
        acc = d if acc is None else acc + d
    epilogue(i, acc, extra, outs)


def _conv(transposed, epilogue, u, halo, w, extra, extra_specs, outs, out_specs, rb=2):
    th, tw, c = u.shape
    full = pl.BlockSpec((th + 2, EB, c), lambda i: (0, 0, 0), pipeline_mode=pl.Buffered(1))
    return pl.pallas_call(
        functools.partial(_conv_kernel, transposed, rb, len(extra), epilogue),
        grid=(th // rb,), out_shape=outs, in_specs=[ANY, ANY, full, full, ANY] + extra_specs, out_specs=out_specs,
        scratch_shapes=[pltpu.VMEM((th + 2, tw, 3 * c), BF16), pltpu.VMEM((3, c, 3 * c) if transposed else (3, 3 * c, c), BF16),
                        pltpu.SemaphoreType.DMA((3,)), pltpu.SemaphoreType.DMA((9,))],
        compiler_params=pltpu.CompilerParams(dimension_semantics=("arbitrary",), vmem_limit_bytes=VMEM_LIMIT),
        cost_estimate=pl.CostEstimate(flops=2 * 9 * th * tw * c * c, bytes_accessed=4 * th * tw * c + 18 * c * c, transcendentals=0),
    )(u, *halo, w, *extra)


def _ep_conv1(i, acc, extra, outs):
    a_ref, s_ref = outs
    a16 = acc.astype(BF16)
    a_ref[...] = a16.reshape(a_ref.shape)
    a = a16.astype(F32)
    s0 = a.sum(0, keepdims=True)
    s1 = (a * a).sum(0, keepdims=True)
    row = lax.broadcasted_iota(jnp.int32, s_ref.shape, 0)
    s = jnp.where(row == 0, s0, jnp.where(row == 1, s1, 0.0))

    @pl.when(i == 0)
    def _():
        s_ref[...] = s

    @pl.when(i > 0)
    def _():
        s_ref[...] += s


def _ep_residual(i, acc, extra, outs):
    o_ref = outs[0]
    r = extra[0][...].astype(F32).reshape(acc.shape)
    o_ref[...] = (acc + r).astype(BF16).reshape(o_ref.shape)


def _ep_dz(i, acc, extra, outs):
    a_ref, st_ref = extra
    dn_ref, s_ref = outs
    st = st_ref[...]
    xhat = (a_ref[...].astype(F32).reshape(acc.shape) - st[0:1]) * st[1:2]
    dn = acc * _gelu_grad(xhat * st[2:3] + st[3:4])
    dn_ref[...] = dn.reshape(dn_ref.shape)
    s0 = (dn * xhat).sum(0, keepdims=True)
    s1 = dn.sum(0, keepdims=True)
    row = lax.broadcasted_iota(jnp.int32, s_ref.shape, 0)
    s = jnp.where(row == 0, s0, jnp.where(row == 1, s1, 0.0))

    @pl.when(i == 0)
    def _():
        s_ref[...] = s

    @pl.when(i > 0)
    def _():
        s_ref[...] += s


def _z_kernel(a_ref, st_ref, z_ref):
    st = st_ref[...]
    xhat = (a_ref[...].astype(F32) - st[0:1]) * st[1:2]
    z_ref[...] = _gelu(xhat * st[2:3] + st[3:4]).astype(BF16)


def _da_kernel(dn_ref, a_ref, st_ref, t_ref, o_ref):
    st = st_ref[...]
    t = t_ref[...]
    xhat = (a_ref[...].astype(F32) - st[0:1]) * st[1:2]
    o_ref[...] = (st[1:2] * (dn_ref[...] * st[2:3] - t[3:4] - xhat * t[2:3])).astype(BF16)


def _wgrad_kernel(u_ref, rows_ref, cl_ref, cr_ref, v_ref, o_ref, p, vt, psem):
    a = pl.program_id(0)
    th, tw, c = v_ref.shape

    @pl.when(a == 0)
    def _():
        cps = _load_patches(u_ref, rows_ref, p, psem)

        def tr(r, _):
            vt[:, pl.ds(pl.multiple_of(r * tw, tw), tw)] = v_ref[r].T
            return 0

        lax.fori_loop(0, th, tr, 0)
        for cp in cps:
            cp.wait()
        _shift_patches(p, cl_ref, cr_ref)

    n = 3 * c
    k = 0
    while k < n:
        m = min(512, n - k)
        rhs = p[pl.ds(a, th), :, k:k + m].reshape(th * tw, m)
        d = jnp.dot(vt[...], rhs, preferred_element_type=F32)
        o_ref[0, k:k + m, :] = d.T
        k += m


def _wgrad(u, halo, v):
    th, tw, c = u.shape
    full = pl.BlockSpec((th + 2, EB, c), lambda i: (0, 0, 0), pipeline_mode=pl.Buffered(1))
    fv = pl.BlockSpec((th, tw, c), lambda i: (0, 0, 0), pipeline_mode=pl.Buffered(1))
    return pl.pallas_call(
        _wgrad_kernel, grid=(3,), out_shape=jax.ShapeDtypeStruct((3, 3 * c, c), F32),
        in_specs=[ANY, ANY, full, full, fv], out_specs=pl.BlockSpec((1, 3 * c, c), lambda a: (a, 0, 0)),
        scratch_shapes=[pltpu.VMEM((th + 2, tw, 3 * c), BF16), pltpu.VMEM((c, th * tw), BF16), pltpu.SemaphoreType.DMA((3,))],
        compiler_params=pltpu.CompilerParams(dimension_semantics=("arbitrary",), vmem_limit_bytes=VMEM_LIMIT),
        cost_estimate=pl.CostEstimate(flops=2 * 9 * th * tw * c * c, bytes_accessed=4 * th * tw * c + 36 * c * c, transcendentals=0),
    )(u, *halo, v)


def _reduce_all(d):
    r, k, c = d.shape
    s = lax.psum_scatter(d.reshape(r * k, c), ("c", "w", "x"), scatter_dimension=0, tiled=True)
    s = lax.all_gather(s, ("w", "x"), axis=0, tiled=True)
    return lax.all_gather(s, "c", axis=0, tiled=True).reshape(3, 3, c, c)


def solution(mesh):
    nh, nw = mesh.shape["h"], mesh.shape["w"]
    mesh3 = Mesh(mesh.devices.reshape(nw, nh // 2, 2), ("w", "x", "c"))
    tile = P(None, ("x", "c"), "w", None)

    def body(x, w1, gamma, beta, w2, g):
        _, th, tw, c = x.shape
        x, g = x[0], g[0]
        cnt = float(th * nh * tw * nw * (c // GROUPS))
        rb = 2
        blk = pl.BlockSpec((rb, tw, c), lambda i: (i, 0, 0))
        small = pl.BlockSpec((8, c), lambda i: (0, 0))
        img16 = jax.ShapeDtypeStruct((th, tw, c), BF16)
        img32 = jax.ShapeDtypeStruct((th, tw, c), F32)
        sums = jax.ShapeDtypeStruct((8, c), F32)
        par = jnp.concatenate([jnp.zeros((2, c), F32), gamma[None], beta[None], jnp.zeros((4, c), F32)])

        xh, gh = _halo(nh, nw, 0, x, g)
        a, s = _conv(False, _ep_conv1, x, xh, w1, [], [], [img16, sums], [blk, small])
        st = _allsum(nh, nw, cnt, 0, 1, s, par)
        z = pl.pallas_call(_z_kernel, grid=(th // rb,), out_shape=img16, in_specs=[blk, small], out_specs=blk, name="act")(a, st)
        (zh,) = _halo(nh, nw, 2, z)
        d2 = _wgrad(z, zh, g)
        g_late, d2 = lax.optimization_barrier((g, d2))
        dw2 = _reduce_all(d2)
        dn, t = _conv(True, _ep_dz, g_late, gh, w2, [a, st], [blk, small], [img32, sums], [blk, small])
        t = _allsum(nh, nw, cnt, 1, 3, t, st)
        da = pl.pallas_call(_da_kernel, grid=(th // rb,), out_shape=img16, in_specs=[blk, blk, small, small], out_specs=blk, name="da")(dn, a, st, t)
        (dah,) = _halo(nh, nw, 4, da)
        d1 = _wgrad(x, xh, da)
        z_late, da_late, d1 = lax.optimization_barrier((z, da, d1))
        dw1 = _reduce_all(d1)
        (y,) = _conv(False, _ep_residual, z_late, zh, w2, [x], [blk], [img16], [blk])
        (dx,) = _conv(True, _ep_residual, da_late, dah, w1, [g], [blk], [img16], [blk])
        return y[None], dx[None], dw1, dw2, t[0], t[1]

    return jax.shard_map(body, mesh=mesh3, in_specs=(tile, P(), P(), P(), P(), tile), out_specs=(tile, tile, P(), P(), P(), P()), check_vma=False)
```

time: 932 us -> 766 us (0.82); the launches traced: 921 us -> 765 us
  Pallas kernels: 0 us -> 376 us
  matrix products: 306 us -> 0 us
  waiting for transfers between devices: 137 us -> 348 us
  local copies, waits for them, and re-layouts: 232 us -> 26.2 us
  other arithmetic: 136 us -> 0.68 us
  starting transfers between devices: 47.9 us -> 0.23 us
  blocking collectives: 47 us -> 0 us
    pallas_call x0 -> x13, Pallas kernels: none -> 376 us  [the longest x4 206 us: _conv(): pl.pallas_call(functools.partial(_conv_kernel, transposed, rb, len(extra)...]
    reduce_scatter x0 -> x2, waiting for transfers between devices: none -> 197 us  [_reduce_all(): lax.psum_scatter(d.reshape(r * k, c), ('c', 'w', 'x'), scatter_dimension=...]
    conv_general_dilated x4 -> x0, matrix products: 191 us -> none  [_conv(): lax.conv_general_dilated(up, w, (1, 1), 'VALID', dimension_numbers=DN, pr...]
    all_gather x0 -> x4, waiting for transfers between devices: none -> 150 us  [the longest x2 150 us: _reduce_all(): s = lax.all_gather(s, ('w', 'x'), axis=0, tiled=True)]
    psum x1 -> x0, waiting for transfers between devices: 137 us -> none  [body(): dw1 = lax.psum(_wgrad(xp, da), ('h', 'w'))]
    dot_general x18 -> x0, matrix products: 115 us -> none  [_wgrad(): jnp.einsum('bhwc,bhwo->co', up[:, a:a + th, b:b + tw], v, preferred_eleme...]
    unnamed x103 -> x2, local copies, waits for them, and re-layouts: 93.6 us -> 23.3 us
    conv_general_dilated x14 -> x0, local copies, waits for them, and re-layouts: 64.1 us -> none  [_conv(): lax.conv_general_dilated(up, w, (1, 1), 'VALID', dimension_numbers=DN, pr...]
  transfers between devices with their start and end apart: 17 -> 6, of which waited for: 1 -> 4; matrix products, arithmetic and copies ran while one was open for 52% -> 0% of each run, Pallas kernels for 0% -> 15%
where the time goes in v1:
time: 766 us; the launch traced here: 765 us
  Pallas kernels  376 us (49%)
  waiting for transfers between devices  348 us (45%)
  local copies, waits for them, and re-layouts  26.2 us (3%)
  between operations  14.2 us (2%)
    pallas_call x4, Pallas kernels, _conv(): pl.pallas_call(functools.partial(_conv_kernel, transposed, rb, len(extra)...  206 us
    reduce_scatter x2, waiting for transfers between devices, _reduce_all(): lax.psum_scatter(d.reshape(r * k, c), ('c', 'w', 'x'), scatter_dimension=...  197 us
    all_gather x2, waiting for transfers between devices, _reduce_all(): s = lax.all_gather(s, ('w', 'x'), axis=0, tiled=True)  150 us
    pallas_call x2, Pallas kernels, _wgrad(): pl.pallas_call(_wgrad_kernel, grid=(3,), out_shape=jax.ShapeDtypeStruct((...  87.6 us
    pallas_call x3, Pallas kernels, _halo(): pl.pallas_call(functools.partial(_halo_kernel, nh, nw, n), out_shape=out,...  45.6 us
    unnamed x2, local copies, waits for them, and re-layouts  23.3 us
    pallas_call x2, Pallas kernels, _allsum(): pl.pallas_call(functools.partial(_allsum_kernel, nh, nw, cnt, mode), out_...  16.6 us
  transfers between devices with their start and end apart: 6, of which 4 were waited for; matrix products, arithmetic and copies ran while one was open for 0% of the time, Pallas kernels for 15%

profile of v1, /device:TPU:0, one launch (start us, length us, event | category | flops | bytes accessed | tf_op | source)
XLA Modules:
  0.0 765.3 jit_solution(3211352888113399444)
XLA Ops:
  7.2 0.0 reduce-scatter.3.cloned.1.call-start
  7.2 0.7 broadcast_in_dim.20
  7.9 0.7 broadcast_in_dim.19
  8.6 0.1 pad.3.clone
  8.7 21.6 %shard_map.109 = (bf16[2,256,640]{2,1,0:T(8,128)(2,1)}, bf16[18,16,640]{2,1,0:T(8,128)(2,1)}, bf16[18,16,640]{2,1,0:T(8,128)(2,1)}, bf16[2,256,640]{2,1,0:T(8,12...) custom-call(bf16[16,256,640]{2,1,0:T(8,128)(2,1)} %bitcast.12, bf16[16,256,640]{2,1,0:T(8,128)(2,1)} %bitcast.16), custom_call_target="tpu_custom_call" | custom-call | tf_op jit(solution)/shard_map/pallas_call | solution.py:126
  30.2 49.3 %shard_map.110 = (bf16[16,256,640]{2,1,0:T(8,128)(2,1)}, f32[8,640]{1,0:T(8,128)}) custom-call(bf16[16,256,640]{2,1,0:T(8,128)(2,1)} %bitcast.13, bf16[2,256,640]{2,1,0:T(8,128)(2,1)} %get-tuple-element.27.rows_ref, bf16[18,16,640]{2,1,0:T(8,128)(2,1)} %get-tuple-element.28.cl_ref, bf16[18,16,640]{2,1,0:T(8,128)(2,1)} %get-tuple-element.29.cr_ref, ...), custom_call_target="tpu_custom_call" | custom-call | flops 30198988800 | bytes 17858560 | tf_op jit(solution)/shard_map/pallas_call | solution.py:260
  79.6 0.7 maximum_maximum_fusion.par_ref
  80.3 8.7 %shard_map.111.st_ref.refs_1_.par_ref = f32[8,640]{1,0:T(8,128)} custom-call(f32[8,640]{1,0:T(8,128)} %get-tuple-element.31.part_ref, f32[8,640]{1,0:T(8,128)} %maximum_maximum_fusion.par_ref), custom_call_target="tpu_custom_call" | custom-call | tf_op jit(solution)/shard_map/pallas_call | solution.py:185
  89.0 9.2 %act.1.refs_0_.u_ref = bf16[16,256,640]{2,1,0:T(8,128)(2,1)} custom-call(bf16[16,256,640]{2,1,0:T(8,128)(2,1)} %get-tuple-element.30.a_ref.refs_0_, f32[8,640]{1,0:T(8,128)} %shard_map.111.st_ref.refs_1_.par_ref), custom_call_target="tpu_custom_call" | custom-call | tf_op jit(solution)/shard_map/act/pallas_call | solution.py:396
  98.3 12.1 %shard_map.112 = (bf16[2,256,640]{2,1,0:T(8,128)(2,1)}, bf16[18,16,640]{2,1,0:T(8,128)(2,1)}, bf16[18,16,640]{2,1,0:T(8,128)(2,1)}) custom-call(bf16[16,256,640]{2,1,0:T(8,128)(2,1)} %act.1.refs_0_.u_ref), custom_call_target="tpu_custom_call" | custom-call | tf_op jit(solution)/shard_map/pallas_call | solution.py:126
  110.4 43.8 %shard_map.113 = f32[3,1920,640]{2,1,0:T(8,128)} custom-call(bf16[16,256,640]{2,1,0:T(8,128)(2,1)} %act.1.refs_0_.u_ref, bf16[2,256,640]{2,1,0:T(8,128)(2,1)} %get-tuple-element.32.rows_ref, bf16[18,16,640]{2,1,0:T(8,128)(2,1)} %get-tuple-element.33.cl_ref, bf16[18,16,640]{2,1,0:T(8,128)(2,1)} %get-tuple-element.34.cr_ref, bf16[16,256,640]{2,1,0:T(8,128)(2,1)} %bitcast.17), custom_call_target="tpu_custom_call" | custom-call | flops 30198988800 | bytes 25231360 | tf_op jit(solution)/shard_map/pallas_call | solution.py:360
  154.2 55.0 %shard_map.114 = (f32[16,256,640]{2,1,0:T(8,128)}, f32[8,640]{1,0:T(8,128)}) custom-call(bf16[16,256,640]{2,1,0:T(8,128)(2,1)} %bitcast.18, bf16[2,256,640]{2,1,0:T(8,128)(2,1)} %get-tuple-element.36.rows_ref, bf16[18,16,640]{2,1,0:T(8,128)(2,1)} %get-tuple-element.37.cl_ref, bf16[18,16,640]{2,1,0:T(8,128)(2,1)} %get-tuple-element.38.cr_ref, ...), custom_call_target="tpu_custom_call" | custom-call | flops 30198988800 | bytes 17858560 | tf_op jit(solution)/shard_map/pallas_call | solution.py:260
  209.2 7.9 %shard_map.115.t_ref = f32[8,640]{1,0:T(8,128)} custom-call(f32[8,640]{1,0:T(8,128)} %get-tuple-element.40.part_ref, f32[8,640]{1,0:T(8,128)} %shard_map.111.st_ref.refs_1_.par_ref), custom_call_target="tpu_custom_call" | custom-call | tf_op jit(solution)/shard_map/pallas_call | solution.py:185
  217.0 10.8 %da.1.v_ref.refs_0_.u_ref = bf16[16,256,640]{2,1,0:T(8,128)(2,1)} custom-call(f32[16,256,640]{2,1,0:T(8,128)} %get-tuple-element.39.dn_ref, bf16[16,256,640]{2,1,0:T(8,128)(2,1)} %get-tuple-element.30.a_ref.refs_0_, f32[8,640]{1,0:T(8,128)} %shard_map.111.st_ref.refs_1_.par_ref, f32[8,640]{1,0:T(8,128)} %shard_map.115.t_ref), custom_call_target="tpu_custom_call" | custom-call | tf_op jit(solution)/shard_map/da/pallas_call | solution.py:403
  227.8 43.8 %shard_map.116 = f32[3,1920,640]{2,1,0:T(8,128)} custom-call(bf16[16,256,640]{2,1,0:T(8,128)(2,1)} %bitcast.14, bf16[2,256,640]{2,1,0:T(8,128)(2,1)} %get-tuple-element.27.rows_ref, bf16[18,16,640]{2,1,0:T(8,128)(2,1)} %get-tuple-element.28.cl_ref, bf16[18,16,640]{2,1,0:T(8,128)(2,1)} %get-tuple-element.29.cr_ref, bf16[16,256,640]{2,1,0:T(8,128)(2,1)} %da.1.v_ref.refs_0_.u_ref), custom_call_target="tpu_custom_call" | custom-call | flops 30198988800 | bytes 25231360 | tf_op jit(solution)/shard_map/pallas_call | solution.py:360
  271.6 0.0 reduce-scatter.3.cloned.1.call-update
  271.7 0.0 reduce-scatter.5.cloned.1.call-start
  271.7 0.7 reduce-scatter.5.cloned.1.call-update
  272.4 0.0 all-gather.5.cloned.1.call-start
  272.5 96.6 %reduce-scatter.3.cloned.1.call-done = f32[720,640]{1,0:T(8,128)} async-done(((f32[5760,640]{1,0:T(8,128)}), f32[720,640]{1,0:T(8,128)}) %reduce-scatter.3.cloned.1.call-update) | async-done | bytes 1843216 | tf_op jit(solution)/shard_map/reduce_scatter | solution.py:371
  369.1 0.0 all-gather.5.cloned.1.call-update
  369.1 0.0 all-gather.9.cloned.1.call-start
  369.2 100.6 %reduce-scatter.5.cloned.1.call-done = f32[720,640]{1,0:T(8,128)} async-done(((f32[5760,640]{1,0:T(8,128)}), f32[720,640]{1,0:T(8,128)}) %reduce-scatter.5.cloned.1.call-update) | async-done | bytes 1843216 | tf_op jit(solution)/shard_map/reduce_scatter | solution.py:371
  469.8 0.0 all-gather.9.cloned.1.call-update
  469.8 0.0 all-gather.7.cloned.1.call-start
  469.9 75.2 %all-gather.5.cloned.1.call-done = f32[2880,640]{1,0:T(8,128)} async-done(((f32[720,640]{1,0:T(8,128)}), f32[2880,640]{1,0:T(8,128)}) %all-gather.5.cloned.1.call-update) | async-done | bytes 7372816 | tf_op jit(solution)/shard_map/all_gather | solution.py:372
  545.1 0.0 all-gather.7.cloned.1.call-update
  545.1 0.0 all-gather.11.cloned.1.call-start
  545.2 75.1 %all-gather.9.cloned.1.call-done = f32[2880,640]{1,0:T(8,128)} async-done(((f32[720,640]{1,0:T(8,128)}), f32[2880,640]{1,0:T(8,128)}) %all-gather.9.cloned.1.call-update) | async-done | bytes 7372816 | tf_op jit(solution)/shard_map/all_gather | solution.py:372
  620.2 0.0 all-gather.11.cloned.1.call-update
  620.2 12.0 %shard_map.118 = (bf16[2,256,640]{2,1,0:T(8,128)(2,1)}, bf16[18,16,640]{2,1,0:T(8,128)(2,1)}, bf16[18,16,640]{2,1,0:T(8,128)(2,1)}) custom-call(bf16[16,256,640]{2,1,0:T(8,128)(2,1)} %da.1.v_ref.refs_0_.u_ref), custom_call_target="tpu_custom_call" | custom-call | tf_op jit(solution)/shard_map/pallas_call | solution.py:126
  632.2 1.4 slice_reduce_fusion
  633.6 51.8 %shard_map.117 = bf16[16,256,640]{2,1,0:T(8,128)(2,1)} custom-call(bf16[16,256,640]{2,1,0:T(8,128)(2,1)} %act.1.refs_0_.u_ref, bf16[2,256,640]{2,1,0:T(8,128)(2,1)} %get-tuple-element.32.rows_ref, bf16[18,16,640]{2,1,0:T(8,128)(2,1)} %get-tuple-element.33.cl_ref, bf16[18,16,640]{2,1,0:T(8,128)(2,1)} %get-tuple-element.34.cr_ref, ...), custom_call_target="tpu_custom_call" | custom-call | flops 30198988800 | bytes 17858560 | tf_op jit(solution)/shard_map/pallas_call | solution.py:260
  685.5 49.7 %shard_map.119 = bf16[16,256,640]{2,1,0:T(8,128)(2,1)} custom-call(bf16[16,256,640]{2,1,0:T(8,128)(2,1)} %da.1.v_ref.refs_0_.u_ref, bf16[2,256,640]{2,1,0:T(8,128)(2,1)} %get-tuple-element.43.rows_ref, bf16[18,16,640]{2,1,0:T(8,128)(2,1)} %get-tuple-element.44.cl_ref, bf16[18,16,640]{2,1,0:T(8,128)(2,1)} %get-tuple-element.45.cr_ref, ...), custom_call_target="tpu_custom_call" | custom-call | flops 30198988800 | bytes 17858560 | tf_op jit(solution)/shard_map/pallas_call | solution.py:260
  735.2 0.0 all-gather.7.cloned.1.call-done
  735.2 0.0 all-gather.11.cloned.1.call-done
  735.2 11.6 %copy.14 = f32[3,3,640,640]{3,2,1,0:T(8,128)} copy(f32[3,3,640,640]{3,2,1,0:T(8,128)} %bitcast.9) | data formatting | bytes 29491200
  746.9 11.6 %copy.15 = f32[3,3,640,640]{3,2,1,0:T(8,128)} copy(f32[3,3,640,640]{3,2,1,0:T(8,128)} %bitcast.10) | data formatting | bytes 29491200
  (3 shorter events, 0.0 us)
Async XLA Ops:
  7.2 361.9 %reduce-scatter.3.cloned.1.call-start = ((), (), s32[]{:S(2)}) async-start(), calls=%async_computation.2 | async-start | bytes 16588800 | tf_op jit(solution)/shard_map/reduce_scatter | solution.py:371
  271.7 198.1 %reduce-scatter.5.cloned.1.call-start = ((), (), s32[]{:S(2)}) async-start(), calls=%async_computation.5 | async-start | bytes 16588800 | tf_op jit(solution)/shard_map/reduce_scatter | solution.py:371
  272.4 272.7 %all-gather.5.cloned.1.call-start = ((), (), s32[]{:S(2)}) async-start(), calls=%async_computation.3 | async-start | bytes 9216000 | tf_op jit(solution)/shard_map/all_gather | solution.py:372
  369.1 251.1 %all-gather.9.cloned.1.call-start = ((), (), s32[]{:S(2)}) async-start(), calls=%async_computation.6 | async-start | bytes 9216000 | tf_op jit(solution)/shard_map/all_gather | solution.py:372
  469.8 265.4 %all-gather.7.cloned.1.call-start = ((), (), s32[]{:S(2)}) async-start(), calls=%async_computation.4 | async-start | bytes 22118400 | tf_op jit(solution)/shard_map/all_gather | solution.py:373
  545.1 190.1 %all-gather.11.cloned.1.call-start = ((), (), s32[]{:S(2)}) async-start(), calls=%async_computation.7 | async-start | bytes 22118400 | tf_op jit(solution)/shard_map/all_gather | solution.py:373
Sparse Core Ops, SparseCore 0:
  271.8 97.2 reduce-scatter.2
  373.1 96.6 reduce-scatter.4
  471.6 73.4 all-gather.4
  546.7 73.4 all-gather.8
  621.6 24.3 all-gather.6
  647.3 25.4 all-gather.10

commit v2 on v1

--- a/solution.py
+++ b/solution.py
@@ -14,7 +14,6 @@
 F32 = jnp.float32
 BF16 = jnp.bfloat16
 MESH = pl.DeviceIdType.MESH
-EB = 16
 VMEM_LIMIT = 61 * 1024 * 1024
 ANY = pl.BlockSpec(memory_space=pl.ANY)
 VM = pl.BlockSpec(memory_space=pltpu.VMEM)
@@ -39,9 +38,9 @@
 
 
 def _halo_kernel(nh, nw, n_arr, *refs):
-    ins = refs[:n_arr]
-    outs = refs[n_arr:4 * n_arr]
-    send, recv = refs[4 * n_arr:]
+    ins = refs[:3 * n_arr]
+    outs = refs[3 * n_arr:6 * n_arr]
+    send, recv = refs[6 * n_arr:]
     th, tw, c = ins[0].shape
     w = lax.axis_index("w")
     h = lax.axis_index("x") * 2 + lax.axis_index("c")
@@ -69,18 +68,17 @@
     pl.semaphore_wait(barrier, nv * nz - 1)
 
     def parts(k, dh, dw):
-        u = ins[k]
+        u, first, last = ins[3 * k:3 * k + 3]
         rows, cl, cr = outs[3 * k:3 * k + 3]
         r = 0 if dh < 0 else th - 1
         to = 1 if dh < 0 else 0
         to18 = th + 1 if dh < 0 else 0
-        cs = slice(0, EB) if dw < 0 else slice(tw - EB, tw)
-        side = cr if dw < 0 else cl
+        edge, side = (first, cr) if dw < 0 else (last, cl)
         if dw == 0:
             return u.at[r], rows.at[to]
         if dh == 0:
-            return u.at[:, cs, :], side.at[1:th + 1]
-        return u.at[r, cs, :], side.at[to18]
+            return edge, side.at[1:th + 1]
+        return edge.at[r], side.at[to18]
 
     def copy(k, i, dh, dw):
         src, dst = parts(k, dh, dw)
@@ -103,9 +101,9 @@
                 if dw == 0:
                     rows[to] = jnp.zeros((tw, c), BF16)
                 elif dh == 0:
-                    side[1:th + 1] = jnp.zeros((th, EB, c), BF16)
+                    side[1:th + 1] = jnp.zeros((th, 1, c), F32)
                 else:
-                    side[to18] = jnp.zeros((EB, c), BF16)
+                    side[to18] = jnp.zeros((1, c), F32)
     for k in range(n_arr):
         for i, (dh, dw) in enumerate(dirs):
             @pl.when(has(dh, dw))
@@ -119,12 +117,12 @@
 
 def _halo(nh, nw, cid, *us):
     th, tw, c = us[0].shape
-    n = len(us)
+    n = len(us) // 3
     out = []
-    for _ in us:
-        out += [jax.ShapeDtypeStruct((2, tw, c), BF16), jax.ShapeDtypeStruct((th + 2, EB, c), BF16), jax.ShapeDtypeStruct((th + 2, EB, c), BF16)]
+    for _ in range(n):
+        out += [jax.ShapeDtypeStruct((2, tw, c), BF16), jax.ShapeDtypeStruct((th + 2, 1, c), F32), jax.ShapeDtypeStruct((th + 2, 1, c), F32)]
     res = pl.pallas_call(
-        functools.partial(_halo_kernel, nh, nw, n), out_shape=out, in_specs=[ANY] * n, out_specs=[VM] * (3 * n),
+        functools.partial(_halo_kernel, nh, nw, n), out_shape=out, in_specs=[ANY] * (3 * n), out_specs=[VM] * (3 * n),
         scratch_shapes=[pltpu.SemaphoreType.DMA((8 * n,)), pltpu.SemaphoreType.DMA((8 * n,))],
         compiler_params=pltpu.CompilerParams(collective_id=cid, has_side_effects=True, vmem_limit_bytes=VMEM_LIMIT),
     )(*us)
@@ -210,8 +208,8 @@
         idx = lax.broadcasted_iota(jnp.int32, (tw, ck), 0)
         for k in range(c // ck):
             f = p[r, :, c + k * ck:c + (k + 1) * ck].astype(F32)
-            lo = cl_ref[r, :, k * ck:(k + 1) * ck].astype(F32)[EB - 1:EB]
-            hi = cr_ref[r, :, k * ck:(k + 1) * ck].astype(F32)[0:1]
+            lo = cl_ref[r, :, k * ck:(k + 1) * ck]
+            hi = cr_ref[r, :, k * ck:(k + 1) * ck]
             p[r, :, k * ck:(k + 1) * ck] = jnp.where(idx == 0, lo, pltpu.roll(f, 1, 0)).astype(BF16)
             p[r, :, 2 * c + k * ck:2 * c + (k + 1) * ck] = jnp.where(idx == tw - 1, hi, pltpu.roll(f, tw - 1, 0)).astype(BF16)
         return 0
@@ -256,7 +254,7 @@
 
 def _conv(transposed, epilogue, u, halo, w, extra, extra_specs, outs, out_specs, rb=2):
     th, tw, c = u.shape
-    full = pl.BlockSpec((th + 2, EB, c), lambda i: (0, 0, 0), pipeline_mode=pl.Buffered(1))
+    full = pl.BlockSpec((th + 2, 1, c), lambda i: (0, 0, 0), pipeline_mode=pl.Buffered(1))
     return pl.pallas_call(
         functools.partial(_conv_kernel, transposed, rb, len(extra), epilogue),
         grid=(th // rb,), out_shape=outs, in_specs=[ANY, ANY, full, full, ANY] + extra_specs, out_specs=out_specs,
@@ -284,12 +282,6 @@
     @pl.when(i > 0)
     def _():
         s_ref[...] += s
-
-
-def _ep_residual(i, acc, extra, outs):
-    o_ref = outs[0]
-    r = extra[0][...].astype(F32).reshape(acc.shape)
-    o_ref[...] = (acc + r).astype(BF16).reshape(o_ref.shape)
 
 
 def _ep_dz(i, acc, extra, outs):
@@ -313,17 +305,26 @@
         s_ref[...] += s
 
 
-def _z_kernel(a_ref, st_ref, z_ref):
+def _edges(v, first_ref, last_ref):
+    first_ref[...] = v[:, 0:1, :]
+    last_ref[...] = v[:, v.shape[1] - 1:, :]
+
+
+def _z_kernel(a_ref, st_ref, z_ref, first_ref, last_ref):
     st = st_ref[...]
     xhat = (a_ref[...].astype(F32) - st[0:1]) * st[1:2]
-    z_ref[...] = _gelu(xhat * st[2:3] + st[3:4]).astype(BF16)
-
-
-def _da_kernel(dn_ref, a_ref, st_ref, t_ref, o_ref):
+    z = _gelu(xhat * st[2:3] + st[3:4]).astype(BF16)
+    z_ref[...] = z
+    _edges(z.astype(F32), first_ref, last_ref)
+
+
+def _da_kernel(dn_ref, a_ref, st_ref, t_ref, o_ref, first_ref, last_ref):
     st = st_ref[...]
     t = t_ref[...]
     xhat = (a_ref[...].astype(F32) - st[0:1]) * st[1:2]
-    o_ref[...] = (st[1:2] * (dn_ref[...] * st[2:3] - t[3:4] - xhat * t[2:3])).astype(BF16)
+    da = (st[1:2] * (dn_ref[...] * st[2:3] - t[3:4] - xhat * t[2:3])).astype(BF16)
+    o_ref[...] = da
+    _edges(da.astype(F32), first_ref, last_ref)
 
 
 def _wgrad_kernel(u_ref, rows_ref, cl_ref, cr_ref, v_ref, o_ref, p, vt, psem):
@@ -355,7 +356,7 @@
 
 def _wgrad(u, halo, v):
     th, tw, c = u.shape
-    full = pl.BlockSpec((th + 2, EB, c), lambda i: (0, 0, 0), pipeline_mode=pl.Buffered(1))
+    full = pl.BlockSpec((th + 2, 1, c), lambda i: (0, 0, 0), pipeline_mode=pl.Buffered(1))
     fv = pl.BlockSpec((th, tw, c), lambda i: (0, 0, 0), pipeline_mode=pl.Buffered(1))
     return pl.pallas_call(
         _wgrad_kernel, grid=(3,), out_shape=jax.ShapeDtypeStruct((3, 3 * c, c), F32),
@@ -366,11 +367,223 @@
     )(u, *halo, v)
 
 
+TICKS = (2, 3, 4, 6, 8, 9, 11, 13, 15, 17, 18, 20, 21, 22)
+
+
+def _tail_kernel(u_ref, urows, ucl, ucr, v_ref, vrows, vcl, vcr, z_ref, zrows, zcl, zcr, w1_ref, w2_ref, xb_ref, gb_ref,
+                 y_ref, dx_ref, dw_ref, p, vt, wb, dsend, hown, recv0, recv1, recv2, psem, wsem, vsem, send, recv, lsem):
+    i = pl.program_id(0)
+    th, tw, c = u_ref.shape
+    nt = 9
+    half, q, e, sub = c // 2, c // 4, c // 8, c // 16
+    wi, xi, ci = lax.axis_index("w"), lax.axis_index("x"), lax.axis_index("c")
+    mate, xn, yn = (wi, xi, 1 - ci), (wi, 1 - xi, ci), (1 - wi, xi, ci)
+    pa, pb = xi * e, q + wi * e
+    fa, fb = pa + wi * sub, pb + xi * sub
+
+    def rows(start, n):
+        return pl.ds(pl.multiple_of(start, 8), n)
+
+    def rc(stage, t, src, dst, dev):
+        return pltpu.make_async_remote_copy(src_ref=src, dst_ref=dst, send_sem=send.at[stage, t], recv_sem=recv.at[stage, t],
+                                            device_id=dev, device_id_type=MESH)
+
+    def base(t):
+        return t * c + ci * half
+
+    def s0(t):
+        return [rc(0, t, dsend.at[lax.rem(t, 2)], recv0.at[lax.rem(t, 2)], mate)]
+
+    def s1(t):
+        return [rc(1, t, hown.at[t, rows((1 - xi) * e, e)], recv1.at[t, 0], xn),
+                rc(2, t, hown.at[t, rows(q + (1 - wi) * e, e)], recv1.at[t, 1], yn)]
+
+    def s2(t):
+        return [rc(3, t, hown.at[t, rows(pa + (1 - wi) * sub, sub)], recv2.at[t, 0], yn),
+                rc(4, t, hown.at[t, rows(pb + (1 - xi) * sub, sub)], recv2.at[t, 1], xn)]
+
+    def s3(t):
+        return [rc(5, t, hown.at[t, rows(fa, sub)], dw_ref.at[rows(base(t) + fa, sub)], yn),
+                rc(6, t, hown.at[t, rows(fb, sub)], dw_ref.at[rows(base(t) + fb, sub)], xn)]
+
+    def keep(t):
+        return [pltpu.make_async_copy(hown.at[t, rows(fa, sub)], dw_ref.at[rows(base(t) + fa, sub)], lsem.at[0, t]),
+                pltpu.make_async_copy(hown.at[t, rows(fb, sub)], dw_ref.at[rows(base(t) + fb, sub)], lsem.at[1, t])]
+
+    def s4(t):
+        return [rc(7, t, dw_ref.at[rows(base(t) + pa, e)], dw_ref.at[rows(base(t) + pa, e)], xn),
+                rc(8, t, dw_ref.at[rows(base(t) + pb, e)], dw_ref.at[rows(base(t) + pb, e)], yn)]
+
+    def s5(t):
+        return [rc(9, t, dw_ref.at[rows(base(t), half)], dw_ref.at[rows(base(t), half)], mate)]
+
+    def start(cps):
+        for cp in cps:
+            cp.start()
+
+    def when_chunk(t, f):
+        @pl.when(jnp.logical_and(t >= 0, t < nt))
+        def _():
+            f(t)
+
+    def tick(j):
+        def t2(t):
+            for cp in s1(t):
+                cp.wait_recv()
+            hown[t, rows(pa, e), :] += recv1[t, 0]
+            hown[t, rows(pb, e), :] += recv1[t, 1]
+
+        def t3(t):
+            for cp in s2(t):
+                cp.wait_recv()
+            hown[t, rows(fa, sub), :] += recv2[t, 0]
+            hown[t, rows(fb, sub), :] += recv2[t, 1]
+
+        def t4(t):
+            for cp in s3(t):
+                cp.wait_recv()
+            for cp in keep(t):
+                cp.wait()
+            start(s4(t))
+
+        def t5(t):
+            for cp in s4(t):
+                cp.wait_recv()
+            start(s5(t))
+
+        def t6(t):
+            for cp in s5(t):
+                cp.wait_recv()
+            for cp in s1(t) + s2(t) + s3(t) + s4(t) + s5(t):
+                cp.wait_send()
+
+        when_chunk(j, lambda t: start(s1(t)))
+        when_chunk(j - 1, t2)
+        when_chunk(j - 2, t3)
+        when_chunk(j - 3, t4)
+        when_chunk(j - 4, t5)
+        when_chunk(j - 1, lambda t: start(s2(t)))
+        when_chunk(j - 2, lambda t: start(s3(t) + keep(t)))
+        when_chunk(j - 5, t6)
+
+    @pl.when(i == 0)
+    def _():
+        vc = pltpu.make_async_copy(v_ref, p.at[1:th + 1, :, 0:c], vsem)
+        vc.start()
+        cps = _load_patches(u_ref, urows, p, psem)
+        pltpu.make_async_copy(w2_ref, wb, wsem.at[0]).start()
+        barrier = pltpu.get_barrier_semaphore()
+        for d in (mate, xn, yn):
+            pl.semaphore_signal(barrier, inc=1, device_id=d, device_id_type=MESH)
+        pl.semaphore_wait(barrier, 3)
+        vc.wait()
+
+        def tr(r, _):
+            vt[:, pl.ds(pl.multiple_of(r * tw, tw), tw)] = p[r + 1, :, 0:c].T
+            return 0
+
+        lax.fori_loop(0, th, tr, 0)
+        for cp in cps:
+            cp.wait()
+        _shift_patches(p, ucl, ucr)
+
+    @pl.when(jnp.logical_and(i >= 2, i < nt + 2))
+    def _():
+        t = i - 2
+        for cp in s0(t):
+            cp.wait()
+        hown[t] += recv0[lax.rem(t, 2)]
+
+    @pl.when(jnp.logical_and(i >= 1, i < nt + 1))
+    def _():
+        start(s0(i - 1))
+
+    @pl.when(i == nt)
+    def _():
+        cps = _load_patches(z_ref, zrows, p, psem)
+        pltpu.make_async_copy(w2_ref, wb, wsem.at[0]).wait()
+        for cp in cps:
+            cp.wait()
+        _shift_patches(p, zcl, zcr)
+
+    @pl.when(i == nt + 8)
+    def _():
+        cps = _load_patches(v_ref, vrows, p, psem)
+        ws = [pltpu.make_async_copy(w1_ref.at[8 - k], wb.at[k], wsem.at[k]) for k in range(9)]
+        start(ws)
+        for cp in cps:
+            cp.wait()
+        _shift_patches(p, vcl, vcr)
+        for cp in ws:
+            cp.wait()
+
+    j = jnp.int32(-1)
+    now = jnp.int32(0)
+    for s in TICKS:
+        j = j + jnp.where(i >= s, 1, 0)
+        now = now + jnp.where(i == s, 1, 0)
+
+    @pl.when(now > 0)
+    def _():
+        tick(j)
+
+    @pl.when(i < nt)
+    def _():
+        a = lax.div(i, 3)
+        b = lax.rem(i, 3)
+        rhs = p[pl.ds(a, th), :, pl.ds(pl.multiple_of(b * c, 128), c)].reshape(th * tw, c)
+        d = jnp.dot(vt[...], rhs, preferred_element_type=F32).T
+        hown[i] = jnp.where(ci == 0, d[:half], d[half:])
+        dsend[lax.rem(i, 2)] = jnp.where(ci == 0, d[half:], d[:half])
+
+    def conv(ib, transposed, r_ref, o_ref):
+        acc = None
+        for a in range(3):
+            lhs = p[pl.ds(ib * 2 + a, 2)].reshape(2 * tw, 3 * c)
+            if transposed:
+                rhs = jnp.concatenate([wb[3 * a], wb[3 * a + 1], wb[3 * a + 2]], axis=1)
+                d = lax.dot_general(lhs, rhs, (((1,), (1,)), ((), ())), preferred_element_type=F32)
+            else:
+                d = jnp.dot(lhs, wb[3 * a:3 * a + 3].reshape(3 * c, c), preferred_element_type=F32)
+            acc = d if acc is None else acc + d
+        r = r_ref[...].astype(F32).reshape(acc.shape)
+        o_ref[...] = (acc + r).astype(BF16).reshape(o_ref.shape)
+
+    @pl.when(jnp.logical_and(i >= nt, i < nt + 8))
+    def _():
+        conv(i - nt, False, xb_ref, y_ref)
+
+    @pl.when(i >= nt + 8)
+    def _():
+        conv(i - nt - 8, True, gb_ref, dx_ref)
+
+
+def _tail(x, xh, da, dah, z, zh, w1, w2, g):
+    th, tw, c = x.shape
+    nt, half = 9, c // 2
+    full = pl.BlockSpec((th + 2, 1, c), lambda i: (0, 0, 0), pipeline_mode=pl.Buffered(1))
+    yb = pl.BlockSpec((2, tw, c), lambda i: (jnp.minimum(jnp.maximum(i - nt, 0), 7), 0, 0))
+    xb = pl.BlockSpec((2, tw, c), lambda i: (jnp.maximum(i - nt - 8, 0), 0, 0))
+    img = [ANY, ANY, full, full]
+    dma = pltpu.SemaphoreType.DMA
+    return pl.pallas_call(
+        _tail_kernel, grid=(nt + 16,),
+        out_shape=[jax.ShapeDtypeStruct((th, tw, c), BF16), jax.ShapeDtypeStruct((th, tw, c), BF16), jax.ShapeDtypeStruct((nt * c, c), F32)],
+        in_specs=img * 3 + [ANY, ANY, yb, xb], out_specs=[yb, xb, ANY],
+        scratch_shapes=[pltpu.VMEM((th + 2, tw, 3 * c), BF16), pltpu.VMEM((c, th * tw), BF16), pltpu.VMEM((9, c, c), BF16),
+                        pltpu.VMEM((2, half, c), F32), pltpu.VMEM((nt, half, c), F32), pltpu.VMEM((2, half, c), F32),
+                        pltpu.VMEM((nt, 2, c // 8, c), F32), pltpu.VMEM((nt, 2, c // 16, c), F32),
+                        dma((3,)), dma((9,)), dma, dma((10, nt)), dma((10, nt)), dma((2, nt))],
+        compiler_params=pltpu.CompilerParams(dimension_semantics=("arbitrary",), vmem_limit_bytes=VMEM_LIMIT, collective_id=5, has_side_effects=True),
+        cost_estimate=pl.CostEstimate(flops=3 * 2 * 9 * th * tw * c * c, bytes_accessed=16 * th * tw * c, transcendentals=0),
+        name="tail",
+    )(x, *xh, da, *dah, z, *zh, w1.reshape(9, c, c), w2.reshape(9, c, c), x, g)
+
+
 def _reduce_all(d):
     r, k, c = d.shape
     s = lax.psum_scatter(d.reshape(r * k, c), ("c", "w", "x"), scatter_dimension=0, tiled=True)
-    s = lax.all_gather(s, ("w", "x"), axis=0, tiled=True)
-    return lax.all_gather(s, "c", axis=0, tiled=True).reshape(3, 3, c, c)
+    return lax.all_gather(s, ("c", "w", "x"), axis=0, tiled=True).reshape(3, 3, c, c)
 
 
 def solution(mesh):
@@ -390,23 +603,25 @@
         sums = jax.ShapeDtypeStruct((8, c), F32)
         par = jnp.concatenate([jnp.zeros((2, c), F32), gamma[None], beta[None], jnp.zeros((4, c), F32)])
 
-        xh, gh = _halo(nh, nw, 0, x, g)
+        edge = jax.ShapeDtypeStruct((th, 1, c), F32)
+        eblk = pl.BlockSpec((rb, 1, c), lambda i: (i, 0, 0))
+
+        def with_edges(u):
+            return u, u[:, 0:1, :].astype(F32), u[:, tw - 1:, :].astype(F32)
+
+        xh, gh = _halo(nh, nw, 0, *with_edges(x), *with_edges(g))
         a, s = _conv(False, _ep_conv1, x, xh, w1, [], [], [img16, sums], [blk, small])
         st = _allsum(nh, nw, cnt, 0, 1, s, par)
-        z = pl.pallas_call(_z_kernel, grid=(th // rb,), out_shape=img16, in_specs=[blk, small], out_specs=blk, name="act")(a, st)
-        (zh,) = _halo(nh, nw, 2, z)
+        z, z0, z1 = pl.pallas_call(_z_kernel, grid=(th // rb,), out_shape=[img16, edge, edge], in_specs=[blk, small], out_specs=[blk, eblk, eblk], name="act")(a, st)
+        (zh,) = _halo(nh, nw, 2, z, z0, z1)
         d2 = _wgrad(z, zh, g)
         g_late, d2 = lax.optimization_barrier((g, d2))
         dw2 = _reduce_all(d2)
         dn, t = _conv(True, _ep_dz, g_late, gh, w2, [a, st], [blk, small], [img32, sums], [blk, small])
         t = _allsum(nh, nw, cnt, 1, 3, t, st)
-        da = pl.pallas_call(_da_kernel, grid=(th // rb,), out_shape=img16, in_specs=[blk, blk, small, small], out_specs=blk, name="da")(dn, a, st, t)
-        (dah,) = _halo(nh, nw, 4, da)
-        d1 = _wgrad(x, xh, da)
-        z_late, da_late, d1 = lax.optimization_barrier((z, da, d1))
-        dw1 = _reduce_all(d1)
-        (y,) = _conv(False, _ep_residual, z_late, zh, w2, [x], [blk], [img16], [blk])
-        (dx,) = _conv(True, _ep_residual, da_late, dah, w1, [g], [blk], [img16], [blk])
-        return y[None], dx[None], dw1, dw2, t[0], t[1]
+        da, da0, da1 = pl.pallas_call(_da_kernel, grid=(th // rb,), out_shape=[img16, edge, edge], in_specs=[blk, blk, small, small], out_specs=[blk, eblk, eblk], name="da")(dn, a, st, t)
+        (dah,) = _halo(nh, nw, 4, da, da0, da1)
+        y, dx, dw1 = _tail(x, xh, da, dah, z, zh, w1, w2, g)
+        return y[None], dx[None], dw1.reshape(3, 3, c, c), dw2, t[0], t[1]
 
     return jax.shard_map(body, mesh=mesh3, in_specs=(tile, P(), P(), P(), P(), tile), out_specs=(tile, tile, P(), P(), P(), P()), check_vma=False)

time: 766 us -> 543 us (0.71)
  waiting for transfers between devices: 348 us -> 101 us
  Pallas kernels: 376 us -> 391 us
  local copies, waits for them, and re-layouts: 26.2 us -> 34.2 us
    pallas_call x2 -> x3, Pallas kernels: 20 us -> 200 us  [the longest x1 180 us: _tail(): pl.pallas_call(_tail_kernel, grid=(nt + 16,), out_shape=[jax.ShapeDtypeSt...]
    all_gather x4 -> x1, waiting for transfers between devices: 150 us -> 0.01 us  [_reduce_all(): lax.all_gather(s, ('c', 'w', 'x'), axis=0, tiled=True).reshape(3, 3, c, c)]
    pallas_call x4 -> x2, Pallas kernels: 206 us -> 104 us  [_conv(): pl.pallas_call(functools.partial(_conv_kernel, transposed, rb, len(extra)...]
    reduce_scatter x2 -> x1, waiting for transfers between devices: 197 us -> 101 us  [_reduce_all(): lax.psum_scatter(d.reshape(r * k, c), ('c', 'w', 'x'), scatter_dimension=...]
    pallas_call x2 -> x1, Pallas kernels: 87.6 us -> 43.7 us  [_wgrad(): pl.pallas_call(_wgrad_kernel, grid=(3,), out_shape=jax.ShapeDtypeStruct((...]
    pallas_call x3, Pallas kernels: 45.6 us -> 19.4 us  [_halo(): pl.pallas_call(functools.partial(_halo_kernel, nh, nw, n), out_shape=out,...]
    unnamed x2 -> x6, local copies, waits for them, and re-layouts: 23.3 us -> 31.3 us
  transfers between devices with their start and end apart: 6 -> 2, of which waited for: 4 -> 1; matrix products, arithmetic and copies ran while one was open for 0% -> 0% of each run, Pallas kernels for 15% -> 48%
where the time goes in v2:
time: 543 us; the launch traced here: 542 us
  Pallas kernels  391 us (72%)
  waiting for transfers between devices  101 us (19%)
  local copies, waits for them, and re-layouts  34.2 us (6%)
  between operations  14.1 us (3%)
    pallas_call x1, Pallas kernels, _tail(): pl.pallas_call(_tail_kernel, grid=(nt + 16,), out_shape=[jax.ShapeDtypeSt...  180 us
    pallas_call x2, Pallas kernels, _conv(): pl.pallas_call(functools.partial(_conv_kernel, transposed, rb, len(extra)...  104 us
    reduce_scatter x1, waiting for transfers between devices, _reduce_all(): lax.psum_scatter(d.reshape(r * k, c), ('c', 'w', 'x'), scatter_dimension=...  101 us
    pallas_call x1, Pallas kernels, _wgrad(): pl.pallas_call(_wgrad_kernel, grid=(3,), out_shape=jax.ShapeDtypeStruct((...  43.7 us
    unnamed x6, local copies, waits for them, and re-layouts  31.3 us
    pallas_call x2, Pallas kernels, _allsum(): pl.pallas_call(functools.partial(_allsum_kernel, nh, nw, cnt, mode), out_...  24 us
    pallas_call x3, Pallas kernels, _halo(): pl.pallas_call(functools.partial(_halo_kernel, nh, nw, n), out_shape=out,...  19.4 us
  transfers between devices with their start and end apart: 2, of which 1 were waited for; matrix products, arithmetic and copies ran while one was open for 0% of the time, Pallas kernels for 48%

profile of v2, /device:TPU:0, one launch (start us, length us, event | category | flops | bytes accessed | tf_op | source)
XLA Modules:
  0.0 542.4 jit_solution(943635369219232416)
XLA Ops:
  7.2 0.0 reduce-scatter.2.cloned.1.call-start
  7.2 0.1 pad.3.clone
  7.3 0.7 broadcast_in_dim.19
  8.0 0.7 broadcast_in_dim.20
  8.7 1.9 slice_convert_fusion
  10.6 0.7 maximum_maximum_fusion.par_ref
  11.3 8.0 %shard_map.109 = (bf16[2,256,640]{2,1,0:T(8,128)(2,1)}, f32[18,1,640]{2,1,0:T(1,128)}, f32[18,1,640]{2,1,0:T(1,128)}, bf16[2,256,640]{2,1,0:T(8,128)(2,1)}, f32[...) custom-call(bf16[16,256,640]{2,1,0:T(8,128)(2,1)} %bitcast.13, f32[16,1,640]{2,1,0:T(1,128)} %get-tuple-element.66.refs_1_, ...), custom_call_target="tpu_custom_call" | custom-call | tf_op jit(solution)/shard_map/pallas_call | solution.py:124
  19.2 49.0 %shard_map.110 = (bf16[16,256,640]{2,1,0:T(8,128)(2,1)}, f32[8,640]{1,0:T(8,128)}) custom-call(bf16[16,256,640]{2,1,0:T(8,128)(2,1)} %bitcast.14, bf16[2,256,640]{2,1,0:T(8,128)(2,1)} %get-tuple-element.33.rows_ref.urows, f32[18,1,640]{2,1,0:T(1,128)} %get-tuple-element.34.cl_ref.ucl, f32[18,1,640]{2,1,0:T(1,128)} %get-tuple-element.35.cr_ref.ucr, ...), custom_call_target="tpu_custom_call" | custom-call | flops 30198988800 | bytes 17858560 | tf_op jit(solution)/shard_map/pallas_call | solution.py:258
  68.3 14.5 %shard_map.111.st_ref.refs_1_.par_ref = f32[8,640]{1,0:T(8,128)} custom-call(f32[8,640]{1,0:T(8,128)} %get-tuple-element.37.part_ref, f32[8,640]{1,0:T(8,128)} %maximum_maximum_fusion.par_ref), custom_call_target="tpu_custom_call" | custom-call | tf_op jit(solution)/shard_map/pallas_call | solution.py:183
  82.8 9.3 %act.1 = (bf16[16,256,640]{2,1,0:T(8,128)(2,1)}, f32[16,1,640]{2,1,0:T(1,128)}, f32[16,1,640]{2,1,0:T(1,128)}) custom-call(bf16[16,256,640]{2,1,0:T(8,128)(2,1)} %get-tuple-element.36.a_ref.refs_0_, f32[8,640]{1,0:T(8,128)} %shard_map.111.st_ref.refs_1_.par_ref), custom_call_target="tpu_custom_call" | custom-call | tf_op jit(solution)/shard_map/act/pallas_call | solution.py:615
  92.1 5.4 shard_map.112
  97.5 43.7 %shard_map.113 = f32[3,1920,640]{2,1,0:T(8,128)} custom-call(bf16[16,256,640]{2,1,0:T(8,128)(2,1)} %get-tuple-element.38.refs_0_.u_ref.z_ref, bf16[2,256,640]{2,1,0:T(8,128)(2,1)} %get-tuple-element.41.rows_ref.zrows, f32[18,1,640]{2,1,0:T(1,128)} %get-tuple-element.42.cl_ref.zcl, f32[18,1,640]{2,1,0:T(1,128)} %get-tuple-element.43.cr_ref.zcr, ...), custom_call_target="tpu_custom_call" | custom-call | flops 30198988800 | bytes 25231360 | tf_op jit(solution)/shard_map/pallas_call | solution.py:361
  141.1 0.0 reduce-scatter.2.cloned.1.call-update
  141.2 0.3 all-gather.2.cloned.1.call-start
  141.4 100.7 %reduce-scatter.2.cloned.1.call-done = f32[720,640]{1,0:T(8,128)} async-done(((f32[5760,640]{1,0:T(8,128)}), f32[720,640]{1,0:T(8,128)}) %reduce-scatter.2.cloned.1.call-update) | async-done | bytes 1843216 | tf_op jit(solution)/shard_map/reduce_scatter | solution.py:585
  242.1 0.0 all-gather.2.cloned.1.call-update
  242.1 54.8 %shard_map.114 = (f32[16,256,640]{2,1,0:T(8,128)}, f32[8,640]{1,0:T(8,128)}) custom-call(bf16[16,256,640]{2,1,0:T(8,128)(2,1)} %bitcast.20, bf16[2,256,640]{2,1,0:T(8,128)(2,1)} %get-tuple-element.45.rows_ref, f32[18,1,640]{2,1,0:T(1,128)} %get-tuple-element.46.cl_ref, f32[18,1,640]{2,1,0:T(1,128)} %get-tuple-element.47.cr_ref, ...), custom_call_target="tpu_custom_call" | custom-call | flops 30198988800 | bytes 17858560 | tf_op jit(solution)/shard_map/pallas_call | solution.py:258
  297.0 9.5 %shard_map.115.t_ref = f32[8,640]{1,0:T(8,128)} custom-call(f32[8,640]{1,0:T(8,128)} %get-tuple-element.49.part_ref, f32[8,640]{1,0:T(8,128)} %shard_map.111.st_ref.refs_1_.par_ref), custom_call_target="tpu_custom_call" | custom-call | tf_op jit(solution)/shard_map/pallas_call | solution.py:183
  306.4 10.5 %da.1 = (bf16[16,256,640]{2,1,0:T(8,128)(2,1)}, f32[16,1,640]{2,1,0:T(1,128)}, f32[16,1,640]{2,1,0:T(1,128)}) custom-call(f32[16,256,640]{2,1,0:T(8,128)} %get-tuple-element.48.dn_ref, bf16[16,256,640]{2,1,0:T(8,128)(2,1)} %get-tuple-element.36.a_ref.refs_0_, f32[8,640]{1,0:T(8,128)} %shard_map.111.st_ref.refs_1_.par_ref, f32[8,640]{1,0:T(8,128)} %shard_map.115.t_ref), custom_call_target="tpu_custom_call" | custom-call | tf_op jit(solution)/shard_map/da/pallas_call | solution.py:622
  316.9 6.1 %shard_map.116 = (bf16[2,256,640]{2,1,0:T(8,128)(2,1)}, f32[18,1,640]{2,1,0:T(1,128)}, f32[18,1,640]{2,1,0:T(1,128)}) custom-call(bf16[16,256,640]{2,1,0:T(8,128)(2,1)} %get-tuple-element.50.refs_0_.v_ref, f32[16,1,640]{2,1,0:T(1,128)} %get-tuple-element.51.refs_1_, f32[16,1,640]{2,1,0:T(1,128)} %get-tuple-element.52.refs_2_), custom_call_target="tpu_custom_call" | custom-call | tf_op jit(solution)/shard_map/pallas_call | solution.py:124
  323.1 179.8 %tail.1 = (bf16[16,256,640]{2,1,0:T(8,128)(2,1)}, bf16[16,256,640]{2,1,0:T(8,128)(2,1)}, f32[5760,640]{1,0:T(8,128)}) custom-call(bf16[16,256,640]{2,1,0:T(8,128)(2,1)} %bitcast.15, bf16[2,256,640]{2,1,0:T(8,128)(2,1)} %get-tuple-element.33.rows_ref.urows, f32[18,1,640]{2,1,0:T(1,128)} %get-tuple-element.34.cl_ref.ucl, ...), custom_call_target="tpu_custom_call" | custom-call | flops 90596966400 | bytes 41943040 | tf_op jit(solution)/shard_map/tail/pallas_call | solution.py:569
  502.8 1.4 slice_reduce_fusion
  504.3 0.0 all-gather.2.cloned.1.call-done
  504.3 0.0 copy-start
  504.3 5.7 %copy.16 = bf16[1,16,256,640]{3,2,1,0:T(8,128)(2,1)} copy(bf16[1,16,256,640]{3,2,1,0:T(8,128)(2,1)} %bitcast.23) | data formatting | bytes 10485760
  509.9 0.0 copy-done
  509.9 2.4 copy.17
  512.3 11.6 %copy.18 = f32[3,3,640,640]{3,2,1,0:T(8,128)} copy(f32[3,3,640,640]{3,2,1,0:T(8,128)} %bitcast.10) | data formatting | bytes 29491200
  523.9 11.6 %copy.19 = f32[3,3,640,640]{3,2,1,0:T(8,128)} copy(f32[3,3,640,640]{3,2,1,0:T(8,128)} %bitcast.9) | data formatting | bytes 29491200
  (3 shorter events, 0.0 us)
Async XLA Ops:
  7.2 234.9 %reduce-scatter.2.cloned.1.call-start = ((), (), s32[]{:S(2)}) async-start(), calls=%async_computation.1 | async-start | bytes 16588800 | tf_op jit(solution)/shard_map/reduce_scatter | solution.py:585
  141.2 363.1 %all-gather.2.cloned.1.call-start = ((), (), s32[]{:S(2)}) async-start(), calls=%async_computation.2 | async-start | bytes 16588800 | tf_op jit(solution)/shard_map/all_gather | solution.py:586
  504.3 5.7 %copy-start = (bf16[16,256,640]{2,1,0:T(8,128)(2,1)S(1)}, bf16[16,256,640]{2,1,0:T(8,128)(2,1)}, u32[]{:S(2)}) copy-start(bf16[16,256,640]{2,1,0:T(8,128)(2,1)} %get-tuple-element.57) | copy-start | bytes 15728644
Sparse Core Ops, SparseCore 0:
  141.3 100.7 reduce-scatter.1
  243.9 77.3 all-gather.1

commit v3 on v2

--- a/solution.py
+++ b/solution.py
@@ -7,7 +7,6 @@
 from jax.experimental.pallas import tpu as pltpu
 from jax.sharding import Mesh
 from jax.sharding import PartitionSpec as P
-
 
 GROUPS = 32
 EPS = 1e-5
@@ -92,7 +91,7 @@
                 copy(k, i, *d).start()
     for k in range(n_arr):
         rows, cl, cr = outs[3 * k:3 * k + 3]
-        for dh, dw in dirs:
+        for i, (dh, dw) in enumerate(dirs):
             @pl.when(jnp.logical_not(has(-dh, -dw)))
             def _(rows=rows, cl=cl, cr=cr, dh=dh, dw=dw):
                 to = 1 if dh < 0 else 0
@@ -125,6 +124,7 @@
         functools.partial(_halo_kernel, nh, nw, n), out_shape=out, in_specs=[ANY] * (3 * n), out_specs=[VM] * (3 * n),
         scratch_shapes=[pltpu.SemaphoreType.DMA((8 * n,)), pltpu.SemaphoreType.DMA((8 * n,))],
         compiler_params=pltpu.CompilerParams(collective_id=cid, has_side_effects=True, vmem_limit_bytes=VMEM_LIMIT),
+        name=f"halo{cid}",
     )(*us)
     return [tuple(res[3 * k:3 * k + 3]) for k in range(n)]
 
@@ -186,6 +186,7 @@
         scratch_shapes=[pltpu.VMEM((8, c), F32), pltpu.VMEM((n - 1, 8, c), F32), pltpu.SemaphoreType.DMA,
                         pltpu.SemaphoreType.DMA((n - 1,)), pltpu.SemaphoreType.DMA((n - 1,))],
         compiler_params=pltpu.CompilerParams(collective_id=cid, has_side_effects=True, vmem_limit_bytes=VMEM_LIMIT),
+        name=f"allsum{cid}",
     )(part, par)
 
 
@@ -217,9 +218,8 @@
     lax.fori_loop(0, n, row, 0)
 
 
-def _conv_kernel(transposed, rb, n_extra, epilogue, u_ref, rows_ref, cl_ref, cr_ref, w_ref, *refs):
-    extra = refs[:n_extra]
-    outs = refs[n_extra:-4]
+def _conv_kernel(rb, epilogue, u_ref, rows_ref, cl_ref, cr_ref, w_ref, *refs):
+    outs = refs[:-4]
     p, wb, psem, wsem = refs[-4:]
     c = u_ref.shape[2]
     i = pl.program_id(0)
@@ -227,42 +227,46 @@
     @pl.when(i == 0)
     def _():
         cps = _load_patches(u_ref, rows_ref, p, psem)
-        ws = []
-        for a in range(3):
-            for b in range(3):
-                if transposed:
-                    ws.append(pltpu.make_async_copy(w_ref.at[2 - a, 2 - b], wb.at[a, :, b * c:(b + 1) * c], wsem.at[a * 3 + b]))
-                else:
-                    ws.append(pltpu.make_async_copy(w_ref.at[a, b], wb.at[a, b * c:(b + 1) * c, :], wsem.at[a * 3 + b]))
-        for cp in ws:
-            cp.start()
+        wc = pltpu.make_async_copy(w_ref, wb, wsem)
+        wc.start()
         for cp in cps:
             cp.wait()
         _shift_patches(p, cl_ref, cr_ref)
-        for cp in ws:
-            cp.wait()
+        wc.wait()
 
     tw = p.shape[1]
     acc = None
     for a in range(3):
         lhs = p[pl.ds(i * rb + a, rb)].reshape(rb * tw, 3 * c)
-        dims = (((1,), (1,)), ((), ())) if transposed else (((1,), (0,)), ((), ()))
-        d = lax.dot_general(lhs, wb[a], dims, preferred_element_type=F32)
+        d = jnp.dot(lhs, wb[a], preferred_element_type=F32)
         acc = d if acc is None else acc + d
-    epilogue(i, acc, extra, outs)
-
-
-def _conv(transposed, epilogue, u, halo, w, extra, extra_specs, outs, out_specs, rb=2):
+    epilogue(i, acc, (), outs)
+
+
+def _conv(name, epilogue, u, halo, w, outs, out_specs, rb=2):
     th, tw, c = u.shape
     full = pl.BlockSpec((th + 2, 1, c), lambda i: (0, 0, 0), pipeline_mode=pl.Buffered(1))
+    wshape = (3, 3 * c, c)
     return pl.pallas_call(
-        functools.partial(_conv_kernel, transposed, rb, len(extra), epilogue),
-        grid=(th // rb,), out_shape=outs, in_specs=[ANY, ANY, full, full, ANY] + extra_specs, out_specs=out_specs,
-        scratch_shapes=[pltpu.VMEM((th + 2, tw, 3 * c), BF16), pltpu.VMEM((3, c, 3 * c) if transposed else (3, 3 * c, c), BF16),
-                        pltpu.SemaphoreType.DMA((3,)), pltpu.SemaphoreType.DMA((9,))],
+        functools.partial(_conv_kernel, rb, epilogue),
+        grid=(th // rb,), out_shape=outs, in_specs=[ANY, ANY, full, full, ANY], out_specs=out_specs,
+        scratch_shapes=[pltpu.VMEM((th + 2, tw, 3 * c), BF16), pltpu.VMEM(wshape, BF16), pltpu.SemaphoreType.DMA((3,)), pltpu.SemaphoreType.DMA],
         compiler_params=pltpu.CompilerParams(dimension_semantics=("arbitrary",), vmem_limit_bytes=VMEM_LIMIT),
-        cost_estimate=pl.CostEstimate(flops=2 * 9 * th * tw * c * c, bytes_accessed=4 * th * tw * c + 18 * c * c, transcendentals=0),
-    )(u, *halo, w, *extra)
+        name=name,
+    )(u, *halo, w.reshape(wshape))
+
+
+def _add_sums(i, s0, s1, s_ref):
+    row = lax.broadcasted_iota(jnp.int32, s_ref.shape, 0)
+    s = jnp.where(row == 0, s0, jnp.where(row == 1, s1, 0.0))
+
+    @pl.when(i == 0)
+    def _():
+        s_ref[...] = s
+
+    @pl.when(i > 0)
+    def _():
+        s_ref[...] += s
 
 
 def _ep_conv1(i, acc, extra, outs):
@@ -272,16 +276,13 @@
     a = a16.astype(F32)
     s0 = a.sum(0, keepdims=True)
     s1 = (a * a).sum(0, keepdims=True)
-    row = lax.broadcasted_iota(jnp.int32, s_ref.shape, 0)
-    s = jnp.where(row == 0, s0, jnp.where(row == 1, s1, 0.0))
-
-    @pl.when(i == 0)
-    def _():
-        s_ref[...] = s
-
-    @pl.when(i > 0)
-    def _():
-        s_ref[...] += s
+    _add_sums(i, s0, s1, s_ref)
+
+
+def _ep_residual(i, acc, extra, outs):
+    o_ref = outs[0]
+    r = extra[0][...].astype(F32).reshape(acc.shape)
+    o_ref[...] = (acc + r).astype(BF16).reshape(o_ref.shape)
 
 
 def _ep_dz(i, acc, extra, outs):
@@ -293,16 +294,7 @@
     dn_ref[...] = dn.reshape(dn_ref.shape)
     s0 = (dn * xhat).sum(0, keepdims=True)
     s1 = dn.sum(0, keepdims=True)
-    row = lax.broadcasted_iota(jnp.int32, s_ref.shape, 0)
-    s = jnp.where(row == 0, s0, jnp.where(row == 1, s1, 0.0))
-
-    @pl.when(i == 0)
-    def _():
-        s_ref[...] = s
-
-    @pl.when(i > 0)
-    def _():
-        s_ref[...] += s
+    _add_sums(i, s0, s1, s_ref)
 
 
 def _edges(v, first_ref, last_ref):
@@ -327,54 +319,15 @@
     _edges(da.astype(F32), first_ref, last_ref)
 
 
-def _wgrad_kernel(u_ref, rows_ref, cl_ref, cr_ref, v_ref, o_ref, p, vt, psem):
-    a = pl.program_id(0)
-    th, tw, c = v_ref.shape
-
-    @pl.when(a == 0)
-    def _():
-        cps = _load_patches(u_ref, rows_ref, p, psem)
-
-        def tr(r, _):
-            vt[:, pl.ds(pl.multiple_of(r * tw, tw), tw)] = v_ref[r].T
-            return 0
-
-        lax.fori_loop(0, th, tr, 0)
-        for cp in cps:
-            cp.wait()
-        _shift_patches(p, cl_ref, cr_ref)
-
-    n = 3 * c
-    k = 0
-    while k < n:
-        m = min(512, n - k)
-        rhs = p[pl.ds(a, th), :, k:k + m].reshape(th * tw, m)
-        d = jnp.dot(vt[...], rhs, preferred_element_type=F32)
-        o_ref[0, k:k + m, :] = d.T
-        k += m
-
-
-def _wgrad(u, halo, v):
-    th, tw, c = u.shape
-    full = pl.BlockSpec((th + 2, 1, c), lambda i: (0, 0, 0), pipeline_mode=pl.Buffered(1))
-    fv = pl.BlockSpec((th, tw, c), lambda i: (0, 0, 0), pipeline_mode=pl.Buffered(1))
-    return pl.pallas_call(
-        _wgrad_kernel, grid=(3,), out_shape=jax.ShapeDtypeStruct((3, 3 * c, c), F32),
-        in_specs=[ANY, ANY, full, full, fv], out_specs=pl.BlockSpec((1, 3 * c, c), lambda a: (a, 0, 0)),
-        scratch_shapes=[pltpu.VMEM((th + 2, tw, 3 * c), BF16), pltpu.VMEM((c, th * tw), BF16), pltpu.SemaphoreType.DMA((3,))],
-        compiler_params=pltpu.CompilerParams(dimension_semantics=("arbitrary",), vmem_limit_bytes=VMEM_LIMIT),
-        cost_estimate=pl.CostEstimate(flops=2 * 9 * th * tw * c * c, bytes_accessed=4 * th * tw * c + 36 * c * c, transcendentals=0),
-    )(u, *halo, v)
-
-
-TICKS = (2, 3, 4, 6, 8, 9, 11, 13, 15, 17, 18, 20, 21, 22)
-
-
-def _tail_kernel(u_ref, urows, ucl, ucr, v_ref, vrows, vcl, vcr, z_ref, zrows, zcl, zcr, w1_ref, w2_ref, xb_ref, gb_ref,
-                 y_ref, dx_ref, dw_ref, p, vt, wb, dsend, hown, recv0, recv1, recv2, psem, wsem, vsem, send, recv, lsem):
+def _fused_kernel(ticks, nu, ep_u, ep_v, n_xu, n_xv, n_ov, u_ref, urows, ucl, ucr, v_ref, vrows, vcl, vcr, w_ref, *refs):
+    xu, refs = refs[:n_xu], refs[n_xu:]
+    xv, refs = refs[:n_xv], refs[n_xv:]
+    ou, refs = (refs[:1], refs[1:]) if nu else ((), refs)
+    ov, refs = refs[:n_ov], refs[n_ov:]
+    dw_ref, p, vt, wb, dsend, hown, recv0, recv1, recv2, psem, wsem, vsem, send, recv, lsem = refs
     i = pl.program_id(0)
     th, tw, c = u_ref.shape
-    nt = 9
+    nt = w_ref.shape[0]
     half, q, e, sub = c // 2, c // 4, c // 8, c // 16
     wi, xi, ci = lax.axis_index("w"), lax.axis_index("x"), lax.axis_index("c")
     mate, xn, yn = (wi, xi, 1 - ci), (wi, 1 - xi, ci), (1 - wi, xi, ci)
@@ -466,12 +419,14 @@
         when_chunk(j - 2, lambda t: start(s3(t) + keep(t)))
         when_chunk(j - 5, t6)
 
+    wcp = pltpu.make_async_copy(w_ref, wb, wsem)
+
     @pl.when(i == 0)
     def _():
         vc = pltpu.make_async_copy(v_ref, p.at[1:th + 1, :, 0:c], vsem)
         vc.start()
         cps = _load_patches(u_ref, urows, p, psem)
-        pltpu.make_async_copy(w2_ref, wb, wsem.at[0]).start()
+        wcp.start()
         barrier = pltpu.get_barrier_semaphore()
         for d in (mate, xn, yn):
             pl.semaphore_signal(barrier, inc=1, device_id=d, device_id_type=MESH)
@@ -500,26 +455,18 @@
 
     @pl.when(i == nt)
     def _():
-        cps = _load_patches(z_ref, zrows, p, psem)
-        pltpu.make_async_copy(w2_ref, wb, wsem.at[0]).wait()
-        for cp in cps:
-            cp.wait()
-        _shift_patches(p, zcl, zcr)
-
-    @pl.when(i == nt + 8)
+        wcp.wait()
+
+    @pl.when(i == nt + nu)
     def _():
         cps = _load_patches(v_ref, vrows, p, psem)
-        ws = [pltpu.make_async_copy(w1_ref.at[8 - k], wb.at[k], wsem.at[k]) for k in range(9)]
-        start(ws)
         for cp in cps:
             cp.wait()
         _shift_patches(p, vcl, vcr)
-        for cp in ws:
-            cp.wait()
 
     j = jnp.int32(-1)
     now = jnp.int32(0)
-    for s in TICKS:
+    for s in ticks:
         j = j + jnp.where(i >= s, 1, 0)
         now = now + jnp.where(i == s, 1, 0)
 
@@ -536,54 +483,54 @@
         hown[i] = jnp.where(ci == 0, d[:half], d[half:])
         dsend[lax.rem(i, 2)] = jnp.where(ci == 0, d[half:], d[:half])
 
-    def conv(ib, transposed, r_ref, o_ref):
+    def conv(ib, transposed):
         acc = None
         for a in range(3):
             lhs = p[pl.ds(ib * 2 + a, 2)].reshape(2 * tw, 3 * c)
             if transposed:
-                rhs = jnp.concatenate([wb[3 * a], wb[3 * a + 1], wb[3 * a + 2]], axis=1)
+                k = nt - 1 - 3 * a
+                rhs = jnp.concatenate([wb[k], wb[k - 1], wb[k - 2]], axis=1)
                 d = lax.dot_general(lhs, rhs, (((1,), (1,)), ((), ())), preferred_element_type=F32)
             else:
                 d = jnp.dot(lhs, wb[3 * a:3 * a + 3].reshape(3 * c, c), preferred_element_type=F32)
             acc = d if acc is None else acc + d
-        r = r_ref[...].astype(F32).reshape(acc.shape)
-        o_ref[...] = (acc + r).astype(BF16).reshape(o_ref.shape)
-
-    @pl.when(jnp.logical_and(i >= nt, i < nt + 8))
-    def _():
-        conv(i - nt, False, xb_ref, y_ref)
-
-    @pl.when(i >= nt + 8)
-    def _():
-        conv(i - nt - 8, True, gb_ref, dx_ref)
-
-
-def _tail(x, xh, da, dah, z, zh, w1, w2, g):
-    th, tw, c = x.shape
+        return acc
+
+    if nu:
+        @pl.when(jnp.logical_and(i >= nt, i < nt + nu))
+        def _():
+            ep_u(i - nt, conv(i - nt, False), xu, ou)
+
+    @pl.when(jnp.logical_and(i >= nt + nu, i < nt + nu + th // 2))
+    def _():
+        ib = i - nt - nu
+        ep_v(ib, conv(ib, True), xv, ov)
+
+
+def _fused(name, cid, steps, ticks, u, uh, v, vh, w, nu, ep_u, xu, ep_v, xv, outs_v):
+    th, tw, c = u.shape
     nt, half = 9, c // 2
+    last = th // 2 - 1
     full = pl.BlockSpec((th + 2, 1, c), lambda i: (0, 0, 0), pipeline_mode=pl.Buffered(1))
-    yb = pl.BlockSpec((2, tw, c), lambda i: (jnp.minimum(jnp.maximum(i - nt, 0), 7), 0, 0))
-    xb = pl.BlockSpec((2, tw, c), lambda i: (jnp.maximum(i - nt - 8, 0), 0, 0))
+    small = pl.BlockSpec((8, c), lambda i: (0, 0))
+    ub = pl.BlockSpec((2, tw, c), lambda i: (jnp.minimum(jnp.maximum(i - nt, 0), nu - 1), 0, 0))
+    vb = pl.BlockSpec((2, tw, c), lambda i: (jnp.minimum(jnp.maximum(i - nt - nu, 0), last), 0, 0))
     img = [ANY, ANY, full, full]
     dma = pltpu.SemaphoreType.DMA
-    return pl.pallas_call(
-        _tail_kernel, grid=(nt + 16,),
-        out_shape=[jax.ShapeDtypeStruct((th, tw, c), BF16), jax.ShapeDtypeStruct((th, tw, c), BF16), jax.ShapeDtypeStruct((nt * c, c), F32)],
-        in_specs=img * 3 + [ANY, ANY, yb, xb], out_specs=[yb, xb, ANY],
-        scratch_shapes=[pltpu.VMEM((th + 2, tw, 3 * c), BF16), pltpu.VMEM((c, th * tw), BF16), pltpu.VMEM((9, c, c), BF16),
+    out_u = [jax.ShapeDtypeStruct((2 * nu, tw, c), BF16)] if nu else []
+    call = pl.pallas_call(
+        functools.partial(_fused_kernel, ticks, nu, ep_u, ep_v, len(xu), len(xv), len(outs_v)), grid=(steps,),
+        out_shape=out_u + [o for o, _ in outs_v] + [jax.ShapeDtypeStruct((nt * c, c), F32)],
+        in_specs=img + img + [ANY] + [ub for _ in xu] + [vb if b else small for _, b in xv],
+        out_specs=[ub for _ in out_u] + [vb if b else small for _, b in outs_v] + [ANY],
+        scratch_shapes=[pltpu.VMEM((th + 2, tw, 3 * c), BF16), pltpu.VMEM((c, th * tw), BF16), pltpu.VMEM((nt, c, c), BF16),
                         pltpu.VMEM((2, half, c), F32), pltpu.VMEM((nt, half, c), F32), pltpu.VMEM((2, half, c), F32),
                         pltpu.VMEM((nt, 2, c // 8, c), F32), pltpu.VMEM((nt, 2, c // 16, c), F32),
-                        dma((3,)), dma((9,)), dma, dma((10, nt)), dma((10, nt)), dma((2, nt))],
-        compiler_params=pltpu.CompilerParams(dimension_semantics=("arbitrary",), vmem_limit_bytes=VMEM_LIMIT, collective_id=5, has_side_effects=True),
-        cost_estimate=pl.CostEstimate(flops=3 * 2 * 9 * th * tw * c * c, bytes_accessed=16 * th * tw * c, transcendentals=0),
-        name="tail",
-    )(x, *xh, da, *dah, z, *zh, w1.reshape(9, c, c), w2.reshape(9, c, c), x, g)
-
-
-def _reduce_all(d):
-    r, k, c = d.shape
-    s = lax.psum_scatter(d.reshape(r * k, c), ("c", "w", "x"), scatter_dimension=0, tiled=True)
-    return lax.all_gather(s, ("c", "w", "x"), axis=0, tiled=True).reshape(3, 3, c, c)
+                        dma((3,)), dma, dma, dma((10, nt)), dma((10, nt)), dma((2, nt))],
+        compiler_params=pltpu.CompilerParams(dimension_semantics=("arbitrary",), vmem_limit_bytes=VMEM_LIMIT, collective_id=cid, has_side_effects=True),
+        name=name,
+    )
+    return call(u, *uh, v, *vh, w.reshape(nt, c, c), *[x for x, _ in xu], *[x for x, _ in xv])
 
 
 def solution(mesh):
@@ -610,18 +557,17 @@
             return u, u[:, 0:1, :].astype(F32), u[:, tw - 1:, :].astype(F32)
 
         xh, gh = _halo(nh, nw, 0, *with_edges(x), *with_edges(g))
-        a, s = _conv(False, _ep_conv1, x, xh, w1, [], [], [img16, sums], [blk, small])
+        a, s = _conv("conv1", _ep_conv1, x, xh, w1, [img16, sums], [blk, small])
         st = _allsum(nh, nw, cnt, 0, 1, s, par)
         z, z0, z1 = pl.pallas_call(_z_kernel, grid=(th // rb,), out_shape=[img16, edge, edge], in_specs=[blk, small], out_specs=[blk, eblk, eblk], name="act")(a, st)
         (zh,) = _halo(nh, nw, 2, z, z0, z1)
-        d2 = _wgrad(z, zh, g)
-        g_late, d2 = lax.optimization_barrier((g, d2))
-        dw2 = _reduce_all(d2)
-        dn, t = _conv(True, _ep_dz, g_late, gh, w2, [a, st], [blk, small], [img32, sums], [blk, small])
+        y, dn, t, dw2 = _fused("mid", 5, 25, (2, 3, 4, 6, 8, 9, 11, 13, 15, 17, 18, 20, 21, 22), z, zh, g, gh, w2, 8, _ep_residual, [(x, True)],
+                               _ep_dz, [(a, True), (st, False)], [(img32, True), (sums, False)])
         t = _allsum(nh, nw, cnt, 1, 3, t, st)
         da, da0, da1 = pl.pallas_call(_da_kernel, grid=(th // rb,), out_shape=[img16, edge, edge], in_specs=[blk, blk, small, small], out_specs=[blk, eblk, eblk], name="da")(dn, a, st, t)
         (dah,) = _halo(nh, nw, 4, da, da0, da1)
-        y, dx, dw1 = _tail(x, xh, da, dah, z, zh, w1, w2, g)
-        return y[None], dx[None], dw1.reshape(3, 3, c, c), dw2, t[0], t[1]
+        dx, dw1 = _fused("tail", 6, 21, (2, 3, 4, 5, 7, 9, 11, 13, 15, 16, 17, 18, 19, 20), x, xh, da, dah, w1, 0, None, [],
+                         _ep_residual, [(g, True)], [(img16, True)])
+        return y[None], dx[None], dw1.reshape(w1.shape), dw2.reshape(w2.shape), t[0], t[1]
 
     return jax.shard_map(body, mesh=mesh3, in_specs=(tile, P(), P(), P(), P(), tile), out_specs=(tile, tile, P(), P(), P(), P()), check_vma=False)

time: 543 us -> 483 us (0.89)
  waiting for transfers between devices: 101 us -> 0 us
  Pallas kernels: 391 us -> 445 us
  between operations: 14.1 us -> 0.72 us
    reduce_scatter x1 -> x0, waiting for transfers between devices: 101 us -> none  [_reduce_all(): lax.psum_scatter(d.reshape(r * k, c), ('c', 'w', 'x'), scatter_dimension=...]
    pallas_call x4 -> x3, Pallas kernels: 327 us -> 384 us  [the longest x2 337 us: _fused(): call(u, *uh, v, *vh, w.reshape(nt, c, c), *[x for x, _ in xu], *[x for x,...]
  transfers between devices with their start and end apart: 2 -> 0, of which waited for: 1 -> 0; matrix products, arithmetic and copies ran while one was open for 0% -> 0% of each run, Pallas kernels for 48% -> 0%
where the time goes in v3:
time: 483 us; the launch traced here: 482 us
  Pallas kernels  445 us (92%)
  local copies, waits for them, and re-layouts  34.2 us (7%)
    pallas_call x2, Pallas kernels, _fused(): call(u, *uh, v, *vh, w.reshape(nt, c, c), *[x for x, _ in xu], *[x for x,...  337 us
    pallas_call x1, Pallas kernels, _conv(): pl.pallas_call(functools.partial(_conv_kernel, rb, epilogue), grid=(th //...  47 us
    unnamed x6, local copies, waits for them, and re-layouts  31.3 us
    pallas_call x2, Pallas kernels, _allsum(): pl.pallas_call(functools.partial(_allsum_kernel, nh, nw, cnt, mode), out_...  22 us
    pallas_call x3, Pallas kernels, _halo(): pl.pallas_call(functools.partial(_halo_kernel, nh, nw, n), out_shape=out,...  18.6 us
    pallas_call x1, Pallas kernels, body(): pl.pallas_call(_da_kernel, grid=(th // rb,), out_shape=[img16, edge, edge...  10.6 us

profile of v3, /device:TPU:0, one launch (start us, length us, event | category | flops | bytes accessed | tf_op | source)
XLA Modules:
  0.0 482.4 jit_solution(994555464908405981)
XLA Ops:
  0.6 0.1 pad.3.clone
  0.7 0.7 broadcast_in_dim.19
  1.4 0.7 broadcast_in_dim.20
  2.1 0.7 maximum_maximum_fusion.par_ref
  2.8 1.9 slice_convert_fusion
  4.7 7.9 %halo0.1 = (bf16[2,256,640]{2,1,0:T(8,128)(2,1)}, f32[18,1,640]{2,1,0:T(1,128)}, f32[18,1,640]{2,1,0:T(1,128)}, bf16[2,256,640]{2,1,0:T(8,128)(2,1)}, f32[18,1,640]{2,1,0:T(1,128)}, /*index=5*/f32[18,1,640]{2,1,0:T(1,128)}) custom-call(bf16[16,256,640]{2,1,0:T(8,128)(2,1)} %bitcast.10, f32[16,1,640]{2,1,0:T(1,128)} %get-tuple-element.64.refs_1_, ...), custom_call_target="tpu_custom_call" | custom-call | tf_op jit(solution)/shard_map/halo0/pallas_call | solution.py:123
  12.5 47.0 %conv1.1 = (bf16[16,256,640]{2,1,0:T(8,128)(2,1)}, f32[8,640]{1,0:T(8,128)}) custom-call(bf16[16,256,640]{2,1,0:T(8,128)(2,1)} %bitcast.11, bf16[2,256,640]{2,1,0:T(8,128)(2,1)} %get-tuple-element.32.rows_ref.urows, f32[18,1,640]{2,1,0:T(1,128)} %get-tuple-element.33.cl_ref.ucl, f32[18,1,640]{2,1,0:T(1,128)} %get-tuple-element.34.cr_ref.ucr, ...), custom_call_target="tpu_custom_call" | custom-call | tf_op jit(solution)/shard_map/conv1/pallas_call | solution.py:250
  59.6 14.5 %allsum1.1.st_ref.refs_2_.par_ref = f32[8,640]{1,0:T(8,128)} custom-call(f32[8,640]{1,0:T(8,128)} %get-tuple-element.36.part_ref, f32[8,640]{1,0:T(8,128)} %maximum_maximum_fusion.par_ref), custom_call_target="tpu_custom_call" | custom-call | tf_op jit(solution)/shard_map/allsum1/pallas_call | solution.py:183
  74.1 9.3 %act.1 = (bf16[16,256,640]{2,1,0:T(8,128)(2,1)}, f32[16,1,640]{2,1,0:T(1,128)}, f32[16,1,640]{2,1,0:T(1,128)}) custom-call(bf16[16,256,640]{2,1,0:T(8,128)(2,1)} %get-tuple-element.35.a_ref.refs_1_, f32[8,640]{1,0:T(8,128)} %allsum1.1.st_ref.refs_2_.par_ref), custom_call_target="tpu_custom_call" | custom-call | tf_op jit(solution)/shard_map/act/pallas_call | solution.py:562
  83.4 5.3 %halo2.1 = (bf16[2,256,640]{2,1,0:T(8,128)(2,1)}, f32[18,1,640]{2,1,0:T(1,128)}, f32[18,1,640]{2,1,0:T(1,128)}) custom-call(bf16[16,256,640]{2,1,0:T(8,128)(2,1)} %get-tuple-element.37.refs_0_.u_ref, f32[16,1,640]{2,1,0:T(1,128)} %get-tuple-element.38.refs_1_, f32[16,1,640]{2,1,0:T(1,128)} %get-tuple-element.39.refs_2_), custom_call_target="tpu_custom_call" | custom-call | tf_op jit(solution)/shard_map/halo2/pallas_call | solution.py:123
  88.7 182.8 %mid.1 = (bf16[16,256,640]{2,1,0:T(8,128)(2,1)}, f32[16,256,640]{2,1,0:T(8,128)}, f32[8,640]{1,0:T(8,128)}, f32[5760,640]{1,0:T(8,128)}) custom-call(bf16[16,256,640]{2,1,0:T(8,128)(2,1)} %get-tuple-element.37.refs_0_.u_ref, bf16[2,256,640]{2,1,0:T(8,128)(2,1)} %get-tuple-element.40.urows, f32[18,1,640]{2,1,0:T(1,128)} %get-tuple-element.41.ucl, ...), custom_call_target="tpu_custom_call" | custom-call | tf_op jit(solution)/shard_map/mid/pallas_call | solution.py:533
  271.5 7.5 %allsum3.1.t_ref = f32[8,640]{1,0:T(8,128)} custom-call(f32[8,640]{1,0:T(8,128)} %get-tuple-element.48.part_ref, f32[8,640]{1,0:T(8,128)} %allsum1.1.st_ref.refs_2_.par_ref), custom_call_target="tpu_custom_call" | custom-call | tf_op jit(solution)/shard_map/allsum3/pallas_call | solution.py:183
  279.0 10.6 %da.1 = (bf16[16,256,640]{2,1,0:T(8,128)(2,1)}, f32[16,1,640]{2,1,0:T(1,128)}, f32[16,1,640]{2,1,0:T(1,128)}) custom-call(f32[16,256,640]{2,1,0:T(8,128)} %get-tuple-element.47.dn_ref, bf16[16,256,640]{2,1,0:T(8,128)(2,1)} %get-tuple-element.35.a_ref.refs_1_, f32[8,640]{1,0:T(8,128)} %allsum1.1.st_ref.refs_2_.par_ref, f32[8,640]{1,0:T(8,128)} %allsum3.1.t_ref), custom_call_target="tpu_custom_call" | custom-call | tf_op jit(solution)/shard_map/da/pallas_call | solution.py:567
  289.6 1.4 slice_reduce_fusion
  291.0 5.5 %halo4.1 = (bf16[2,256,640]{2,1,0:T(8,128)(2,1)}, f32[18,1,640]{2,1,0:T(1,128)}, f32[18,1,640]{2,1,0:T(1,128)}) custom-call(bf16[16,256,640]{2,1,0:T(8,128)(2,1)} %get-tuple-element.49.refs_0_.v_ref, f32[16,1,640]{2,1,0:T(1,128)} %get-tuple-element.50.refs_1_, f32[16,1,640]{2,1,0:T(1,128)} %get-tuple-element.51.refs_2_), custom_call_target="tpu_custom_call" | custom-call | tf_op jit(solution)/shard_map/halo4/pallas_call | solution.py:123
  296.4 154.6 %tail.1 = (bf16[16,256,640]{2,1,0:T(8,128)(2,1)}, f32[5760,640]{1,0:T(8,128)}) custom-call(bf16[16,256,640]{2,1,0:T(8,128)(2,1)} %bitcast.13, bf16[2,256,640]{2,1,0:T(8,128)(2,1)} %get-tuple-element.32.rows_ref.urows, f32[18,1,640]{2,1,0:T(1,128)} %get-tuple-element.33.cl_ref.ucl, f32[18,1,640]{2,1,0:T(1,128)} %get-tuple-element.34.cr_ref.ucr, ...), custom_call_target="tpu_custom_call" | custom-call | tf_op jit(solution)/shard_map/tail/pallas_call | solution.py:533
  451.1 0.0 copy-start
  451.1 5.7 %copy.16 = bf16[1,16,256,640]{3,2,1,0:T(8,128)(2,1)} copy(bf16[1,16,256,640]{3,2,1,0:T(8,128)(2,1)} %bitcast.23) | data formatting | bytes 10485760
  456.8 0.0 copy-done
  456.8 2.4 copy.17
  459.1 11.6 %copy.18 = f32[3,3,640,640]{3,2,1,0:T(8,128)} copy(f32[3,3,640,640]{3,2,1,0:T(8,128)} %bitcast.21) | data formatting | bytes 29491200
  470.8 11.6 %copy.19 = f32[3,3,640,640]{3,2,1,0:T(8,128)} copy(f32[3,3,640,640]{3,2,1,0:T(8,128)} %bitcast.20) | data formatting | bytes 29491200
  (3 shorter events, 0.0 us)
Async XLA Ops:
  451.1 5.7 %copy-start = (bf16[16,256,640]{2,1,0:T(8,128)(2,1)S(1)}, bf16[16,256,640]{2,1,0:T(8,128)(2,1)}, u32[]{:S(2)}) copy-start(bf16[16,256,640]{2,1,0:T(8,128)(2,1)} %get-tuple-element.55) | copy-start | bytes 15728644

commit v4 on v3

--- a/solution.py
+++ b/solution.py
@@ -200,7 +200,7 @@
     return cps
 
 
-def _shift_patches(p, cl_ref, cr_ref):
+def _shift_patches(p, cl_ref, cr_ref, r0=0):
     n, tw, c3 = p.shape
     c = c3 // 3
     ck = 128
@@ -209,8 +209,8 @@
         idx = lax.broadcasted_iota(jnp.int32, (tw, ck), 0)
         for k in range(c // ck):
             f = p[r, :, c + k * ck:c + (k + 1) * ck].astype(F32)
-            lo = cl_ref[r, :, k * ck:(k + 1) * ck]
-            hi = cr_ref[r, :, k * ck:(k + 1) * ck]
+            lo = cl_ref[r0 + r, :, k * ck:(k + 1) * ck]
+            hi = cr_ref[r0 + r, :, k * ck:(k + 1) * ck]
             p[r, :, k * ck:(k + 1) * ck] = jnp.where(idx == 0, lo, pltpu.roll(f, 1, 0)).astype(BF16)
             p[r, :, 2 * c + k * ck:2 * c + (k + 1) * ck] = jnp.where(idx == tw - 1, hi, pltpu.roll(f, tw - 1, 0)).astype(BF16)
         return 0
@@ -288,33 +288,38 @@
 def _ep_dz(i, acc, extra, outs):
     a_ref, st_ref = extra
     dn_ref, s_ref = outs
-    st = st_ref[...]
-    xhat = (a_ref[...].astype(F32).reshape(acc.shape) - st[0:1]) * st[1:2]
-    dn = acc * _gelu_grad(xhat * st[2:3] + st[3:4])
+    mean, rstd, gamma, beta = _params(st_ref)
+    xhat = (a_ref[...].astype(F32).reshape(acc.shape) - mean) * rstd
+    dn = acc * _gelu_grad(xhat * gamma + beta)
     dn_ref[...] = dn.reshape(dn_ref.shape)
     s0 = (dn * xhat).sum(0, keepdims=True)
     s1 = dn.sum(0, keepdims=True)
     _add_sums(i, s0, s1, s_ref)
 
 
+def _params(st_ref):
+    st = st_ref[...]
+    return [st[k:k + 1] for k in range(4)]
+
+
 def _edges(v, first_ref, last_ref):
     first_ref[...] = v[:, 0:1, :]
     last_ref[...] = v[:, v.shape[1] - 1:, :]
 
 
 def _z_kernel(a_ref, st_ref, z_ref, first_ref, last_ref):
-    st = st_ref[...]
-    xhat = (a_ref[...].astype(F32) - st[0:1]) * st[1:2]
-    z = _gelu(xhat * st[2:3] + st[3:4]).astype(BF16)
+    mean, rstd, gamma, beta = _params(st_ref)
+    xhat = (a_ref[...].astype(F32) - mean) * rstd
+    z = _gelu(xhat * gamma + beta).astype(BF16)
     z_ref[...] = z
     _edges(z.astype(F32), first_ref, last_ref)
 
 
 def _da_kernel(dn_ref, a_ref, st_ref, t_ref, o_ref, first_ref, last_ref):
-    st = st_ref[...]
-    t = t_ref[...]
-    xhat = (a_ref[...].astype(F32) - st[0:1]) * st[1:2]
-    da = (st[1:2] * (dn_ref[...] * st[2:3] - t[3:4] - xhat * t[2:3])).astype(BF16)
+    mean, rstd, gamma, _ = _params(st_ref)
+    _, _, u0, u1 = _params(t_ref)
+    xhat = (a_ref[...].astype(F32) - mean) * rstd
+    da = (rstd * (dn_ref[...] * gamma - u1 - xhat * u0)).astype(BF16)
     o_ref[...] = da
     _edges(da.astype(F32), first_ref, last_ref)
 
@@ -410,14 +415,15 @@
             for cp in s1(t) + s2(t) + s3(t) + s4(t) + s5(t):
                 cp.wait_send()
 
+        lag = 2
         when_chunk(j, lambda t: start(s1(t)))
-        when_chunk(j - 1, t2)
-        when_chunk(j - 2, t3)
-        when_chunk(j - 3, t4)
-        when_chunk(j - 4, t5)
-        when_chunk(j - 1, lambda t: start(s2(t)))
-        when_chunk(j - 2, lambda t: start(s3(t) + keep(t)))
-        when_chunk(j - 5, t6)
+        when_chunk(j - lag, t2)
+        when_chunk(j - 2 * lag, t3)
+        when_chunk(j - 3 * lag, t4)
+        when_chunk(j - 4 * lag, t5)
+        when_chunk(j - lag, lambda t: start(s2(t)))
+        when_chunk(j - 2 * lag, lambda t: start(s3(t) + keep(t)))
+        when_chunk(j - 5 * lag, t6)
 
     wcp = pltpu.make_async_copy(w_ref, wb, wsem)
 
@@ -533,6 +539,103 @@
     return call(u, *uh, v, *vh, w.reshape(nt, c, c), *[x for x, _ in xu], *[x for x, _ in xv])
 
 
+def _finish_kernel(u_ref, rows_ref, cl_ref, cr_ref, w_ref, x_ref, y0_ref, dx0_ref, d1_ref, d2_ref,
+                   y_ref, dx_ref, dw1_ref, dw2_ref, p, wb, yb, by, bx, b1, b2, psem, wsem, ysem, insem, outsem):
+    i = pl.program_id(0)
+    steps = pl.num_programs(0)
+    th, tw, c = u_ref.shape
+    r0 = th - steps
+    slot = lax.rem(i, 2)
+    moves = [(y0_ref, by, y_ref), (dx0_ref, bx, dx_ref), (d1_ref, b1, dw1_ref), (d2_ref, b2, dw2_ref)]
+
+    def ins(k):
+        out = []
+        for m, (src, buf, _) in enumerate(moves):
+            n = buf.shape[1]
+            out.append(pltpu.make_async_copy(src.at[pl.ds(k * n, n)], buf.at[lax.rem(k, 2)], insem.at[m, lax.rem(k, 2)]))
+        return out
+
+    def outs(k):
+        out = []
+        for m, (_, buf, dst) in enumerate(moves):
+            n = buf.shape[1]
+            out.append(pltpu.make_async_copy(buf.at[lax.rem(k, 2)], dst.at[pl.ds(k * n, n)], outsem.at[m, lax.rem(k, 2)]))
+        return out
+
+    def yout(k):
+        return pltpu.make_async_copy(yb.at[lax.rem(k, 2)], y_ref.at[r0 + k], ysem.at[lax.rem(k, 2)])
+
+    def each(cps, f):
+        for cp in cps:
+            f(cp)
+
+    start, wait = (lambda cp: cp.start()), (lambda cp: cp.wait())
+
+    @pl.when(i == 0)
+    def _():
+        n = th - r0 + 1
+        cps = [pltpu.make_async_copy(u_ref.at[r0 - 1:], p.at[:n, :, c:2 * c], psem.at[0]),
+               pltpu.make_async_copy(rows_ref.at[1], p.at[n, :, c:2 * c], psem.at[1])]
+        wc = pltpu.make_async_copy(w_ref, wb, wsem)
+        each(cps + [wc], start)
+        each(ins(i), start)
+        each(cps, wait)
+        _shift_patches(p, cl_ref, cr_ref, r0)
+        wc.wait()
+
+    each(ins(i), wait)
+    each(outs(i), start)
+
+    @pl.when(i > 0)
+    def _():
+        each(outs(i - 1), wait)
+
+    @pl.when(i + 1 < steps)
+    def _():
+        each(ins(i + 1), start)
+
+    acc = None
+    for a in range(3):
+        d = jnp.dot(p[i + a], wb[a], preferred_element_type=F32)
+        acc = d if acc is None else acc + d
+
+    @pl.when(i > 1)
+    def _():
+        yout(i - 2).wait()
+
+    yb[slot] = (acc + x_ref[0].astype(F32)).astype(BF16)
+    yout(i).start()
+
+    @pl.when(i == steps - 1)
+    def _():
+        yout(i - 1).wait()
+        yout(i).wait()
+        each(outs(i), wait)
+
+
+def _finish(u, halo, w, x, y0, dx0, d1, d2):
+    th, tw, c = u.shape
+    r0 = y0.shape[0]
+    steps = th - r0
+    full = pl.BlockSpec((th + 2, 1, c), lambda i: (0, 0, 0), pipeline_mode=pl.Buffered(1))
+    wshape = (3, 3 * c, c)
+    dma = pltpu.SemaphoreType.DMA
+    raw = (y0, dx0, d1, d2)
+
+    def buf(v):
+        return pltpu.VMEM((2, v.shape[0] // steps) + v.shape[1:], v.dtype)
+
+    return pl.pallas_call(
+        _finish_kernel, grid=(steps,),
+        out_shape=[jax.ShapeDtypeStruct((th, tw, c), BF16)] + [jax.ShapeDtypeStruct(v.shape, v.dtype) for v in raw[1:]],
+        in_specs=[ANY, ANY, full, full, ANY, pl.BlockSpec((1, tw, c), lambda i: (r0 + i, 0, 0))] + [ANY] * 4, out_specs=[ANY] * 4,
+        scratch_shapes=[pltpu.VMEM((steps + 2, tw, 3 * c), BF16), pltpu.VMEM(wshape, BF16), pltpu.VMEM((2, tw, c), BF16)] + [buf(v) for v in raw]
+        + [dma((2,)), dma, dma((2,)), dma((4, 2)), dma((4, 2))],
+        compiler_params=pltpu.CompilerParams(dimension_semantics=("arbitrary",), vmem_limit_bytes=VMEM_LIMIT),
+        name="finish",
+    )(u, *halo, w.reshape(wshape), x, *raw)
+
+
 def solution(mesh):
     nh, nw = mesh.shape["h"], mesh.shape["w"]
     mesh3 = Mesh(mesh.devices.reshape(nw, nh // 2, 2), ("w", "x", "c"))
@@ -561,13 +664,14 @@
         st = _allsum(nh, nw, cnt, 0, 1, s, par)
         z, z0, z1 = pl.pallas_call(_z_kernel, grid=(th // rb,), out_shape=[img16, edge, edge], in_specs=[blk, small], out_specs=[blk, eblk, eblk], name="act")(a, st)
         (zh,) = _halo(nh, nw, 2, z, z0, z1)
-        y, dn, t, dw2 = _fused("mid", 5, 25, (2, 3, 4, 6, 8, 9, 11, 13, 15, 17, 18, 20, 21, 22), z, zh, g, gh, w2, 8, _ep_residual, [(x, True)],
+        y, dn, t, dw2 = _fused("mid", 5, 24, (*range(2, 9), *range(10, 15, 2), *range(15, 24)), z, zh, g, gh, w2, 4, _ep_residual, [(x, True)],
                                _ep_dz, [(a, True), (st, False)], [(img32, True), (sums, False)])
         t = _allsum(nh, nw, cnt, 1, 3, t, st)
         da, da0, da1 = pl.pallas_call(_da_kernel, grid=(th // rb,), out_shape=[img16, edge, edge], in_specs=[blk, blk, small, small], out_specs=[blk, eblk, eblk], name="da")(dn, a, st, t)
         (dah,) = _halo(nh, nw, 4, da, da0, da1)
-        dx, dw1 = _fused("tail", 6, 21, (2, 3, 4, 5, 7, 9, 11, 13, 15, 16, 17, 18, 19, 20), x, xh, da, dah, w1, 0, None, [],
+        dx, dw1 = _fused("tail", 6, 25, (*range(2, 9), *range(10, 15, 2), *range(16, 25)), x, xh, da, dah, w1, 0, None, [],
                          _ep_residual, [(g, True)], [(img16, True)])
+        y, dx, dw1, dw2 = _finish(z, zh, w2, x, y, dx, dw1, dw2)
         return y[None], dx[None], dw1.reshape(w1.shape), dw2.reshape(w2.shape), t[0], t[1]
 
     return jax.shard_map(body, mesh=mesh3, in_specs=(tile, P(), P(), P(), P(), tile), out_specs=(tile, tile, P(), P(), P(), P()), check_vma=False)

time: 483 us -> 459 us (0.950)
  local copies, waits for them, and re-layouts: 34.2 us -> 2.88 us
  Pallas kernels: 445 us -> 451 us
    pallas_call x0 -> x1, Pallas kernels: none -> 44.8 us  [_finish(): pl.pallas_call(_finish_kernel, grid=(steps,), out_shape=[jax.ShapeDtypeSt...]
    pallas_call x2, Pallas kernels: 337 us -> 299 us  [_fused(): call(u, *uh, v, *vh, w.reshape(nt, c, c), *[x for x, _ in xu], *[x for x,...]
    unnamed x6 -> x0, local copies, waits for them, and re-layouts: 31.3 us -> none
where the time goes in v4:
time: 459 us; the launch traced here: 458 us
  Pallas kernels  451 us (98%)
    pallas_call x2, Pallas kernels, _fused(): call(u, *uh, v, *vh, w.reshape(nt, c, c), *[x for x, _ in xu], *[x for x,...  299 us
    pallas_call x1, Pallas kernels, _conv(): pl.pallas_call(functools.partial(_conv_kernel, rb, epilogue), grid=(th //...  47 us
    pallas_call x1, Pallas kernels, _finish(): pl.pallas_call(_finish_kernel, grid=(steps,), out_shape=[jax.ShapeDtypeSt...  44.8 us
    pallas_call x2, Pallas kernels, _allsum(): pl.pallas_call(functools.partial(_allsum_kernel, nh, nw, cnt, mode), out_...  22.5 us
    pallas_call x3, Pallas kernels, _halo(): pl.pallas_call(functools.partial(_halo_kernel, nh, nw, n), out_shape=out,...  18.2 us
    pallas_call x1, Pallas kernels, body(): pl.pallas_call(_da_kernel, grid=(th // rb,), out_shape=[img16, edge, edge...  10.6 us
    pallas_call x1, Pallas kernels, body(): pl.pallas_call(_z_kernel, grid=(th // rb,), out_shape=[img16, edge, edge]...  9.34 us

profile of v4, /device:TPU:0, one launch (start us, length us, event | category | flops | bytes accessed | tf_op | source)
XLA Modules:
  0.0 457.6 jit_solution(15025027262560135096)
XLA Ops:
  0.6 0.1 pad.3.clone
  0.7 0.7 broadcast_in_dim.19
  1.4 0.7 broadcast_in_dim.20
  2.1 0.7 maximum_maximum_fusion.par_ref
  2.8 1.9 slice_convert_fusion
  4.7 7.9 %halo0.1 = (bf16[2,256,640]{2,1,0:T(8,128)(2,1)}, f32[18,1,640]{2,1,0:T(1,128)}, f32[18,1,640]{2,1,0:T(1,128)}, bf16[2,256,640]{2,1,0:T(8,128)(2,1)}, f32[18,1,640]{2,1,0:T(1,128)}, /*index=5*/f32[18,1,640]{2,1,0:T(1,128)}) custom-call(bf16[16,256,640]{2,1,0:T(8,128)(2,1)} %bitcast.11, f32[16,1,640]{2,1,0:T(1,128)} %get-tuple-element.72.refs_1_, ...), custom_call_target="tpu_custom_call" | custom-call | tf_op jit(solution)/shard_map/halo0/pallas_call | solution.py:123
  12.6 47.0 %conv1.1 = (bf16[16,256,640]{2,1,0:T(8,128)(2,1)}, f32[8,640]{1,0:T(8,128)}) custom-call(bf16[16,256,640]{2,1,0:T(8,128)(2,1)} %bitcast.12, bf16[2,256,640]{2,1,0:T(8,128)(2,1)} %get-tuple-element.36.rows_ref.urows, f32[18,1,640]{2,1,0:T(1,128)} %get-tuple-element.37.cl_ref.ucl, f32[18,1,640]{2,1,0:T(1,128)} %get-tuple-element.38.cr_ref.ucr, ...), custom_call_target="tpu_custom_call" | custom-call | tf_op jit(solution)/shard_map/conv1/pallas_call | solution.py:250
  59.6 14.5 %allsum1.1.st_ref.refs_2_.par_ref = f32[8,640]{1,0:T(8,128)} custom-call(f32[8,640]{1,0:T(8,128)} %get-tuple-element.40.part_ref, f32[8,640]{1,0:T(8,128)} %maximum_maximum_fusion.par_ref), custom_call_target="tpu_custom_call" | custom-call | tf_op jit(solution)/shard_map/allsum1/pallas_call | solution.py:183
  74.2 9.3 %act.1 = (bf16[16,256,640]{2,1,0:T(8,128)(2,1)}, f32[16,1,640]{2,1,0:T(1,128)}, f32[16,1,640]{2,1,0:T(1,128)}) custom-call(bf16[16,256,640]{2,1,0:T(8,128)(2,1)} %get-tuple-element.39.a_ref.refs_1_, f32[8,640]{1,0:T(8,128)} %allsum1.1.st_ref.refs_2_.par_ref), custom_call_target="tpu_custom_call" | custom-call | tf_op jit(solution)/shard_map/act/pallas_call | solution.py:665
  83.5 5.2 %halo2.1 = (bf16[2,256,640]{2,1,0:T(8,128)(2,1)}, f32[18,1,640]{2,1,0:T(1,128)}, f32[18,1,640]{2,1,0:T(1,128)}) custom-call(bf16[16,256,640]{2,1,0:T(8,128)(2,1)} %get-tuple-element.41.refs_0_.u_ref, f32[16,1,640]{2,1,0:T(1,128)} %get-tuple-element.42.refs_1_, f32[16,1,640]{2,1,0:T(1,128)} %get-tuple-element.43.refs_2_), custom_call_target="tpu_custom_call" | custom-call | tf_op jit(solution)/shard_map/halo2/pallas_call | solution.py:123
  88.7 152.9 %mid.1 = (bf16[8,256,640]{2,1,0:T(8,128)(2,1)}, f32[16,256,640]{2,1,0:T(8,128)}, f32[8,640]{1,0:T(8,128)}, f32[5760,640]{1,0:T(8,128)}) custom-call(bf16[16,256,640]{2,1,0:T(8,128)(2,1)} %get-tuple-element.41.refs_0_.u_ref, bf16[2,256,640]{2,1,0:T(8,128)(2,1)} %get-tuple-element.44.urows.rows_ref, f32[18,1,640]{2,1,0:T(1,128)} %get-tuple-element.45.ucl.cl_ref, ...), custom_call_target="tpu_custom_call" | custom-call | tf_op jit(solution)/shard_map/mid/pallas_call | solution.py:539
  241.6 8.0 %allsum3.1.t_ref = f32[8,640]{1,0:T(8,128)} custom-call(f32[8,640]{1,0:T(8,128)} %get-tuple-element.52.part_ref, f32[8,640]{1,0:T(8,128)} %allsum1.1.st_ref.refs_2_.par_ref), custom_call_target="tpu_custom_call" | custom-call | tf_op jit(solution)/shard_map/allsum3/pallas_call | solution.py:183
  249.6 10.6 %da.1 = (bf16[16,256,640]{2,1,0:T(8,128)(2,1)}, f32[16,1,640]{2,1,0:T(1,128)}, f32[16,1,640]{2,1,0:T(1,128)}) custom-call(f32[16,256,640]{2,1,0:T(8,128)} %get-tuple-element.51.dn_ref, bf16[16,256,640]{2,1,0:T(8,128)(2,1)} %get-tuple-element.39.a_ref.refs_1_, f32[8,640]{1,0:T(8,128)} %allsum1.1.st_ref.refs_2_.par_ref, f32[8,640]{1,0:T(8,128)} %allsum3.1.t_ref), custom_call_target="tpu_custom_call" | custom-call | tf_op jit(solution)/shard_map/da/pallas_call | solution.py:670
  260.2 1.4 slice_reduce_fusion
  261.6 5.1 %halo4.1 = (bf16[2,256,640]{2,1,0:T(8,128)(2,1)}, f32[18,1,640]{2,1,0:T(1,128)}, f32[18,1,640]{2,1,0:T(1,128)}) custom-call(bf16[16,256,640]{2,1,0:T(8,128)(2,1)} %get-tuple-element.53.refs_0_.v_ref, f32[16,1,640]{2,1,0:T(1,128)} %get-tuple-element.54.refs_1_, f32[16,1,640]{2,1,0:T(1,128)} %get-tuple-element.55.refs_2_), custom_call_target="tpu_custom_call" | custom-call | tf_op jit(solution)/shard_map/halo4/pallas_call | solution.py:123
  266.8 145.9 %tail.1 = (bf16[16,256,640]{2,1,0:T(8,128)(2,1)}, f32[5760,640]{1,0:T(8,128)}) custom-call(bf16[16,256,640]{2,1,0:T(8,128)(2,1)} %bitcast.14, bf16[2,256,640]{2,1,0:T(8,128)(2,1)} %get-tuple-element.36.rows_ref.urows, f32[18,1,640]{2,1,0:T(1,128)} %get-tuple-element.37.cl_ref.ucl, f32[18,1,640]{2,1,0:T(1,128)} %get-tuple-element.38.cr_ref.ucr, ...), custom_call_target="tpu_custom_call" | custom-call | tf_op jit(solution)/shard_map/tail/pallas_call | solution.py:539
  412.7 44.8 %finish.1 = (bf16[16,256,640]{2,1,0:T(8,128)(2,1)}, bf16[16,256,640]{2,1,0:T(8,128)(2,1)}, f32[5760,640]{1,0:T(8,128)}, f32[5760,640]{1,0:T(8,128)}) custom-call(bf16[16,256,640]{2,1,0:T(8,128)(2,1)} %get-tuple-element.41.refs_0_.u_ref, bf16[2,256,640]{2,1,0:T(8,128)(2,1)} %get-tuple-element.44.urows.rows_ref, f32[18,1,640]{2,1,0:T(1,128)} %get-tuple-element.45.ucl.cl_ref, ...), custom_call_target="tpu_custom_call" | custom-call | tf_op jit(solution)/shard_map/finish/pallas_call | solution.py:628
  (3 shorter events, 0.0 us)

commit v5 on v3

--- a/solution.py
+++ b/solution.py
@@ -36,13 +36,12 @@
     return 0.5 * (1.0 + t) + 0.5 * n * (1.0 - t * t) * (GELU_C * (1.0 + 3.0 * GELU_A * n2))
 
 
-def _halo_kernel(nh, nw, n_arr, *refs):
-    ins = refs[:3 * n_arr]
-    outs = refs[3 * n_arr:6 * n_arr]
-    send, recv = refs[6 * n_arr:]
-    th, tw, c = ins[0].shape
+def _exchange(nh, nw, arrays, send, recv):
+    th, tw, c = arrays[0][0].shape
     w = lax.axis_index("w")
     h = lax.axis_index("x") * 2 + lax.axis_index("c")
+    dirs = [(dh, dw) for dh in (-1, 0, 1) for dw in (-1, 0, 1) if (dh, dw) != (0, 0)]
+    sends = [(k, i, dh, dw) for k in range(len(arrays)) for i, (dh, dw) in enumerate(dirs)]
 
     def dev(dh, dw):
         hh = h + dh
@@ -54,57 +53,48 @@
             ok = cond if ok is None else jnp.logical_and(ok, cond)
         return ok
 
-    dirs = [(dh, dw) for dh in (-1, 0, 1) for dw in (-1, 0, 1) if (dh, dw) != (0, 0)]
-    barrier = pltpu.get_barrier_semaphore()
-    for d in dirs:
-        @pl.when(has(*d))
-        def _(d=d):
-            pl.semaphore_signal(barrier, inc=1, device_id=dev(*d), device_id_type=MESH)
-    one = jnp.int32(1)
-    zero = jnp.int32(0)
-    nv = one + jnp.where(h > 0, one, zero) + jnp.where(h < nh - 1, one, zero)
-    nz = one + jnp.where(w > 0, one, zero) + jnp.where(w < nw - 1, one, zero)
-    pl.semaphore_wait(barrier, nv * nz - 1)
-
-    def parts(k, dh, dw):
-        u, first, last = ins[3 * k:3 * k + 3]
-        rows, cl, cr = outs[3 * k:3 * k + 3]
+    def announce(barrier):
+        for d in dirs:
+            @pl.when(has(*d))
+            def _(d=d):
+                pl.semaphore_signal(barrier, inc=1, device_id=dev(*d), device_id_type=MESH)
+        one = jnp.int32(1)
+        zero = jnp.int32(0)
+        nv = one + jnp.where(h > 0, one, zero) + jnp.where(h < nh - 1, one, zero)
+        nz = one + jnp.where(w > 0, one, zero) + jnp.where(w < nw - 1, one, zero)
+        return nv * nz - 1
+
+    def landing(k, dh, dw):
+        rows, cl, cr = arrays[k][3:]
+        side = cr if dw < 0 else cl
+        if dw == 0:
+            return rows, 1 if dh < 0 else 0
+        if dh == 0:
+            return side, slice(1, th + 1)
+        return side, th + 1 if dh < 0 else 0
+
+    def copy(k, i, dh, dw):
+        u, first, last = arrays[k][:3]
         r = 0 if dh < 0 else th - 1
-        to = 1 if dh < 0 else 0
-        to18 = th + 1 if dh < 0 else 0
-        edge, side = (first, cr) if dw < 0 else (last, cl)
-        if dw == 0:
-            return u.at[r], rows.at[to]
-        if dh == 0:
-            return edge, side.at[1:th + 1]
-        return edge.at[r], side.at[to18]
-
-    def copy(k, i, dh, dw):
-        src, dst = parts(k, dh, dw)
-        return pltpu.make_async_remote_copy(src_ref=src, dst_ref=dst, send_sem=send.at[k * 8 + i], recv_sem=recv.at[k * 8 + i],
+        edge = first if dw < 0 else last
+        src = u.at[r] if dw == 0 else edge if dh == 0 else edge.at[r]
+        ref, at = landing(k, dh, dw)
+        return pltpu.make_async_remote_copy(src_ref=src, dst_ref=ref.at[at], send_sem=send.at[k * 8 + i], recv_sem=recv.at[k * 8 + i],
                                             device_id=dev(dh, dw), device_id_type=MESH)
 
-    for k in range(n_arr):
-        for i, d in enumerate(dirs):
-            @pl.when(has(*d))
-            def _(k=k, i=i, d=d):
-                copy(k, i, *d).start()
-    for k in range(n_arr):
-        rows, cl, cr = outs[3 * k:3 * k + 3]
-        for i, (dh, dw) in enumerate(dirs):
+    def start():
+        for k, i, dh, dw in sends:
+            @pl.when(has(dh, dw))
+            def _(k=k, i=i, dh=dh, dw=dw):
+                copy(k, i, dh, dw).start()
+
+    def finish():
+        for k, i, dh, dw in sends:
             @pl.when(jnp.logical_not(has(-dh, -dw)))
-            def _(rows=rows, cl=cl, cr=cr, dh=dh, dw=dw):
-                to = 1 if dh < 0 else 0
-                to18 = th + 1 if dh < 0 else 0
-                side = cr if dw < 0 else cl
-                if dw == 0:
-                    rows[to] = jnp.zeros((tw, c), BF16)
-                elif dh == 0:
-                    side[1:th + 1] = jnp.zeros((th, 1, c), F32)
-                else:
-                    side[to18] = jnp.zeros((1, c), F32)
-    for k in range(n_arr):
-        for i, (dh, dw) in enumerate(dirs):
+            def _(k=k, dh=dh, dw=dw):
+                ref, at = landing(k, dh, dw)
+                ref[at] = jnp.zeros(ref.at[at].shape, ref.dtype)
+
             @pl.when(has(dh, dw))
             def _(k=k, i=i, dh=dh, dw=dw):
                 copy(k, i, dh, dw).wait_send()
@@ -112,6 +102,18 @@
             @pl.when(has(-dh, -dw))
             def _(k=k, i=i, dh=dh, dw=dw):
                 copy(k, i, dh, dw).wait_recv()
+
+    return announce, start, finish
+
+
+def _halo_kernel(nh, nw, n_arr, *refs):
+    ins = refs[:3 * n_arr]
+    outs = refs[3 * n_arr:6 * n_arr]
+    announce, start, finish = _exchange(nh, nw, [ins[3 * k:3 * k + 3] + outs[3 * k:3 * k + 3] for k in range(n_arr)], *refs[6 * n_arr:])
+    barrier = pltpu.get_barrier_semaphore()
+    pl.semaphore_wait(barrier, announce(barrier))
+    start()
+    finish()
 
 
 def _halo(nh, nw, cid, *us):
@@ -129,7 +131,7 @@
     return [tuple(res[3 * k:3 * k + 3]) for k in range(n)]
 
 
-def _allsum_kernel(nh, nw, cnt, mode, part_ref, par_ref, out_ref, mine, buf, lsem, send, recv):
+def _allsum_kernel(nh, nw, cnt, mode, part_ref, par_ref, out_ref, mine, buf, same, lsem, send, recv):
     n = nh * nw
     w = lax.axis_index("w")
     h = lax.axis_index("x") * 2 + lax.axis_index("c")
@@ -141,6 +143,18 @@
 
     local = pltpu.make_async_copy(part_ref, mine, lsem)
     local.start()
+    c = mine.shape[-1]
+    gi = jnp.floor((lax.broadcasted_iota(jnp.int32, (c, c), 0).astype(F32) + 0.5) * (GROUPS / c))
+    gj = jnp.floor((lax.broadcasted_iota(jnp.int32, (c, c), 1).astype(F32) + 0.5) * (GROUPS / c))
+    same[...] = jnp.where(gi == gj, 1.0, 0.0).astype(BF16)
+
+    def group_means(v):
+        hi = v.astype(BF16)
+        rest = v - hi.astype(F32)
+        mid = rest.astype(BF16)
+        lo = (rest - mid.astype(F32)).astype(BF16)
+        return sum(jnp.dot(x, same[...], preferred_element_type=F32) for x in (lo, mid, hi)) / cnt
+
     barrier = pltpu.get_barrier_semaphore()
     for k in range(1, n):
         pl.semaphore_signal(barrier, inc=1, device_id=dev(lax.rem(me + k, n)), device_id_type=MESH)
@@ -162,18 +176,14 @@
         for k in range(n):
             t = t + jnp.where(off == k, vals[k], 0.0)
         total = t if total is None else total + t
-    c = total.shape[-1]
-    gi = jnp.floor((lax.broadcasted_iota(jnp.int32, (c, c), 0).astype(F32) + 0.5) * (GROUPS / c))
-    gj = jnp.floor((lax.broadcasted_iota(jnp.int32, (c, c), 1).astype(F32) + 0.5) * (GROUPS / c))
-    same = jnp.where(gi == gj, 1.0, 0.0).astype(F32)
     row = lax.broadcasted_iota(jnp.int32, (8, c), 0)
     if mode == 0:
-        m = jnp.dot(total, same, precision=lax.Precision.HIGHEST, preferred_element_type=F32) / cnt
+        m = group_means(total)
         mean, sq = m[0:1], m[1:2]
         rstd = lax.rsqrt(sq - mean * mean + EPS)
         out_ref[...] = jnp.where(row == 0, mean, jnp.where(row == 1, rstd, par_ref[...]))
     else:
-        u = jnp.dot(total * par_ref[2:3], same, precision=lax.Precision.HIGHEST, preferred_element_type=F32) / cnt
+        u = group_means(total * par_ref[2:3])
         out_ref[...] = jnp.where(row == 0, total[0:1], jnp.where(row == 1, total[1:2], jnp.where(row == 2, u[0:1], u[1:2])))
 
 
@@ -183,7 +193,7 @@
     return pl.pallas_call(
         functools.partial(_allsum_kernel, nh, nw, cnt, mode), out_shape=jax.ShapeDtypeStruct((8, c), F32),
         in_specs=[ANY, VM], out_specs=VM,
-        scratch_shapes=[pltpu.VMEM((8, c), F32), pltpu.VMEM((n - 1, 8, c), F32), pltpu.SemaphoreType.DMA,
+        scratch_shapes=[pltpu.VMEM((8, c), F32), pltpu.VMEM((n - 1, 8, c), F32), pltpu.VMEM((c, c), BF16), pltpu.SemaphoreType.DMA,
                         pltpu.SemaphoreType.DMA((n - 1,)), pltpu.SemaphoreType.DMA((n - 1,))],
         compiler_params=pltpu.CompilerParams(collective_id=cid, has_side_effects=True, vmem_limit_bytes=VMEM_LIMIT),
         name=f"allsum{cid}",
@@ -200,7 +210,7 @@
     return cps
 
 
-def _shift_patches(p, cl_ref, cr_ref):
+def _shift_patches(p, cl_ref, cr_ref, r0=0):
     n, tw, c3 = p.shape
     c = c3 // 3
     ck = 128
@@ -209,8 +219,8 @@
         idx = lax.broadcasted_iota(jnp.int32, (tw, ck), 0)
         for k in range(c // ck):
             f = p[r, :, c + k * ck:c + (k + 1) * ck].astype(F32)
-            lo = cl_ref[r, :, k * ck:(k + 1) * ck]
-            hi = cr_ref[r, :, k * ck:(k + 1) * ck]
+            lo = cl_ref[r0 + r, :, k * ck:(k + 1) * ck]
+            hi = cr_ref[r0 + r, :, k * ck:(k + 1) * ck]
             p[r, :, k * ck:(k + 1) * ck] = jnp.where(idx == 0, lo, pltpu.roll(f, 1, 0)).astype(BF16)
             p[r, :, 2 * c + k * ck:2 * c + (k + 1) * ck] = jnp.where(idx == tw - 1, hi, pltpu.roll(f, tw - 1, 0)).astype(BF16)
         return 0
@@ -218,7 +228,11 @@
     lax.fori_loop(0, n, row, 0)
 
 
-def _conv_kernel(rb, epilogue, u_ref, rows_ref, cl_ref, cr_ref, w_ref, *refs):
+def _transposed(v):
+    return v.reshape(v.shape[0] * v.shape[1], v.shape[2]).T
+
+
+def _conv_kernel(rb, epilogue, u_ref, rows_ref, cl_ref, cr_ref, w_ref, v_ref, vt_ref, *refs):
     outs = refs[:-4]
     p, wb, psem, wsem = refs[-4:]
     c = u_ref.shape[2]
@@ -234,6 +248,7 @@
         _shift_patches(p, cl_ref, cr_ref)
         wc.wait()
 
+    vt_ref[...] = _transposed(v_ref[...])
     tw = p.shape[1]
     acc = None
     for a in range(3):
@@ -243,17 +258,18 @@
     epilogue(i, acc, (), outs)
 
 
-def _conv(name, epilogue, u, halo, w, outs, out_specs, rb=2):
+def _conv(name, epilogue, u, halo, w, v, outs, out_specs, rb=2):
     th, tw, c = u.shape
     full = pl.BlockSpec((th + 2, 1, c), lambda i: (0, 0, 0), pipeline_mode=pl.Buffered(1))
     wshape = (3, 3 * c, c)
     return pl.pallas_call(
         functools.partial(_conv_kernel, rb, epilogue),
-        grid=(th // rb,), out_shape=outs, in_specs=[ANY, ANY, full, full, ANY], out_specs=out_specs,
+        grid=(th // rb,), out_shape=[jax.ShapeDtypeStruct((c, th * tw), BF16)] + outs, in_specs=[ANY, ANY, full, full, ANY, out_specs[0]],
+        out_specs=[pl.BlockSpec((c, rb * tw), lambda i: (0, i))] + out_specs,
         scratch_shapes=[pltpu.VMEM((th + 2, tw, 3 * c), BF16), pltpu.VMEM(wshape, BF16), pltpu.SemaphoreType.DMA((3,)), pltpu.SemaphoreType.DMA],
         compiler_params=pltpu.CompilerParams(dimension_semantics=("arbitrary",), vmem_limit_bytes=VMEM_LIMIT),
         name=name,
-    )(u, *halo, w.reshape(wshape))
+    )(u, *halo, w.reshape(wshape), v)
 
 
 def _add_sums(i, s0, s1, s_ref):
@@ -288,43 +304,56 @@
 def _ep_dz(i, acc, extra, outs):
     a_ref, st_ref = extra
     dn_ref, s_ref = outs
-    st = st_ref[...]
-    xhat = (a_ref[...].astype(F32).reshape(acc.shape) - st[0:1]) * st[1:2]
-    dn = acc * _gelu_grad(xhat * st[2:3] + st[3:4])
+    mean, rstd, gamma, beta = _params(st_ref)
+    xhat = (a_ref[...].astype(F32).reshape(acc.shape) - mean) * rstd
+    dn = acc * _gelu_grad(xhat * gamma + beta)
     dn_ref[...] = dn.reshape(dn_ref.shape)
     s0 = (dn * xhat).sum(0, keepdims=True)
     s1 = dn.sum(0, keepdims=True)
     _add_sums(i, s0, s1, s_ref)
 
 
+def _params(st_ref):
+    st = st_ref[...]
+    return [st[k:k + 1] for k in range(4)]
+
+
 def _edges(v, first_ref, last_ref):
     first_ref[...] = v[:, 0:1, :]
     last_ref[...] = v[:, v.shape[1] - 1:, :]
 
 
 def _z_kernel(a_ref, st_ref, z_ref, first_ref, last_ref):
-    st = st_ref[...]
-    xhat = (a_ref[...].astype(F32) - st[0:1]) * st[1:2]
-    z = _gelu(xhat * st[2:3] + st[3:4]).astype(BF16)
+    mean, rstd, gamma, beta = _params(st_ref)
+    xhat = (a_ref[...].astype(F32) - mean) * rstd
+    z = _gelu(xhat * gamma + beta).astype(BF16)
     z_ref[...] = z
     _edges(z.astype(F32), first_ref, last_ref)
 
 
-def _da_kernel(dn_ref, a_ref, st_ref, t_ref, o_ref, first_ref, last_ref):
-    st = st_ref[...]
-    t = t_ref[...]
-    xhat = (a_ref[...].astype(F32) - st[0:1]) * st[1:2]
-    da = (st[1:2] * (dn_ref[...] * st[2:3] - t[3:4] - xhat * t[2:3])).astype(BF16)
+def _copy_kernel(*refs):
+    n = len(refs) // 2
+    for src, dst in zip(refs[:n], refs[n:]):
+        dst[...] = src[...]
+
+
+def _da_kernel(dn_ref, a_ref, st_ref, t_ref, y0_ref, w0_ref, o_ref, ot_ref, first_ref, last_ref, y_ref, w_ref):
+    _copy_kernel(y0_ref, w0_ref, y_ref, w_ref)
+    mean, rstd, gamma, _ = _params(st_ref)
+    _, _, u0, u1 = _params(t_ref)
+    xhat = (a_ref[...].astype(F32) - mean) * rstd
+    da = (rstd * (dn_ref[...] * gamma - u1 - xhat * u0)).astype(BF16)
     o_ref[...] = da
+    ot_ref[...] = _transposed(da)
     _edges(da.astype(F32), first_ref, last_ref)
 
 
-def _fused_kernel(ticks, nu, ep_u, ep_v, n_xu, n_xv, n_ov, u_ref, urows, ucl, ucr, v_ref, vrows, vcl, vcr, w_ref, *refs):
+def _fused_kernel(nh, nw, own_u, ticks, nu, ep_u, ep_v, n_xu, n_xv, n_ov, u_ref, v_ref, vt_ref, first_ref, last_ref, rows_ref, cl_ref, cr_ref, w_ref, *refs):
     xu, refs = refs[:n_xu], refs[n_xu:]
     xv, refs = refs[:n_xv], refs[n_xv:]
     ou, refs = (refs[:1], refs[1:]) if nu else ((), refs)
     ov, refs = refs[:n_ov], refs[n_ov:]
-    dw_ref, p, vt, wb, dsend, hown, recv0, recv1, recv2, psem, wsem, vsem, send, recv, lsem = refs
+    dw_ref, p, vt, wb, dsend, hown, recv0, recv1, recv2, erows, ecl, ecr, psem, wsem, vsem, send, recv, lsem, esend, erecv = refs
     i = pl.program_id(0)
     th, tw, c = u_ref.shape
     nt = w_ref.shape[0]
@@ -341,8 +370,12 @@
         return pltpu.make_async_remote_copy(src_ref=src, dst_ref=dst, send_sem=send.at[stage, t], recv_sem=recv.at[stage, t],
                                             device_id=dev, device_id_type=MESH)
 
+    def tap(t):
+        return lax.rem(2 * lax.rem(t, 3) + 1, 3), lax.rem(2 * lax.div(t, 3) + 1, 3)
+
     def base(t):
-        return t * c + ci * half
+        a, b = tap(t)
+        return (a * 3 + b) * c + ci * half
 
     def s0(t):
         return [rc(0, t, dsend.at[lax.rem(t, 2)], recv0.at[lax.rem(t, 2)], mate)]
@@ -410,37 +443,59 @@
             for cp in s1(t) + s2(t) + s3(t) + s4(t) + s5(t):
                 cp.wait_send()
 
+        lag = 2
         when_chunk(j, lambda t: start(s1(t)))
-        when_chunk(j - 1, t2)
-        when_chunk(j - 2, t3)
-        when_chunk(j - 3, t4)
-        when_chunk(j - 4, t5)
-        when_chunk(j - 1, lambda t: start(s2(t)))
-        when_chunk(j - 2, lambda t: start(s3(t) + keep(t)))
-        when_chunk(j - 5, t6)
+        when_chunk(j - lag, t2)
+        when_chunk(j - 2 * lag, t3)
+        when_chunk(j - 3 * lag, t4)
+        when_chunk(j - 4 * lag, t5)
+        when_chunk(j - lag, lambda t: start(s2(t)))
+        when_chunk(j - 2 * lag, lambda t: start(s3(t) + keep(t)))
+        when_chunk(j - 5 * lag, t6)
 
     wcp = pltpu.make_async_copy(w_ref, wb, wsem)
+    exchanged = u_ref if own_u else v_ref
+    announce, ex_start, ex_finish = _exchange(nh, nw, [(exchanged, first_ref, last_ref, erows, ecl, ecr)], esend, erecv)
+
+    def given_rows():
+        return [pltpu.make_async_copy(rows_ref.at[k], p.at[k * (th + 1), :, c:2 * c], psem.at[k]) for k in range(2)]
+
+    def middle(src):
+        return pltpu.make_async_copy(src, p.at[1:th + 1, :, c:2 * c], psem.at[2])
+
+    def rows_in(own):
+        if own:
+            ex_finish()
+            for k in range(2):
+                p[k * (th + 1), :, c:2 * c] = erows[k]
+        else:
+            for cp in given_rows():
+                cp.wait()
+
+    def shift(own):
+        _shift_patches(p, *((ecl, ecr) if own else (cl_ref, cr_ref)))
 
     @pl.when(i == 0)
     def _():
-        vc = pltpu.make_async_copy(v_ref, p.at[1:th + 1, :, 0:c], vsem)
-        vc.start()
-        cps = _load_patches(u_ref, urows, p, psem)
+        vc = pltpu.make_async_copy(vt_ref, vt, vsem)
+        mc = middle(u_ref)
+        start([vc, mc] + ([] if own_u else given_rows()))
+        barrier = pltpu.get_barrier_semaphore()
+        n = announce(barrier)
+        pl.semaphore_signal(barrier, inc=1, device_id=xn, device_id_type=MESH)
+        pl.semaphore_wait(barrier, n + 1)
+        ex_start()
         wcp.start()
-        barrier = pltpu.get_barrier_semaphore()
-        for d in (mate, xn, yn):
-            pl.semaphore_signal(barrier, inc=1, device_id=d, device_id_type=MESH)
-        pl.semaphore_wait(barrier, 3)
         vc.wait()
-
-        def tr(r, _):
-            vt[:, pl.ds(pl.multiple_of(r * tw, tw), tw)] = p[r + 1, :, 0:c].T
-            return 0
-
-        lax.fori_loop(0, th, tr, 0)
-        for cp in cps:
-            cp.wait()
-        _shift_patches(p, ucl, ucr)
+        mc.wait()
+
+    @pl.when(i == 1)
+    def _():
+        rows_in(own_u)
+
+    @pl.when(i == 3)
+    def _():
+        shift(own_u)
 
     @pl.when(jnp.logical_and(i >= 2, i < nt + 2))
     def _():
@@ -459,10 +514,11 @@
 
     @pl.when(i == nt + nu)
     def _():
-        cps = _load_patches(v_ref, vrows, p, psem)
-        for cp in cps:
-            cp.wait()
-        _shift_patches(p, vcl, vcr)
+        mc = middle(v_ref)
+        start([mc] + (given_rows() if own_u else []))
+        mc.wait()
+        rows_in(not own_u)
+        shift(not own_u)
 
     j = jnp.int32(-1)
     now = jnp.int32(0)
@@ -476,8 +532,7 @@
 
     @pl.when(i < nt)
     def _():
-        a = lax.div(i, 3)
-        b = lax.rem(i, 3)
+        a, b = tap(i)
         rhs = p[pl.ds(a, th), :, pl.ds(pl.multiple_of(b * c, 128), c)].reshape(th * tw, c)
         d = jnp.dot(vt[...], rhs, preferred_element_type=F32).T
         hown[i] = jnp.where(ci == 0, d[:half], d[half:])
@@ -507,7 +562,7 @@
         ep_v(ib, conv(ib, True), xv, ov)
 
 
-def _fused(name, cid, steps, ticks, u, uh, v, vh, w, nu, ep_u, xu, ep_v, xv, outs_v):
+def _fused(nh, nw, name, cid, own_u, steps, ticks, u, v, vt, edges, halo, w, nu, ep_u, xu, ep_v, xv, outs_v):
     th, tw, c = u.shape
     nt, half = 9, c // 2
     last = th // 2 - 1
@@ -515,22 +570,23 @@
     small = pl.BlockSpec((8, c), lambda i: (0, 0))
     ub = pl.BlockSpec((2, tw, c), lambda i: (jnp.minimum(jnp.maximum(i - nt, 0), nu - 1), 0, 0))
     vb = pl.BlockSpec((2, tw, c), lambda i: (jnp.minimum(jnp.maximum(i - nt - nu, 0), last), 0, 0))
-    img = [ANY, ANY, full, full]
     dma = pltpu.SemaphoreType.DMA
+    side = pltpu.VMEM((th + 2, 1, c), F32)
     out_u = [jax.ShapeDtypeStruct((2 * nu, tw, c), BF16)] if nu else []
     call = pl.pallas_call(
-        functools.partial(_fused_kernel, ticks, nu, ep_u, ep_v, len(xu), len(xv), len(outs_v)), grid=(steps,),
+        functools.partial(_fused_kernel, nh, nw, own_u, ticks, nu, ep_u, ep_v, len(xu), len(xv), len(outs_v)), grid=(steps,),
         out_shape=out_u + [o for o, _ in outs_v] + [jax.ShapeDtypeStruct((nt * c, c), F32)],
-        in_specs=img + img + [ANY] + [ub for _ in xu] + [vb if b else small for _, b in xv],
+        in_specs=[ANY] * 6 + [full, full, ANY] + [ub for _ in xu] + [vb if b else small for _, b in xv],
         out_specs=[ub for _ in out_u] + [vb if b else small for _, b in outs_v] + [ANY],
         scratch_shapes=[pltpu.VMEM((th + 2, tw, 3 * c), BF16), pltpu.VMEM((c, th * tw), BF16), pltpu.VMEM((nt, c, c), BF16),
                         pltpu.VMEM((2, half, c), F32), pltpu.VMEM((nt, half, c), F32), pltpu.VMEM((2, half, c), F32),
                         pltpu.VMEM((nt, 2, c // 8, c), F32), pltpu.VMEM((nt, 2, c // 16, c), F32),
-                        dma((3,)), dma, dma, dma((10, nt)), dma((10, nt)), dma((2, nt))],
+                        pltpu.VMEM((2, tw, c), BF16), side, side,
+                        dma((3,)), dma, dma, dma((10, nt)), dma((10, nt)), dma((2, nt)), dma((8,)), dma((8,))],
         compiler_params=pltpu.CompilerParams(dimension_semantics=("arbitrary",), vmem_limit_bytes=VMEM_LIMIT, collective_id=cid, has_side_effects=True),
         name=name,
     )
-    return call(u, *uh, v, *vh, w.reshape(nt, c, c), *[x for x, _ in xu], *[x for x, _ in xv])
+    return call(u, v, vt, *edges, *halo, w.reshape(nt, c, c), *[x for x, _ in xu], *[x for x, _ in xv])
 
 
 def solution(mesh):
@@ -557,17 +613,20 @@
             return u, u[:, 0:1, :].astype(F32), u[:, tw - 1:, :].astype(F32)
 
         xh, gh = _halo(nh, nw, 0, *with_edges(x), *with_edges(g))
-        a, s = _conv("conv1", _ep_conv1, x, xh, w1, [img16, sums], [blk, small])
+        gt, a, s = _conv("conv1", _ep_conv1, x, xh, w1, g, [img16, sums], [blk, small])
         st = _allsum(nh, nw, cnt, 0, 1, s, par)
-        z, z0, z1 = pl.pallas_call(_z_kernel, grid=(th // rb,), out_shape=[img16, edge, edge], in_specs=[blk, small], out_specs=[blk, eblk, eblk], name="act")(a, st)
-        (zh,) = _halo(nh, nw, 2, z, z0, z1)
-        y, dn, t, dw2 = _fused("mid", 5, 25, (2, 3, 4, 6, 8, 9, 11, 13, 15, 17, 18, 20, 21, 22), z, zh, g, gh, w2, 8, _ep_residual, [(x, True)],
-                               _ep_dz, [(a, True), (st, False)], [(img32, True), (sums, False)])
+        z, *ze = pl.pallas_call(_z_kernel, grid=(th // rb,), out_shape=[img16, edge, edge], in_specs=[blk, small], out_specs=[blk, eblk, eblk], name="act")(a, st)
+        y, dn, t, dw2 = _fused(nh, nw, "mid", 5, True, 25, (*range(2, 9), *range(10, 15, 2), *range(15, 24)), z, g, gt, ze, gh, w2, th // 2, _ep_residual,
+                               [(x, True)], _ep_dz, [(a, True), (st, False)], [(img32, True), (sums, False)])
         t = _allsum(nh, nw, cnt, 1, 3, t, st)
-        da, da0, da1 = pl.pallas_call(_da_kernel, grid=(th // rb,), out_shape=[img16, edge, edge], in_specs=[blk, blk, small, small], out_specs=[blk, eblk, eblk], name="da")(dn, a, st, t)
-        (dah,) = _halo(nh, nw, 4, da, da0, da1)
-        dx, dw1 = _fused("tail", 6, 21, (2, 3, 4, 5, 7, 9, 11, 13, 15, 16, 17, 18, 19, 20), x, xh, da, dah, w1, 0, None, [],
+        wblk = pl.BlockSpec((dw2.shape[0] * rb // th, c), lambda i: (i, 0))
+        wout = jax.ShapeDtypeStruct(dw2.shape, F32)
+        da, dat, da0, da1, y, dw2 = pl.pallas_call(
+            _da_kernel, grid=(th // rb,), out_shape=[img16, jax.ShapeDtypeStruct((c, th * tw), BF16), edge, edge, img16, wout], in_specs=[blk, blk, small, small, blk, wblk],
+            out_specs=[blk, pl.BlockSpec((c, rb * tw), lambda i: (0, i)), eblk, eblk, blk, wblk], name="da")(dn, a, st, t, y, dw2)
+        dx, dw1 = _fused(nh, nw, "tail", 6, False, 25, (*range(2, 9), *range(10, 15, 2), *range(16, 25)), x, da, dat, (da0, da1), xh, w1, 0, None, [],
                          _ep_residual, [(g, True)], [(img16, True)])
+        dx, dw1 = pl.pallas_call(_copy_kernel, grid=(th // rb,), out_shape=[img16, wout], in_specs=[blk, wblk], out_specs=[blk, wblk], name="finish")(dx, dw1)
         return y[None], dx[None], dw1.reshape(w1.shape), dw2.reshape(w2.shape), t[0], t[1]
 
     return jax.shard_map(body, mesh=mesh3, in_specs=(tile, P(), P(), P(), P(), tile), out_specs=(tile, tile, P(), P(), P(), P()), check_vma=False)

time: 483 us -> 446 us (0.923)
  local copies, waits for them, and re-layouts: 34.2 us -> 2.88 us
  Pallas kernels: 445 us -> 439 us
    unnamed x6 -> x0, local copies, waits for them, and re-layouts: 31.3 us -> none
    pallas_call x3 -> x1, Pallas kernels: 18.6 us -> 7.84 us  [_halo(): pl.pallas_call(functools.partial(_halo_kernel, nh, nw, n), out_shape=out,...]
    pallas_call x3 -> x4, Pallas kernels: 348 us -> 353 us  [the longest x2 315 us: _fused(): call(u, v, vt, *edges, *halo, w.reshape(nt, c, c), *[x for x, _ in xu], *...]
where the time goes in v5:
time: 446 us
  Pallas kernels  439 us (98%)
    pallas_call x2, Pallas kernels, _fused(): call(u, v, vt, *edges, *halo, w.reshape(nt, c, c), *[x for x, _ in xu], *...  315 us
    pallas_call x1, Pallas kernels, _conv(): pl.pallas_call(functools.partial(_conv_kernel, rb, epilogue), grid=(th //...  47.7 us
    pallas_call x1, Pallas kernels, body(): pl.pallas_call(_da_kernel, grid=(th // rb,), out_shape=[img16, jax.ShapeD...  22.4 us
    pallas_call x2, Pallas kernels, _allsum(): pl.pallas_call(functools.partial(_allsum_kernel, nh, nw, cnt, mode), out_...  21.9 us
    pallas_call x1, Pallas kernels, body(): pl.pallas_call(_copy_kernel, grid=(th // rb,), out_shape=[img16, wout], i...  15.6 us
    pallas_call x1, Pallas kernels, body(): pl.pallas_call(_z_kernel, grid=(th // rb,), out_shape=[img16, edge, edge]...  9.3 us

profile of v5, /device:TPU:0, one launch (start us, length us, event | category | flops | bytes accessed | tf_op | source)
XLA Modules:
  0.0 445.6 jit_solution(16041788152048931886)
XLA Ops:
  0.6 0.1 pad.3.clone
  0.7 0.7 broadcast_in_dim.19
  1.4 0.7 broadcast_in_dim.20
  2.1 0.7 maximum_maximum_fusion.par_ref
  2.8 1.9 slice_convert_fusion
  4.7 7.8 %halo0.1 = (bf16[2,256,640]{2,1,0:T(8,128)(2,1)}, f32[18,1,640]{2,1,0:T(1,128)}, f32[18,1,640]{2,1,0:T(1,128)}, bf16[2,256,640]{2,1,0:T(8,128)(2,1)}, f32[18,1,640]{2,1,0:T(1,128)}, /*index=5*/f32[18,1,640]{2,1,0:T(1,128)}) custom-call(bf16[16,256,640]{2,1,0:T(8,128)(2,1)} %bitcast.10, f32[16,1,640]{2,1,0:T(1,128)} %get-tuple-element.64.refs_1_, ...), custom_call_target="tpu_custom_call" | custom-call | tf_op jit(solution)/shard_map/halo0/pallas_call | solution.py:125
  12.5 47.7 %conv1.1 = (bf16[640,4096]{1,0:T(8,128)(2,1)}, bf16[16,256,640]{2,1,0:T(8,128)(2,1)}, f32[8,640]{1,0:T(8,128)}) custom-call(bf16[16,256,640]{2,1,0:T(8,128)(2,1)} %bitcast.11, bf16[2,256,640]{2,1,0:T(8,128)(2,1)} %get-tuple-element.32.rows_ref, f32[18,1,640]{2,1,0:T(1,128)} %get-tuple-element.33.cl_ref, f32[18,1,640]{2,1,0:T(1,128)} %get-tuple-element.34.cr_ref, ...), custom_call_target="tpu_custom_call" | custom-call | tf_op jit(solution)/shard_map/conv1/pallas_call | solution.py:265
  60.2 14.2 %allsum1.1.st_ref.refs_2_.par_ref = f32[8,640]{1,0:T(8,128)} custom-call(f32[8,640]{1,0:T(8,128)} %get-tuple-element.36.part_ref, f32[8,640]{1,0:T(8,128)} %maximum_maximum_fusion.par_ref), custom_call_target="tpu_custom_call" | custom-call | tf_op jit(solution)/shard_map/allsum1/pallas_call | solution.py:193
  74.4 9.3 %act.1 = (bf16[16,256,640]{2,1,0:T(8,128)(2,1)}, f32[16,1,640]{2,1,0:T(1,128)}, f32[16,1,640]{2,1,0:T(1,128)}) custom-call(bf16[16,256,640]{2,1,0:T(8,128)(2,1)} %get-tuple-element.35.a_ref.refs_1_, f32[8,640]{1,0:T(8,128)} %allsum1.1.st_ref.refs_2_.par_ref), custom_call_target="tpu_custom_call" | custom-call | tf_op jit(solution)/shard_map/act/pallas_call | solution.py:618
  83.7 170.9 %mid.1 = (bf16[16,256,640]{2,1,0:T(8,128)(2,1)}, f32[16,256,640]{2,1,0:T(8,128)}, f32[8,640]{1,0:T(8,128)}, f32[5760,640]{1,0:T(8,128)}) custom-call(bf16[16,256,640]{2,1,0:T(8,128)(2,1)} %get-tuple-element.37.u_ref, bf16[16,256,640]{2,1,0:T(8,128)(2,1)} %bitcast.17, bf16[640,4096]{1,0:T(8,128)(2,1)} %get-tuple-element.38.vt_ref, ...), custom_call_target="tpu_custom_call" | custom-call | tf_op jit(solution)/shard_map/mid/pallas_call | solution.py:589
  254.6 7.7 %allsum3.1.t_ref = f32[8,640]{1,0:T(8,128)} custom-call(f32[8,640]{1,0:T(8,128)} %get-tuple-element.45.part_ref, f32[8,640]{1,0:T(8,128)} %allsum1.1.st_ref.refs_2_.par_ref), custom_call_target="tpu_custom_call" | custom-call | tf_op jit(solution)/shard_map/allsum3/pallas_call | solution.py:193
  262.3 22.4 %da.1 = (bf16[16,256,640]{2,1,0:T(8,128)(2,1)}, bf16[640,4096]{1,0:T(8,128)(2,1)}, f32[16,1,640]{2,1,0:T(1,128)}, f32[16,1,640]{2,1,0:T(1,128)}, bf16[16,256,640]{2,1,0:T(8,128)(2,1)}, /*index=5*/f32[5760,640]{1,0:T(8,128)}) custom-call(f32[16,256,640]{2,1,0:T(8,128)} %get-tuple-element.44.dn_ref, bf16[16,256,640]{2,1,0:T(8,128)(2,1)} %get-tuple-element.35.a_ref.refs_1_, ...), custom_call_target="tpu_custom_call" | custom-call | tf_op jit(solution)/shard_map/da/pallas_call | solution.py:624
  284.7 1.4 slice_reduce_fusion
  286.1 143.9 %tail.1 = (bf16[16,256,640]{2,1,0:T(8,128)(2,1)}, f32[5760,640]{1,0:T(8,128)}) custom-call(bf16[16,256,640]{2,1,0:T(8,128)(2,1)} %bitcast.13, bf16[16,256,640]{2,1,0:T(8,128)(2,1)} %get-tuple-element.49.v_ref, bf16[640,4096]{1,0:T(8,128)(2,1)} %get-tuple-element.50.vt_ref, f32[16,1,640]{2,1,0:T(1,128)} %get-tuple-element.51.first_ref, ...), custom_call_target="tpu_custom_call" | custom-call | tf_op jit(solution)/shard_map/tail/pallas_call | solution.py:589
  430.0 15.6 %finish.1 = (bf16[16,256,640]{2,1,0:T(8,128)(2,1)}, f32[5760,640]{1,0:T(8,128)}) custom-call(bf16[16,256,640]{2,1,0:T(8,128)(2,1)} %get-tuple-element.53.refs_0_, f32[5760,640]{1,0:T(8,128)} %get-tuple-element.54.refs_1_), custom_call_target="tpu_custom_call" | custom-call | tf_op jit(solution)/shard_map/finish/pallas_call | solution.py:629
  (3 shorter events, 0.0 us)

commit v6 on v5

--- a/solution.py
+++ b/solution.py
@@ -18,6 +18,10 @@
 VM = pl.BlockSpec(memory_space=pltpu.VMEM)
 GELU_C = 0.7978845608028654
 GELU_A = 0.044715
+
+
+def _whole(*shape, **kw):
+    return pl.BlockSpec(shape, lambda i: (0,) * len(shape), **kw)
 
 
 def _gelu_parts(n):
@@ -210,7 +214,7 @@
     return cps
 
 
-def _shift_patches(p, cl_ref, cr_ref, r0=0):
+def _shift_patches(p, cl_ref, cr_ref, first=0):
     n, tw, c3 = p.shape
     c = c3 // 3
     ck = 128
@@ -219,13 +223,13 @@
         idx = lax.broadcasted_iota(jnp.int32, (tw, ck), 0)
         for k in range(c // ck):
             f = p[r, :, c + k * ck:c + (k + 1) * ck].astype(F32)
-            lo = cl_ref[r0 + r, :, k * ck:(k + 1) * ck]
-            hi = cr_ref[r0 + r, :, k * ck:(k + 1) * ck]
+            lo = cl_ref[r, :, k * ck:(k + 1) * ck]
+            hi = cr_ref[r, :, k * ck:(k + 1) * ck]
             p[r, :, k * ck:(k + 1) * ck] = jnp.where(idx == 0, lo, pltpu.roll(f, 1, 0)).astype(BF16)
             p[r, :, 2 * c + k * ck:2 * c + (k + 1) * ck] = jnp.where(idx == tw - 1, hi, pltpu.roll(f, tw - 1, 0)).astype(BF16)
         return 0
 
-    lax.fori_loop(0, n, row, 0)
+    lax.fori_loop(first, n, row, 0)
 
 
 def _transposed(v):
@@ -260,7 +264,7 @@
 
 def _conv(name, epilogue, u, halo, w, v, outs, out_specs, rb=2):
     th, tw, c = u.shape
-    full = pl.BlockSpec((th + 2, 1, c), lambda i: (0, 0, 0), pipeline_mode=pl.Buffered(1))
+    full = _whole(th + 2, 1, c, pipeline_mode=pl.Buffered(1))
     wshape = (3, 3 * c, c)
     return pl.pallas_call(
         functools.partial(_conv_kernel, rb, epilogue),
@@ -331,14 +335,22 @@
     _edges(z.astype(F32), first_ref, last_ref)
 
 
-def _copy_kernel(*refs):
-    n = len(refs) // 2
-    for src, dst in zip(refs[:n], refs[n:]):
-        dst[...] = src[...]
-
-
-def _da_kernel(dn_ref, a_ref, st_ref, t_ref, y0_ref, w0_ref, o_ref, ot_ref, first_ref, last_ref, y_ref, w_ref):
-    _copy_kernel(y0_ref, w0_ref, y_ref, w_ref)
+def _finish_kernel(ny, y0_ref, y1_ref, dx0_ref, w0_ref, y_ref, dx_ref, w_ref):
+    dx_ref[...] = dx0_ref[...]
+    w_ref[...] = w0_ref[...]
+    first = pl.program_id(0) < ny
+
+    @pl.when(first)
+    def _():
+        y_ref[...] = y0_ref[...]
+
+    @pl.when(jnp.logical_not(first))
+    def _():
+        y_ref[...] = y1_ref[...]
+
+
+def _da_kernel(dn_ref, a_ref, st_ref, t_ref, w0_ref, o_ref, ot_ref, first_ref, last_ref, w_ref):
+    w_ref[...] = w0_ref[...]
     mean, rstd, gamma, _ = _params(st_ref)
     _, _, u0, u1 = _params(t_ref)
     xhat = (a_ref[...].astype(F32) - mean) * rstd
@@ -348,11 +360,17 @@
     _edges(da.astype(F32), first_ref, last_ref)
 
 
-def _fused_kernel(nh, nw, own_u, ticks, nu, ep_u, ep_v, n_xu, n_xv, n_ov, u_ref, v_ref, vt_ref, first_ref, last_ref, rows_ref, cl_ref, cr_ref, w_ref, *refs):
+def _fused_kernel(nh, nw, own_u, ticks, nu, nz, ep_u, ep_v, n_xu, n_xv, n_ov, u_ref, v_ref, vt_ref, first_ref, last_ref, rows_ref, cl_ref, cr_ref, w_ref, *refs):
     xu, refs = refs[:n_xu], refs[n_xu:]
     xv, refs = refs[:n_xv], refs[n_xv:]
+    if nz:
+        (z_ref, zrows, zcl, zcr, w2_ref), xz, refs = refs[:5], refs[5:6], refs[6:]
     ou, refs = (refs[:1], refs[1:]) if nu else ((), refs)
     ov, refs = refs[:n_ov], refs[n_ov:]
+    if nz:
+        oz, refs = refs[:1], refs[1:]
+    if own_u:
+        handed, refs = refs[:3], refs[3:]
     dw_ref, p, vt, wb, dsend, hown, recv0, recv1, recv2, erows, ecl, ecr, psem, wsem, vsem, send, recv, lsem, esend, erecv = refs
     i = pl.program_id(0)
     th, tw, c = u_ref.shape
@@ -457,8 +475,8 @@
     exchanged = u_ref if own_u else v_ref
     announce, ex_start, ex_finish = _exchange(nh, nw, [(exchanged, first_ref, last_ref, erows, ecl, ecr)], esend, erecv)
 
-    def given_rows():
-        return [pltpu.make_async_copy(rows_ref.at[k], p.at[k * (th + 1), :, c:2 * c], psem.at[k]) for k in range(2)]
+    def given_rows(ref=rows_ref):
+        return [pltpu.make_async_copy(ref.at[k], p.at[k * (th + 1), :, c:2 * c], psem.at[k]) for k in range(2)]
 
     def middle(src):
         return pltpu.make_async_copy(src, p.at[1:th + 1, :, c:2 * c], psem.at[2])
@@ -492,6 +510,9 @@
     @pl.when(i == 1)
     def _():
         rows_in(own_u)
+        if own_u:
+            for dst, src in zip(handed, (erows, ecl, ecr)):
+                dst[...] = src[...]
 
     @pl.when(i == 3)
     def _():
@@ -519,6 +540,15 @@
         mc.wait()
         rows_in(not own_u)
         shift(not own_u)
+
+    if nz:
+        @pl.when(i == nt + nu + th // 2)
+        def _():
+            cps = [middle(z_ref), pltpu.make_async_copy(w2_ref, wb, wsem)] + given_rows(zrows)
+            start(cps)
+            for cp in cps:
+                cp.wait()
+            _shift_patches(p, zcl, zcr, th - 2 * nz)
 
     j = jnp.int32(-1)
     now = jnp.int32(0)
@@ -561,23 +591,35 @@
         ib = i - nt - nu
         ep_v(ib, conv(ib, True), xv, ov)
 
-
-def _fused(nh, nw, name, cid, own_u, steps, ticks, u, v, vt, edges, halo, w, nu, ep_u, xu, ep_v, xv, outs_v):
+    if nz:
+        @pl.when(jnp.logical_and(i >= nt + nu + th // 2, i < nt + nu + th // 2 + nz))
+        def _():
+            ib = i - nt - nu - nz
+            ep_u(ib, conv(ib, False), xz, oz)
+
+
+def _fused(nh, nw, name, cid, own_u, steps, ticks, u, v, vt, edges, halo, w, nu, ep_u, xu, ep_v, xv, outs_v, z_args=(), nz=0):
     th, tw, c = u.shape
     nt, half = 9, c // 2
     last = th // 2 - 1
-    full = pl.BlockSpec((th + 2, 1, c), lambda i: (0, 0, 0), pipeline_mode=pl.Buffered(1))
-    small = pl.BlockSpec((8, c), lambda i: (0, 0))
+    full = _whole(th + 2, 1, c, pipeline_mode=pl.Buffered(1))
+    small = _whole(8, c)
     ub = pl.BlockSpec((2, tw, c), lambda i: (jnp.minimum(jnp.maximum(i - nt, 0), nu - 1), 0, 0))
     vb = pl.BlockSpec((2, tw, c), lambda i: (jnp.minimum(jnp.maximum(i - nt - nu, 0), last), 0, 0))
     dma = pltpu.SemaphoreType.DMA
     side = pltpu.VMEM((th + 2, 1, c), F32)
     out_u = [jax.ShapeDtypeStruct((2 * nu, tw, c), BF16)] if nu else []
+    zb, yb = [pl.BlockSpec((2, tw, c), lambda i, k=k: (jnp.minimum(jnp.maximum(i - nt - nu - last - 1, 0), nz - 1) + k, 0, 0)) for k in (last + 1 - nz, 0)]
+    out_z = [jax.ShapeDtypeStruct((2 * nz, tw, c), BF16)] if nz else []
+    rblk = _whole(2, tw, c)
+    sblk = _whole(th + 2, 1, c)
+    given = jax.ShapeDtypeStruct((th + 2, 1, c), F32)
+    out_h = [jax.ShapeDtypeStruct((2, tw, c), BF16), given, given] if own_u else []
     call = pl.pallas_call(
-        functools.partial(_fused_kernel, nh, nw, own_u, ticks, nu, ep_u, ep_v, len(xu), len(xv), len(outs_v)), grid=(steps,),
-        out_shape=out_u + [o for o, _ in outs_v] + [jax.ShapeDtypeStruct((nt * c, c), F32)],
-        in_specs=[ANY] * 6 + [full, full, ANY] + [ub for _ in xu] + [vb if b else small for _, b in xv],
-        out_specs=[ub for _ in out_u] + [vb if b else small for _, b in outs_v] + [ANY],
+        functools.partial(_fused_kernel, nh, nw, own_u, ticks, nu, nz, ep_u, ep_v, len(xu), len(xv), len(outs_v)), grid=(steps,),
+        out_shape=out_u + [o for o, _ in outs_v] + out_z + out_h + [jax.ShapeDtypeStruct((nt * c, c), F32)],
+        in_specs=[ANY] * 6 + [full, full, ANY] + [ub for _ in xu] + [vb if b else small for _, b in xv] + ([ANY, ANY, full, full, ANY, zb] if nz else []),
+        out_specs=[ub for _ in out_u] + [vb if b else small for _, b in outs_v] + [yb for _ in out_z] + ([rblk, sblk, sblk] if own_u else []) + [ANY],
         scratch_shapes=[pltpu.VMEM((th + 2, tw, 3 * c), BF16), pltpu.VMEM((c, th * tw), BF16), pltpu.VMEM((nt, c, c), BF16),
                         pltpu.VMEM((2, half, c), F32), pltpu.VMEM((nt, half, c), F32), pltpu.VMEM((2, half, c), F32),
                         pltpu.VMEM((nt, 2, c // 8, c), F32), pltpu.VMEM((nt, 2, c // 16, c), F32),
@@ -586,7 +628,7 @@
         compiler_params=pltpu.CompilerParams(dimension_semantics=("arbitrary",), vmem_limit_bytes=VMEM_LIMIT, collective_id=cid, has_side_effects=True),
         name=name,
     )
-    return call(u, v, vt, *edges, *halo, w.reshape(nt, c, c), *[x for x, _ in xu], *[x for x, _ in xv])
+    return call(u, v, vt, *edges, *halo, w.reshape(nt, c, c), *[x for x, _ in xu], *[x for x, _ in xv], *z_args)
 
 
 def solution(mesh):
@@ -600,7 +642,7 @@
         cnt = float(th * nh * tw * nw * (c // GROUPS))
         rb = 2
         blk = pl.BlockSpec((rb, tw, c), lambda i: (i, 0, 0))
-        small = pl.BlockSpec((8, c), lambda i: (0, 0))
+        small = _whole(8, c)
         img16 = jax.ShapeDtypeStruct((th, tw, c), BF16)
         img32 = jax.ShapeDtypeStruct((th, tw, c), F32)
         sums = jax.ShapeDtypeStruct((8, c), F32)
@@ -616,17 +658,20 @@
         gt, a, s = _conv("conv1", _ep_conv1, x, xh, w1, g, [img16, sums], [blk, small])
         st = _allsum(nh, nw, cnt, 0, 1, s, par)
         z, *ze = pl.pallas_call(_z_kernel, grid=(th // rb,), out_shape=[img16, edge, edge], in_specs=[blk, small], out_specs=[blk, eblk, eblk], name="act")(a, st)
-        y, dn, t, dw2 = _fused(nh, nw, "mid", 5, True, 25, (*range(2, 9), *range(10, 15, 2), *range(15, 24)), z, g, gt, ze, gh, w2, th // 2, _ep_residual,
-                               [(x, True)], _ep_dz, [(a, True), (st, False)], [(img32, True), (sums, False)])
+        ny, nz = 3, th // rb - 3
+        y0, dn, t, *zh, dw2 = _fused(nh, nw, "mid", 5, True, 24, (*range(2, 9), *range(10, 15, 2), *range(15, 24)), z, g, gt, ze, gh, w2, ny, _ep_residual,
+                                     [(x, True)], _ep_dz, [(a, True), (st, False)], [(img32, True), (sums, False)])
         t = _allsum(nh, nw, cnt, 1, 3, t, st)
         wblk = pl.BlockSpec((dw2.shape[0] * rb // th, c), lambda i: (i, 0))
         wout = jax.ShapeDtypeStruct(dw2.shape, F32)
-        da, dat, da0, da1, y, dw2 = pl.pallas_call(
-            _da_kernel, grid=(th // rb,), out_shape=[img16, jax.ShapeDtypeStruct((c, th * tw), BF16), edge, edge, img16, wout], in_specs=[blk, blk, small, small, blk, wblk],
-            out_specs=[blk, pl.BlockSpec((c, rb * tw), lambda i: (0, i)), eblk, eblk, blk, wblk], name="da")(dn, a, st, t, y, dw2)
-        dx, dw1 = _fused(nh, nw, "tail", 6, False, 25, (*range(2, 9), *range(10, 15, 2), *range(16, 25)), x, da, dat, (da0, da1), xh, w1, 0, None, [],
-                         _ep_residual, [(g, True)], [(img16, True)])
-        dx, dw1 = pl.pallas_call(_copy_kernel, grid=(th // rb,), out_shape=[img16, wout], in_specs=[blk, wblk], out_specs=[blk, wblk], name="finish")(dx, dw1)
+        da, dat, da0, da1, dw2 = pl.pallas_call(
+            _da_kernel, grid=(th // rb,), out_shape=[img16, jax.ShapeDtypeStruct((c, th * tw), BF16), edge, edge, wout], in_specs=[blk, blk, small, small, wblk],
+            out_specs=[blk, pl.BlockSpec((c, rb * tw), lambda i: (0, i)), eblk, eblk, wblk], name="da")(dn, a, st, t, dw2)
+        dx, y1, dw1 = _fused(nh, nw, "tail", 6, False, 25, (*range(2, 9), *range(10, 15, 2), *range(16, 25)), x, da, dat, (da0, da1), xh, w1, 0, _ep_residual, [],
+                             _ep_residual, [(g, True)], [(img16, True)], (z, *zh, w2.reshape(9, c, c), x), nz)
+        lo, hi = pl.BlockSpec((rb, tw, c), lambda i: (jnp.minimum(i, ny - 1), 0, 0)), pl.BlockSpec((rb, tw, c), lambda i: (jnp.maximum(i - ny, 0), 0, 0))
+        y, dx, dw1 = pl.pallas_call(functools.partial(_finish_kernel, ny), grid=(th // rb,), out_shape=[img16, img16, wout],
+                                    in_specs=[lo, hi, blk, wblk], out_specs=[blk, blk, wblk], name="finish")(y0, y1, dx, dw1)
         return y[None], dx[None], dw1.reshape(w1.shape), dw2.reshape(w2.shape), t[0], t[1]
 
     return jax.shard_map(body, mesh=mesh3, in_specs=(tile, P(), P(), P(), P(), tile), out_specs=(tile, tile, P(), P(), P(), P()), check_vma=False)

time: 446 us -> 424 us (0.951)
  Pallas kernels: 439 us -> 418 us
    pallas_call x2, Pallas kernels: 315 us -> 292 us  [_fused(): call(u, v, vt, *edges, *halo, w.reshape(nt, c, c), *[x for x, _ in xu], *...]
where the time goes in v6:
time: 424 us
  Pallas kernels  418 us (99%)
    pallas_call x2, Pallas kernels, _fused(): call(u, v, vt, *edges, *halo, w.reshape(nt, c, c), *[x for x, _ in xu], *...  292 us
    pallas_call x1, Pallas kernels, _conv(): pl.pallas_call(functools.partial(_conv_kernel, rb, epilogue), grid=(th //...  47.7 us
    pallas_call x2, Pallas kernels, _allsum(): pl.pallas_call(functools.partial(_allsum_kernel, nh, nw, cnt, mode), out_...  21.9 us
    pallas_call x1, Pallas kernels, body(): pl.pallas_call(_da_kernel, grid=(th // rb,), out_shape=[img16, jax.ShapeD...  19.9 us
    pallas_call x1, Pallas kernels, body(): pl.pallas_call(functools.partial(_finish_kernel, ny), grid=(th // rb,), o...  18.5 us
    pallas_call x1, Pallas kernels, body(): pl.pallas_call(_z_kernel, grid=(th // rb,), out_shape=[img16, edge, edge]...  9.3 us

profile of v6, /device:TPU:0, one launch (start us, length us, event | category | flops | bytes accessed | tf_op | source)
XLA Modules:
  0.0 423.7 jit_solution(10660864736746438474)
XLA Ops:
  0.6 0.1 pad.3.clone
  0.7 0.7 broadcast_in_dim.19
  1.4 0.7 broadcast_in_dim.20
  2.1 0.7 maximum_maximum_fusion.par_ref
  2.8 1.9 slice_convert_fusion
  4.7 7.9 %halo0.1 = (bf16[2,256,640]{2,1,0:T(8,128)(2,1)}, f32[18,1,640]{2,1,0:T(1,128)}, f32[18,1,640]{2,1,0:T(1,128)}, bf16[2,256,640]{2,1,0:T(8,128)(2,1)}, f32[18,1,640]{2,1,0:T(1,128)}, /*index=5*/f32[18,1,640]{2,1,0:T(1,128)}) custom-call(bf16[16,256,640]{2,1,0:T(8,128)(2,1)} %bitcast.10, f32[16,1,640]{2,1,0:T(1,128)} %get-tuple-element.72.refs_1_, ...), custom_call_target="tpu_custom_call" | custom-call | tf_op jit(solution)/shard_map/halo0/pallas_call | solution.py:129
  12.6 47.7 %conv1.1 = (bf16[640,4096]{1,0:T(8,128)(2,1)}, bf16[16,256,640]{2,1,0:T(8,128)(2,1)}, f32[8,640]{1,0:T(8,128)}) custom-call(bf16[16,256,640]{2,1,0:T(8,128)(2,1)} %bitcast.11, bf16[2,256,640]{2,1,0:T(8,128)(2,1)} %get-tuple-element.36.rows_ref, f32[18,1,640]{2,1,0:T(1,128)} %get-tuple-element.37.cl_ref, f32[18,1,640]{2,1,0:T(1,128)} %get-tuple-element.38.cr_ref, ...), custom_call_target="tpu_custom_call" | custom-call | tf_op jit(solution)/shard_map/conv1/pallas_call | solution.py:269
  60.3 14.2 %allsum1.1.st_ref.refs_2_.par_ref = f32[8,640]{1,0:T(8,128)} custom-call(f32[8,640]{1,0:T(8,128)} %get-tuple-element.40.part_ref, f32[8,640]{1,0:T(8,128)} %maximum_maximum_fusion.par_ref), custom_call_target="tpu_custom_call" | custom-call | tf_op jit(solution)/shard_map/allsum1/pallas_call | solution.py:197
  74.5 9.3 %act.1 = (bf16[16,256,640]{2,1,0:T(8,128)(2,1)}, f32[16,1,640]{2,1,0:T(1,128)}, f32[16,1,640]{2,1,0:T(1,128)}) custom-call(bf16[16,256,640]{2,1,0:T(8,128)(2,1)} %get-tuple-element.39.a_ref.refs_1_, f32[8,640]{1,0:T(8,128)} %allsum1.1.st_ref.refs_2_.par_ref), custom_call_target="tpu_custom_call" | custom-call | tf_op jit(solution)/shard_map/act/pallas_call | solution.py:660
  83.8 145.3 %mid.1 = (bf16[6,256,640]{2,1,0:T(8,128)(2,1)}, f32[16,256,640]{2,1,0:T(8,128)}, f32[8,640]{1,0:T(8,128)}, bf16[2,256,640]{2,1,0:T(8,128)(2,1)}, f32[18,1,640]{2...) custom-call(bf16[16,256,640]{2,1,0:T(8,128)(2,1)} %get-tuple-element.41.u_ref.refs_1_, ...), custom_call_target="tpu_custom_call" | custom-call | tf_op jit(solution)/shard_map/mid/pallas_call | solution.py:631
  229.2 7.7 %allsum3.1.t_ref = f32[8,640]{1,0:T(8,128)} custom-call(f32[8,640]{1,0:T(8,128)} %get-tuple-element.50.part_ref, f32[8,640]{1,0:T(8,128)} %allsum1.1.st_ref.refs_2_.par_ref), custom_call_target="tpu_custom_call" | custom-call | tf_op jit(solution)/shard_map/allsum3/pallas_call | solution.py:197
  236.9 19.9 %da.1 = (bf16[16,256,640]{2,1,0:T(8,128)(2,1)}, bf16[640,4096]{1,0:T(8,128)(2,1)}, f32[16,1,640]{2,1,0:T(1,128)}, f32[16,1,640]{2,1,0:T(1,128)}, f32[5760,640]{1,0:T(8,128)}) custom-call(f32[16,256,640]{2,1,0:T(8,128)} %get-tuple-element.49.dn_ref, bf16[16,256,640]{2,1,0:T(8,128)(2,1)} %get-tuple-element.39.a_ref.refs_1_, ...), custom_call_target="tpu_custom_call" | custom-call | tf_op jit(solution)/shard_map/da/pallas_call | solution.py:667
  256.8 1.4 slice_reduce_fusion
  258.2 147.0 %tail.1 = (bf16[16,256,640]{2,1,0:T(8,128)(2,1)}, bf16[10,256,640]{2,1,0:T(8,128)(2,1)}, f32[5760,640]{1,0:T(8,128)}) custom-call(bf16[16,256,640]{2,1,0:T(8,128)(2,1)} %bitcast.13, bf16[16,256,640]{2,1,0:T(8,128)(2,1)} %get-tuple-element.52.v_ref, bf16[640,4096]{1,0:T(8,128)(2,1)} %get-tuple-element.53.vt_ref, f32[16,1,640]{2,1,0:T(1,128)} %get-tuple-element.54.first_ref, ...), custom_call_target="tpu_custom_call" | custom-call | tf_op jit(solution)/shard_map/tail/pallas_call | solution.py:631
  405.1 18.5 %finish.1 = (bf16[16,256,640]{2,1,0:T(8,128)(2,1)}, bf16[16,256,640]{2,1,0:T(8,128)(2,1)}, f32[5760,640]{1,0:T(8,128)}) custom-call(bf16[6,256,640]{2,1,0:T(8,128)(2,1)} %get-tuple-element.48.y0_ref, bf16[10,256,640]{2,1,0:T(8,128)(2,1)} %get-tuple-element.59.y1_ref, bf16[16,256,640]{2,1,0:T(8,128)(2,1)} %get-tuple-element.60.dx0_ref, ...), custom_call_target="tpu_custom_call" | custom-call | tf_op jit(solution)/shard_map/finish/pallas_call | solution.py:673
  (3 shorter events, 0.0 us)

commit v7 on v5

v7 whole, which is shorter than its diff:
```python
import functools

import jax
import jax.numpy as jnp
from jax import lax
from jax.experimental import pallas as pl
from jax.experimental.pallas import tpu as pltpu
from jax.sharding import Mesh
from jax.sharding import PartitionSpec as P

GROUPS = 32
EPS = 1e-5
F32 = jnp.float32
BF16 = jnp.bfloat16
MESH = pl.DeviceIdType.MESH
VMEM_LIMIT = 67043328
ANY = pl.BlockSpec(memory_space=pl.ANY)
VM = pl.BlockSpec(memory_space=pltpu.VMEM)
GELU_C = 0.7978845608028654
GELU_A = 0.044715


def _whole(*shape, **kw):
    return pl.BlockSpec(shape, lambda i: (0,) * len(shape), **kw)


def _gelu_parts(n):
    n2 = n * n
    t = jnp.tanh(GELU_C * (n + GELU_A * n * n2))
    return n2, t


def _gelu(n):
    _, t = _gelu_parts(n)
    return 0.5 * n * (1.0 + t)


def _gelu_grad(n):
    n2, t = _gelu_parts(n)
    return 0.5 * (1.0 + t) + 0.5 * n * (1.0 - t * t) * (GELU_C * (1.0 + 3.0 * GELU_A * n2))


def _exchange(nh, nw, arrays, send, recv):
    th, tw, c = arrays[0][0].shape
    w = lax.axis_index("w")
    h = lax.axis_index("x") * 2 + lax.axis_index("c")
    dirs = [(dh, dw) for dh in (-1, 0, 1) for dw in (-1, 0, 1) if (dh, dw) != (0, 0)]
    sends = [(k, i, dh, dw) for k in range(len(arrays)) for i, (dh, dw) in enumerate(dirs)]

    def dev(dh, dw):
        hh = h + dh
        return (w + dw, hh // 2, hh % 2)

    def has(dh, dw):
        ok = None
        for cond in ([h > 0] if dh < 0 else [h < nh - 1] if dh > 0 else []) + ([w > 0] if dw < 0 else [w < nw - 1] if dw > 0 else []):
            ok = cond if ok is None else jnp.logical_and(ok, cond)
        return ok

    def announce(barrier):
        for d in dirs:
            @pl.when(has(*d))
            def _(d=d):
                pl.semaphore_signal(barrier, inc=1, device_id=dev(*d), device_id_type=MESH)
        one = jnp.int32(1)
        zero = jnp.int32(0)
        nv = one + jnp.where(h > 0, one, zero) + jnp.where(h < nh - 1, one, zero)
        nz = one + jnp.where(w > 0, one, zero) + jnp.where(w < nw - 1, one, zero)
        return nv * nz - 1

    def landing(k, dh, dw):
        rows, cl, cr = arrays[k][3:]
        side = cr if dw < 0 else cl
        if dw == 0:
            return rows, 1 if dh < 0 else 0
        if dh == 0:
            return side, slice(1, th + 1)
        return side, th + 1 if dh < 0 else 0

    def copy(k, i, dh, dw):
        u, first, last = arrays[k][:3]
        r = 0 if dh < 0 else th - 1
        edge = first if dw < 0 else last
        src = u.at[r] if dw == 0 else edge if dh == 0 else edge.at[r]
        ref, at = landing(k, dh, dw)
        return pltpu.make_async_remote_copy(src_ref=src, dst_ref=ref.at[at], send_sem=send.at[k * 8 + i], recv_sem=recv.at[k * 8 + i],
                                            device_id=dev(dh, dw), device_id_type=MESH)

    def start():
        for k, i, dh, dw in sends:
            @pl.when(has(dh, dw))
            def _(k=k, i=i, dh=dh, dw=dw):
                copy(k, i, dh, dw).start()

    def finish():
        for k, i, dh, dw in sends:
            @pl.when(jnp.logical_not(has(-dh, -dw)))
            def _(k=k, dh=dh, dw=dw):
                ref, at = landing(k, dh, dw)
                ref[at] = jnp.zeros(ref.at[at].shape, ref.dtype)

            @pl.when(has(dh, dw))
            def _(k=k, i=i, dh=dh, dw=dw):
                copy(k, i, dh, dw).wait_send()

            @pl.when(has(-dh, -dw))
            def _(k=k, i=i, dh=dh, dw=dw):
                copy(k, i, dh, dw).wait_recv()

    return announce, start, finish


def _halo_kernel(nh, nw, n_arr, *refs):
    ins = refs[:3 * n_arr]
    outs = refs[3 * n_arr:6 * n_arr]
    announce, start, finish = _exchange(nh, nw, [ins[3 * k:3 * k + 3] + outs[3 * k:3 * k + 3] for k in range(n_arr)], *refs[6 * n_arr:])
    barrier = pltpu.get_barrier_semaphore()
    pl.semaphore_wait(barrier, announce(barrier))
    start()
    finish()


def _halo(nh, nw, cid, *us):
    th, tw, c = us[0].shape
    n = len(us) // 3
    out = []
    for _ in range(n):
        out += [jax.ShapeDtypeStruct((2, tw, c), BF16), jax.ShapeDtypeStruct((th + 2, 1, c), F32), jax.ShapeDtypeStruct((th + 2, 1, c), F32)]
    res = pl.pallas_call(
        functools.partial(_halo_kernel, nh, nw, n), out_shape=out, in_specs=[ANY] * (3 * n), out_specs=[VM] * (3 * n),
        scratch_shapes=[pltpu.SemaphoreType.DMA((8 * n,)), pltpu.SemaphoreType.DMA((8 * n,))],
        compiler_params=pltpu.CompilerParams(collective_id=cid, has_side_effects=True, vmem_limit_bytes=VMEM_LIMIT),
        name=f"halo{cid}",
    )(*us)
    return [tuple(res[3 * k:3 * k + 3]) for k in range(n)]


def _peers(nh, nw):
    n = nh * nw
    me = lax.axis_index("w") * nh + lax.axis_index("x") * 2 + lax.axis_index("c")

    def dev(j):
        hh = lax.rem(j, nh)
        return (lax.div(j, nh), lax.div(hh, 2), lax.rem(hh, 2))

    return me, [dev(lax.rem(me + k, n)) for k in range(1, n)]


def _meet(peers):
    barrier = pltpu.get_barrier_semaphore()
    for d in peers:
        pl.semaphore_signal(barrier, inc=1, device_id=d, device_id_type=MESH)
    pl.semaphore_wait(barrier, len(peers))


def _sum_devices(me, peers, mine, buf, send, recv):
    copies = [pltpu.make_async_remote_copy(src_ref=mine, dst_ref=buf.at[k], send_sem=send.at[k], recv_sem=recv.at[k],
                                           device_id=d, device_id_type=MESH) for k, d in enumerate(peers)]
    for cp in copies:
        cp.start()
    for cp in copies:
        cp.wait()
    n = len(peers) + 1
    vals = [mine[...]] + [buf[k] for k in range(n - 1)]
    total = 0.0
    for j in range(n):
        off = lax.rem(me - j + n, n)
        total = total + sum(jnp.where(off == k, v, 0.0) for k, v in enumerate(vals))
    return total


def _fill_same(same):
    c = same.shape[0]
    gi, gj = [jnp.floor((lax.broadcasted_iota(jnp.int32, (c, c), d).astype(F32) + 0.5) * (GROUPS / c)) for d in range(2)]
    same[...] = jnp.where(gi == gj, 1.0, 0.0).astype(BF16)


def _group_means(v, same, cnt):
    hi = v.astype(BF16)
    rest = v - hi.astype(F32)
    mid = rest.astype(BF16)
    lo = (rest - mid.astype(F32)).astype(BF16)
    return sum(jnp.dot(x, same[...], preferred_element_type=F32) for x in (lo, mid, hi)) / cnt


def _allsum_kernel(nh, nw, cnt, part_ref, par_ref, out_ref, mine, buf, same, lsem, send, recv):
    me, peers = _peers(nh, nw)
    local = pltpu.make_async_copy(part_ref, mine, lsem)
    local.start()
    _fill_same(same)
    local.wait()
    _meet(peers)
    m = _group_means(_sum_devices(me, peers, mine, buf, send, recv), same, cnt)
    mean = m[0:1]
    row = lax.broadcasted_iota(jnp.int32, m.shape, 0)
    out_ref[...] = jnp.where(row == 0, mean, jnp.where(row == 1, lax.rsqrt(m[1:2] - mean * mean + EPS), par_ref[...]))


def _allsum(nh, nw, cnt, cid, part, par):
    c = part.shape[-1]
    n = nh * nw
    return pl.pallas_call(
        functools.partial(_allsum_kernel, nh, nw, cnt), out_shape=jax.ShapeDtypeStruct((8, c), F32),
        in_specs=[ANY, VM], out_specs=VM,
        scratch_shapes=[pltpu.VMEM((8, c), F32), pltpu.VMEM((n - 1, 8, c), F32), pltpu.VMEM((c, c), BF16), pltpu.SemaphoreType.DMA,
                        pltpu.SemaphoreType.DMA((n - 1,)), pltpu.SemaphoreType.DMA((n - 1,))],
        compiler_params=pltpu.CompilerParams(collective_id=cid, has_side_effects=True, vmem_limit_bytes=VMEM_LIMIT),
        name=f"allsum{cid}",
    )(part, par)


def _load_patches(u_ref, rows_ref, p, sems):
    th, c = u_ref.shape[0], u_ref.shape[2]
    cps = [pltpu.make_async_copy(u_ref, p.at[1:th + 1, :, c:2 * c], sems.at[0]),
           pltpu.make_async_copy(rows_ref.at[0], p.at[0, :, c:2 * c], sems.at[1]),
           pltpu.make_async_copy(rows_ref.at[1], p.at[th + 1, :, c:2 * c], sems.at[2])]
    for cp in cps:
        cp.start()
    return cps


def _shift_patches(p, cl_ref, cr_ref, first=0):
    n, tw, c3 = p.shape
    c = c3 // 3
    ck = 128

    def row(r, _):
        idx = lax.broadcasted_iota(jnp.int32, (tw, ck), 0)
        for k in range(c // ck):
            f = p[r, :, c + k * ck:c + (k + 1) * ck].astype(F32)
            lo = cl_ref[r, :, k * ck:(k + 1) * ck]
            hi = cr_ref[r, :, k * ck:(k + 1) * ck]
            p[r, :, k * ck:(k + 1) * ck] = jnp.where(idx == 0, lo, pltpu.roll(f, 1, 0)).astype(BF16)
            p[r, :, 2 * c + k * ck:2 * c + (k + 1) * ck] = jnp.where(idx == tw - 1, hi, pltpu.roll(f, tw - 1, 0)).astype(BF16)
        return 0

    lax.fori_loop(first, n, row, 0)


def _transposed(v):
    return v.reshape(v.shape[0] * v.shape[1], v.shape[2]).T


def _conv_kernel(rb, epilogue, u_ref, rows_ref, cl_ref, cr_ref, w_ref, v_ref, vt_ref, *refs):
    outs = refs[:-4]
    p, wb, psem, wsem = refs[-4:]
    c = u_ref.shape[2]
    i = pl.program_id(0)

    @pl.when(i == 0)
    def _():
        cps = _load_patches(u_ref, rows_ref, p, psem)
        wc = pltpu.make_async_copy(w_ref, wb, wsem)
        wc.start()
        for cp in cps:
            cp.wait()
        _shift_patches(p, cl_ref, cr_ref)
        wc.wait()

    vt_ref[...] = _transposed(v_ref[...])
    tw = p.shape[1]
    acc = None
    for a in range(3):
        lhs = p[pl.ds(i * rb + a, rb)].reshape(rb * tw, 3 * c)
        d = jnp.dot(lhs, wb[a], preferred_element_type=F32)
        acc = d if acc is None else acc + d
    epilogue(i, acc, (), outs)


def _conv(name, epilogue, u, halo, w, v, outs, out_specs, rb=2):
    th, tw, c = u.shape
    full = _whole(th + 2, 1, c, pipeline_mode=pl.Buffered(1))
    wshape = (3, 3 * c, c)
    return pl.pallas_call(
        functools.partial(_conv_kernel, rb, epilogue),
        grid=(th // rb,), out_shape=[jax.ShapeDtypeStruct((c, th * tw), BF16)] + outs, in_specs=[ANY, ANY, full, full, ANY, out_specs[0]],
        out_specs=[pl.BlockSpec((c, rb * tw), lambda i: (0, i))] + out_specs,
        scratch_shapes=[pltpu.VMEM((th + 2, tw, 3 * c), BF16), pltpu.VMEM(wshape, BF16), pltpu.SemaphoreType.DMA((3,)), pltpu.SemaphoreType.DMA],
        compiler_params=pltpu.CompilerParams(dimension_semantics=("arbitrary",), vmem_limit_bytes=VMEM_LIMIT),
        name=name,
    )(u, *halo, w.reshape(wshape), v)


def _add_sums(i, s0, s1, s_ref):
    row = lax.broadcasted_iota(jnp.int32, s_ref.shape, 0)
    s = jnp.where(row == 0, s0, jnp.where(row == 1, s1, 0.0))

    @pl.when(i == 0)
    def _():
        s_ref[...] = s

    @pl.when(i > 0)
    def _():
        s_ref[...] += s


def _ep_residual(acc, r_ref, o_ref):
    o_ref[...] = (acc + r_ref[...].astype(F32).reshape(acc.shape)).astype(BF16).reshape(o_ref.shape)


def _ep_conv1(i, acc, extra, outs):
    a_ref, s_ref = outs
    a16 = acc.astype(BF16)
    a_ref[...] = a16.reshape(a_ref.shape)
    a = a16.astype(F32)
    s0 = a.sum(0, keepdims=True)
    s1 = (a * a).sum(0, keepdims=True)
    _add_sums(i, s0, s1, s_ref)


def _params(st_ref):
    st = st_ref[...]
    return [st[k:k + 1] for k in range(4)]


def _edges(v, first_ref, last_ref):
    first_ref[...] = v[:, 0:1, :]
    last_ref[...] = v[:, v.shape[1] - 1:, :]


def _z_kernel(a_ref, st_ref, z_ref, first_ref, last_ref):
    mean, rstd, gamma, beta = _params(st_ref)
    xhat = (a_ref[...].astype(F32) - mean) * rstd
    z = _gelu(xhat * gamma + beta).astype(BF16)
    z_ref[...] = z
    _edges(z.astype(F32), first_ref, last_ref)


def _plan(nt, nb):
    starts = [0, nt, nt + nb, nt + 2 * nb, 2 * nt + 2 * nb, 2 * nt + 3 * nb, 2 * nt + 4 * nb]
    late = [*range(2, 9), *range(10, 15, 2), *range(16, 25)]
    return starts, [*range(2, 10), 11, 13, 16, 17, 20, 24, 26] + [starts[3] + s for s in late], 15


def _main_kernel(nh, nw, cnt, z_ref, z0_ref, z1_ref, g_ref, gt_ref, grows, gcl, gcr, x_ref, xrows, xcl, xcr, w1_ref, w2_ref, st_ref, xb_ref, gb_ref, ab_ref,
                 y_ref, dx_ref, t_ref, dn_ref, da_ref, dw_ref,
                 p, vt, wb, dsend, hown, recv0, recv1, recv2, zrows, zcl, zcr, arows, acl, acr, e0, e1, dnb, dab, sacc, sbuf, same,
                 psem, wsem, vsem, send, recv, lsem, zsend, zrecv, asend, arecv, ssend, srecv, dsem):
    i = pl.program_id(0)
    th, tw, c = x_ref.shape
    nt, nb = w1_ref.shape[0], th // 2
    (_, s_z, s_a, s_w, s_x, s_y, _), ticks, second = _plan(nt, nb)
    half, q, e, sub = c // 2, c // 4, c // 8, c // 16
    wi, xi, ci = lax.axis_index("w"), lax.axis_index("x"), lax.axis_index("c")
    mate, xn, yn = (wi, xi, 1 - ci), (wi, 1 - xi, ci), (1 - wi, xi, ci)
    pa, pb = xi * e, q + wi * e
    fa, fb = pa + wi * sub, pb + xi * sub
    me, peers = _peers(nh, nw)

    def slot(t):
        return jnp.where(t < nt, t, t - second)

    def sem_of(t):
        return jnp.where(t < nt, t, t - second + nt)

    def rows(start, n):
        return pl.ds(pl.multiple_of(start, 8), n)

    def rc(stage, t, src, dst, dev):
        return pltpu.make_async_remote_copy(src_ref=src, dst_ref=dst, send_sem=send.at[stage, sem_of(t)], recv_sem=recv.at[stage, sem_of(t)],
                                            device_id=dev, device_id_type=MESH)

    def tap(k):
        return lax.rem(2 * lax.rem(k, 3) + 1, 3), lax.rem(2 * lax.div(k, 3) + 1, 3)

    def base(t):
        a, b = tap(slot(t))
        return (jnp.where(t < nt, 0, nt) + a * 3 + b) * c + ci * half

    def s0(t):
        return [rc(0, t, dsend.at[lax.rem(slot(t), 2)], recv0.at[lax.rem(slot(t), 2)], mate)]

    def s1(t):
        return [rc(1, t, hown.at[slot(t), rows((1 - xi) * e, e)], recv1.at[slot(t), 0], xn),
                rc(2, t, hown.at[slot(t), rows(q + (1 - wi) * e, e)], recv1.at[slot(t), 1], yn)]

    def s2(t):
        return [rc(3, t, hown.at[slot(t), rows(pa + (1 - wi) * sub, sub)], recv2.at[slot(t), 0], yn),
                rc(4, t, hown.at[slot(t), rows(pb + (1 - xi) * sub, sub)], recv2.at[slot(t), 1], xn)]

    def s3(t):
        return [rc(5, t, hown.at[slot(t), rows(fa, sub)], dw_ref.at[rows(base(t) + fa, sub)], yn),
                rc(6, t, hown.at[slot(t), rows(fb, sub)], dw_ref.at[rows(base(t) + fb, sub)], xn)]

    def keep(t):
        return [pltpu.make_async_copy(hown.at[slot(t), rows(fa, sub)], dw_ref.at[rows(base(t) + fa, sub)], lsem.at[0, sem_of(t)]),
                pltpu.make_async_copy(hown.at[slot(t), rows(fb, sub)], dw_ref.at[rows(base(t) + fb, sub)], lsem.at[1, sem_of(t)])]

    def s4(t):
        return [rc(7, t, dw_ref.at[rows(base(t) + pa, e)], dw_ref.at[rows(base(t) + pa, e)], xn),
                rc(8, t, dw_ref.at[rows(base(t) + pb, e)], dw_ref.at[rows(base(t) + pb, e)], yn)]

    def s5(t):
        return [rc(9, t, dw_ref.at[rows(base(t), half)], dw_ref.at[rows(base(t), half)], mate)]

    def start(cps):
        for cp in cps:
            cp.start()

    def when_chunk(t, f):
        one = jnp.logical_and(t >= 0, t < nt)
        two = jnp.logical_and(t >= second, t < second + nt)

        @pl.when(jnp.logical_or(one, two))
        def _():
            f(t)

    def tick(j):
        def t2(t):
            for cp in s1(t):
                cp.wait_recv()
            hown[slot(t), rows(pa, e), :] += recv1[slot(t), 0]
            hown[slot(t), rows(pb, e), :] += recv1[slot(t), 1]

        def t3(t):
            for cp in s2(t):
                cp.wait_recv()
            hown[slot(t), rows(fa, sub), :] += recv2[slot(t), 0]
            hown[slot(t), rows(fb, sub), :] += recv2[slot(t), 1]

        def t4(t):
            for cp in s3(t):
                cp.wait_recv()
            for cp in keep(t):
                cp.wait()
            for cp in s1(t) + s2(t) + s3(t):
                cp.wait_send()
            start(s4(t))

        def t5(t):
            for cp in s4(t):
                cp.wait_recv()
            start(s5(t))

        def t6(t):
            for cp in s5(t):
                cp.wait_recv()
            for cp in s4(t) + s5(t):
                cp.wait_send()

        lag = 2
        when_chunk(j, lambda t: start(s1(t)))
        when_chunk(j - lag, t2)
        when_chunk(j - 2 * lag, t3)
        when_chunk(j - 3 * lag, t4)
        when_chunk(j - 4 * lag, t5)
        when_chunk(j - lag, lambda t: start(s2(t)))
        when_chunk(j - 2 * lag, lambda t: start(s3(t) + keep(t)))
        when_chunk(j - 5 * lag, t6)

    _, z_start, z_finish = _exchange(nh, nw, [(z_ref, z0_ref, z1_ref, zrows, zcl, zcr)], zsend, zrecv)
    _, a_start, a_finish = _exchange(nh, nw, [(da_ref, e0, e1, arows, acl, acr)], asend, arecv)

    def wcp(ref):
        return pltpu.make_async_copy(ref, wb, wsem)

    def middle(src):
        return pltpu.make_async_copy(src, p.at[1:th + 1, :, c:2 * c], psem.at[2])

    def given(ref):
        return [pltpu.make_async_copy(ref.at[k], p.at[k * (th + 1), :, c:2 * c], psem.at[k]) for k in range(2)]

    def put_rows(ref):
        for k in range(2):
            p[k * (th + 1), :, c:2 * c] = ref[k]

    def run(cps):
        start(cps)
        for cp in cps:
            cp.wait()

    def at(step):
        return pl.when(i == step)

    def within(a, b):
        return pl.when(jnp.logical_and(i >= a, i < b))

    @at(0)
    def _():
        cps = [pltpu.make_async_copy(gt_ref, vt, vsem), middle(z_ref)]
        start(cps)
        _meet(peers)
        z_start()
        wcp(w2_ref).start()
        _fill_same(same)
        sacc[...] = jnp.zeros_like(sacc)
        for cp in cps:
            cp.wait()

    @at(1)
    def _():
        z_finish()
        put_rows(zrows)

    @at(3)
    def _():
        _shift_patches(p, zcl, zcr)

    @at(s_z)
    def _():
        run([middle(g_ref)] + given(grows))
        _shift_patches(p, gcl, gcr)
        wcp(w2_ref).wait()

    @at(s_w + 3)
    def _():
        _shift_patches(p, xcl, xcr)

    def dn_out(k):
        return pltpu.make_async_copy(dnb.at[lax.rem(k, 2)], dn_ref.at[pl.ds(2 * k, 2)], dsem.at[0, lax.rem(k, 2)])

    def dn_in(k):
        return pltpu.make_async_copy(dn_ref.at[pl.ds(2 * k, 2)], dnb.at[lax.rem(k, 2)], dsem.at[1, lax.rem(k, 2)])

    def da_out(k):
        return pltpu.make_async_copy(dab.at[lax.rem(k, 2)], da_ref.at[pl.ds(2 * k, 2)], dsem.at[2, lax.rem(k, 2)])

    @at(s_a)
    def _():
        for k in range(2):
            dn_out(nb - 2 + k).wait()
        start([dn_in(0), middle(x_ref), wcp(w1_ref)] + given(xrows))
        total = _sum_devices(me, peers, sacc, sbuf, ssend, srecv)
        u = _group_means(total * _params(st_ref)[2], same, cnt)
        row = lax.broadcasted_iota(jnp.int32, total.shape, 0)
        t_ref[...] = jnp.where(row < 2, total, jnp.where(row == 2, u[0:1], u[1:2]))

    @at(s_w)
    def _():
        for k in range(2):
            da_out(nb - 2 + k).wait()
        a_start()
        for cp in [middle(x_ref)] + given(xrows):
            cp.wait()

    @at(s_x)
    def _():
        start([middle(da_ref)])
        a_finish()
        middle(da_ref).wait()
        put_rows(arows)
        _shift_patches(p, acl, acr)
        wcp(w1_ref).wait()

    @at(s_y)
    def _():
        cps = [middle(z_ref), wcp(w2_ref)]
        start(cps)
        put_rows(zrows)
        for cp in cps:
            cp.wait()
        _shift_patches(p, zcl, zcr)

    later = i >= s_w
    step = jnp.where(later, i - s_w, i)
    chunk0 = jnp.where(later, second, 0)

    @pl.when(jnp.logical_and(step >= 2, step < nt + 2))
    def _():
        k = step - 2
        for cp in s0(chunk0 + k):
            cp.wait()
        hown[k] += recv0[lax.rem(k, 2)]

    @pl.when(jnp.logical_and(step >= 1, step < nt + 1))
    def _():
        start(s0(chunk0 + step - 1))

    j = jnp.int32(-1)
    now = jnp.int32(0)
    for s in ticks:
        j = j + jnp.where(i >= s, 1, 0)
        now = now + jnp.where(i == s, 1, 0)

    @pl.when(now > 0)
    def _():
        tick(j)

    @pl.when(step < nt)
    def _():
        a, b = tap(step)
        rhs = p[pl.ds(a, th), :, pl.ds(pl.multiple_of(b * c, 128), c)].reshape(th * tw, c)
        d = jnp.dot(vt[...], rhs, preferred_element_type=F32).T
        hown[step] = jnp.where(ci == 0, d[:half], d[half:])
        dsend[lax.rem(step, 2)] = jnp.where(ci == 0, d[half:], d[:half])

    def conv(ib, transposed):
        acc = None
        for a in range(3):
            lhs = p[pl.ds(ib * 2 + a, 2)].reshape(2 * tw, 3 * c)
            if transposed:
                k = nt - 1 - 3 * a
                rhs = jnp.concatenate([wb[k], wb[k - 1], wb[k - 2]], axis=1)
                d = lax.dot_general(lhs, rhs, (((1,), (1,)), ((), ())), preferred_element_type=F32)
            else:
                d = jnp.dot(lhs, wb[3 * a:3 * a + 3].reshape(3 * c, c), preferred_element_type=F32)
            acc = d if acc is None else acc + d
        return acc

    @within(s_z, s_a)
    def _():
        k = i - s_z

        @pl.when(k > 1)
        def _():
            dn_out(k - 2).wait()

        acc = conv(k, True)
        mean, rstd, gamma, beta = _params(st_ref)
        xhat = (ab_ref[...].astype(F32).reshape(acc.shape) - mean) * rstd
        dn = acc * _gelu_grad(xhat * gamma + beta)
        dnb[lax.rem(k, 2)] = dn.reshape(2, tw, c)
        dn_out(k).start()
        row = lax.broadcasted_iota(jnp.int32, sacc.shape, 0)
        sacc[...] += jnp.where(row == 0, (dn * xhat).sum(0, keepdims=True), jnp.where(row == 1, dn.sum(0, keepdims=True), 0.0))

    @within(s_a, s_w)
    def _():
        k = i - s_a

        @pl.when(k + 1 < nb)
        def _():
            dn_in(k + 1).start()

        @pl.when(k > 1)
        def _():
            da_out(k - 2).wait()

        dn_in(k).wait()
        mean, rstd, gamma, _ = _params(st_ref)
        _, _, u0, u1 = _params(t_ref)
        xhat = (ab_ref[...].astype(F32) - mean) * rstd
        da = (rstd * (dnb[lax.rem(k, 2)] * gamma - u1 - xhat * u0)).astype(BF16)
        dab[lax.rem(k, 2)] = da
        _edges(da.astype(F32), e0.at[pl.ds(2 * k, 2)], e1.at[pl.ds(2 * k, 2)])
        vt[:, pl.ds(pl.multiple_of(2 * k * tw, 2 * tw), 2 * tw)] = _transposed(da)
        da_out(k).start()

    @within(s_x, s_y)
    def _():
        _ep_residual(conv(i - s_x, True), gb_ref, dx_ref)

    @pl.when(i >= s_y)
    def _():
        _ep_residual(conv(i - s_y, False), xb_ref, y_ref)


def _main(nh, nw, cnt, z, z0, z1, g, gt, gh, x, xh, w1, w2, st, a):
    th, tw, c = x.shape
    nt, nb, half = 9, th // 2, c // 2
    (_, s_z, _, _, s_x, s_y, end), _, _ = _plan(nt, nb)
    full = _whole(th + 2, 1, c, pipeline_mode=pl.Buffered(1))
    one = _whole(8, c)

    def blocks(first, passes=1):
        return pl.BlockSpec((2, tw, c), lambda i: (lax.rem(jnp.minimum(jnp.maximum(i - first, 0), passes * nb - 1), nb), 0, 0))

    dma = pltpu.SemaphoreType.DMA
    img16, img32 = jax.ShapeDtypeStruct((th, tw, c), BF16), jax.ShapeDtypeStruct((th, tw, c), F32)
    side, edge, hrow = pltpu.VMEM((th + 2, 1, c), F32), pltpu.VMEM((th, 1, c), F32), pltpu.VMEM((2, tw, c), BF16)
    n = nh * nw - 1
    return pl.pallas_call(
        functools.partial(_main_kernel, nh, nw, cnt), grid=(end,),
        out_shape=[img16, img16, jax.ShapeDtypeStruct((8, c), F32), img32, img16, jax.ShapeDtypeStruct((2 * nt * c, c), F32)],
        in_specs=[ANY] * 6 + [full, full, ANY, ANY, full, full, ANY, ANY, one, blocks(s_y), blocks(s_x), blocks(s_z, 2)],
        out_specs=[blocks(s_y), blocks(s_x), one, ANY, ANY, ANY],
        scratch_shapes=[pltpu.VMEM((th + 2, tw, 3 * c), BF16), pltpu.VMEM((c, th * tw), BF16), pltpu.VMEM((nt, c, c), BF16),
                        pltpu.VMEM((2, half, c), F32), pltpu.VMEM((nt, half, c), F32), pltpu.VMEM((2, half, c), F32),
                        pltpu.VMEM((nt, 2, c // 8, c), F32), pltpu.VMEM((nt, 2, c // 16, c), F32),
                        hrow, side, side, hrow, side, side, edge, edge, pltpu.VMEM((2, 2, tw, c), F32), pltpu.VMEM((2, 2, tw, c), BF16),
                        pltpu.VMEM((8, c), F32), pltpu.VMEM((n, 8, c), F32), pltpu.VMEM((c, c), BF16),
                        dma((3,)), dma, dma, dma((10, 2 * nt)), dma((10, 2 * nt)), dma((2, 2 * nt)), dma((8,)), dma((8,)), dma((8,)), dma((8,)), dma((n,)), dma((n,)), dma((3, 2))],
        compiler_params=pltpu.CompilerParams(dimension_semantics=("arbitrary",), vmem_limit_bytes=VMEM_LIMIT, collective_id=5, has_side_effects=True),
        name="main",
    )(z, z0, z1, g, gt, *gh, x, *xh, w1.reshape(nt, c, c), w2.reshape(nt, c, c), st, x, g, a)


def _finish_kernel(*refs):
    n = len(refs) // 2
    for src, dst in zip(refs[:n], refs[n:]):
        dst[...] = src[...]


def solution(mesh):
    nh, nw = mesh.shape["h"], mesh.shape["w"]
    mesh3 = Mesh(mesh.devices.reshape(nw, nh // 2, 2), ("w", "x", "c"))
    tile = P(None, ("x", "c"), "w", None)

    def body(x, w1, gamma, beta, w2, g):
        _, th, tw, c = x.shape
        x, g = x[0], g[0]
        cnt = float(th * nh * tw * nw * (c // GROUPS))
        rb = 2
        blk = pl.BlockSpec((rb, tw, c), lambda i: (i, 0, 0))
        small = _whole(8, c)
        img16 = jax.ShapeDtypeStruct((th, tw, c), BF16)
        img32 = jax.ShapeDtypeStruct((th, tw, c), F32)
        sums = jax.ShapeDtypeStruct((8, c), F32)
        par = jnp.concatenate([jnp.zeros((2, c), F32), gamma[None], beta[None], jnp.zeros((4, c), F32)])

        edge = jax.ShapeDtypeStruct((th, 1, c), F32)
        eblk = pl.BlockSpec((rb, 1, c), lambda i: (i, 0, 0))

        def with_edges(u):
            return u, u[:, 0:1, :].astype(F32), u[:, tw - 1:, :].astype(F32)

        xh, gh = _halo(nh, nw, 0, *with_edges(x), *with_edges(g))
        gt, a, s = _conv("conv1", _ep_conv1, x, xh, w1, g, [img16, sums], [blk, small])
        st = _allsum(nh, nw, cnt, 1, s, par)
        z, *ze = pl.pallas_call(_z_kernel, grid=(th // rb,), out_shape=[img16, edge, edge], in_specs=[blk, small], out_specs=[blk, eblk, eblk], name="act")(a, st)
        y, dx, t, _, _, d = _main(nh, nw, cnt, z, *ze, g, gt, gh, x, xh, w1, w2, st, a)
        rows = d.shape[0] // th
        halves = [pl.BlockSpec((rows, c), lambda i, k=k: (i + k, 0)) for k in (th // 2, 0)]
        own = pl.BlockSpec((rows, c), lambda i: (i, 0))
        wout = jax.ShapeDtypeStruct((d.shape[0] // 2, c), F32)
        y, dx, dw1, dw2 = pl.pallas_call(_finish_kernel, grid=(th // rb,), out_shape=[img16, img16, wout, wout], in_specs=[blk, blk] + halves,
                                         out_specs=[blk, blk, own, own], name="finish")(y, dx, d, d)
        return y[None], dx[None], dw1.reshape(w1.shape), dw2.reshape(w2.shape), t[0], t[1]

    return jax.shard_map(body, mesh=mesh3, in_specs=(tile, P(), P(), P(), P(), tile), out_specs=(tile, tile, P(), P(), P(), P()), check_vma=False)
```

time: 446 us -> 403 us (0.904)
  Pallas kernels: 439 us -> 397 us
    pallas_call x6 -> x3, Pallas kernels: 375 us -> 332 us  [the longest x1 291 us: _main(): pl.pallas_call(functools.partial(_main_kernel, nh, nw, cnt), grid=(end,),...]
where the time goes in v7:
time: 403 us
  Pallas kernels  397 us (99%)
    pallas_call x1, Pallas kernels, _main(): pl.pallas_call(functools.partial(_main_kernel, nh, nw, cnt), grid=(end,),...  291 us
    pallas_call x1, Pallas kernels, _conv(): pl.pallas_call(functools.partial(_conv_kernel, rb, epilogue), grid=(th //...  47.7 us
    pallas_call x1, Pallas kernels, body(): pl.pallas_call(_finish_kernel, grid=(th // rb,), out_shape=[img16, img16,...  26.1 us
    pallas_call x1, Pallas kernels, _allsum(): pl.pallas_call(functools.partial(_allsum_kernel, nh, nw, cnt), out_shape=...  14.6 us
    pallas_call x1, Pallas kernels, body(): pl.pallas_call(_z_kernel, grid=(th // rb,), out_shape=[img16, edge, edge]...  9.3 us

profile of v7, /device:TPU:0, one launch (start us, length us, event | category | flops | bytes accessed | tf_op | source)
XLA Modules:
  0.0 402.7 jit_solution(18230680826099791236)
XLA Ops:
  0.6 0.1 pad.3.clone
  0.7 0.7 broadcast_in_dim.19
  1.4 0.7 broadcast_in_dim.20
  2.1 0.7 maximum_maximum_fusion.par_ref
  2.8 1.9 slice_convert_fusion
  4.7 7.8 %halo0.1 = (bf16[2,256,640]{2,1,0:T(8,128)(2,1)}, f32[18,1,640]{2,1,0:T(1,128)}, f32[18,1,640]{2,1,0:T(1,128)}, bf16[2,256,640]{2,1,0:T(8,128)(2,1)}, f32[18,1,640]{2,1,0:T(1,128)}, /*index=5*/f32[18,1,640]{2,1,0:T(1,128)}) custom-call(bf16[16,256,640]{2,1,0:T(8,128)(2,1)} %bitcast.10, f32[16,1,640]{2,1,0:T(1,128)} %get-tuple-element.52.refs_1_, ...), custom_call_target="tpu_custom_call" | custom-call | tf_op jit(solution)/shard_map/halo0/pallas_call | solution.py:129
  12.5 47.7 %conv1.1 = (bf16[640,4096]{1,0:T(8,128)(2,1)}, bf16[16,256,640]{2,1,0:T(8,128)(2,1)}, f32[8,640]{1,0:T(8,128)}) custom-call(bf16[16,256,640]{2,1,0:T(8,128)(2,1)} %bitcast.11, bf16[2,256,640]{2,1,0:T(8,128)(2,1)} %get-tuple-element.26.rows_ref.xrows, f32[18,1,640]{2,1,0:T(1,128)} %get-tuple-element.27.cl_ref.xcl, ...), custom_call_target="tpu_custom_call" | custom-call | tf_op jit(solution)/shard_map/conv1/pallas_call | solution.py:274
  60.2 14.6 %allsum1.1.st_ref = f32[8,640]{1,0:T(8,128)} custom-call(f32[8,640]{1,0:T(8,128)} %get-tuple-element.30.part_ref, f32[8,640]{1,0:T(8,128)} %maximum_maximum_fusion.par_ref), custom_call_target="tpu_custom_call" | custom-call | tf_op jit(solution)/shard_map/allsum1/pallas_call | solution.py:202
  74.9 9.3 %act.1 = (bf16[16,256,640]{2,1,0:T(8,128)(2,1)}, f32[16,1,640]{2,1,0:T(1,128)}, f32[16,1,640]{2,1,0:T(1,128)}) custom-call(bf16[16,256,640]{2,1,0:T(8,128)(2,1)} %get-tuple-element.29.a_ref.ab_ref, f32[8,640]{1,0:T(8,128)} %allsum1.1.st_ref), custom_call_target="tpu_custom_call" | custom-call | tf_op jit(solution)/shard_map/act/pallas_call | solution.py:710
  84.2 291.0 %main.1 = (bf16[16,256,640]{2,1,0:T(8,128)(2,1)}, bf16[16,256,640]{2,1,0:T(8,128)(2,1)}, f32[8,640]{1,0:T(8,128)}, f32[16,256,640]{2,1,0:T(8,128)}, bf16[16,256,640]{2,1,0:T(8,128)(2,1)}, /*index=5*/f32[11520,640]{1,0:T(8,128)}) custom-call(bf16[16,256,640]{2,1,0:T(8,128)(2,1)} %get-tuple-element.31.z_ref, f32[16,1,640]{2,1,0:T(1,128)} %get-tuple-element.32.z0_ref, ...), custom_call_target="tpu_custom_call" | custom-call | tf_op jit(solution)/shard_map/main/pallas_call | solution.py:662
  375.2 26.1 %finish.1 = (bf16[16,256,640]{2,1,0:T(8,128)(2,1)}, bf16[16,256,640]{2,1,0:T(8,128)(2,1)}, f32[5760,640]{1,0:T(8,128)}, f32[5760,640]{1,0:T(8,128)}) custom-call(bf16[16,256,640]{2,1,0:T(8,128)(2,1)} %get-tuple-element.38.refs_0_, bf16[16,256,640]{2,1,0:T(8,128)(2,1)} %get-tuple-element.39.refs_1_, f32[11520,640]{1,0:T(8,128)} %get-tuple-element.40.refs_2_.refs_3_, ...), custom_call_target="tpu_custom_call" | custom-call | tf_op jit(solution)/shard_map/finish/pallas_call | solution.py:716
  401.3 1.4 slice_reduce_fusion
  (3 shorter events, 0.0 us)

commit v8 on v7

--- a/solution.py
+++ b/solution.py
@@ -57,17 +57,6 @@
             ok = cond if ok is None else jnp.logical_and(ok, cond)
         return ok
 
-    def announce(barrier):
-        for d in dirs:
-            @pl.when(has(*d))
-            def _(d=d):
-                pl.semaphore_signal(barrier, inc=1, device_id=dev(*d), device_id_type=MESH)
-        one = jnp.int32(1)
-        zero = jnp.int32(0)
-        nv = one + jnp.where(h > 0, one, zero) + jnp.where(h < nh - 1, one, zero)
-        nz = one + jnp.where(w > 0, one, zero) + jnp.where(w < nw - 1, one, zero)
-        return nv * nz - 1
-
     def landing(k, dh, dw):
         rows, cl, cr = arrays[k][3:]
         side = cr if dw < 0 else cl
@@ -107,32 +96,7 @@
             def _(k=k, i=i, dh=dh, dw=dw):
                 copy(k, i, dh, dw).wait_recv()
 
-    return announce, start, finish
-
-
-def _halo_kernel(nh, nw, n_arr, *refs):
-    ins = refs[:3 * n_arr]
-    outs = refs[3 * n_arr:6 * n_arr]
-    announce, start, finish = _exchange(nh, nw, [ins[3 * k:3 * k + 3] + outs[3 * k:3 * k + 3] for k in range(n_arr)], *refs[6 * n_arr:])
-    barrier = pltpu.get_barrier_semaphore()
-    pl.semaphore_wait(barrier, announce(barrier))
-    start()
-    finish()
-
-
-def _halo(nh, nw, cid, *us):
-    th, tw, c = us[0].shape
-    n = len(us) // 3
-    out = []
-    for _ in range(n):
-        out += [jax.ShapeDtypeStruct((2, tw, c), BF16), jax.ShapeDtypeStruct((th + 2, 1, c), F32), jax.ShapeDtypeStruct((th + 2, 1, c), F32)]
-    res = pl.pallas_call(
-        functools.partial(_halo_kernel, nh, nw, n), out_shape=out, in_specs=[ANY] * (3 * n), out_specs=[VM] * (3 * n),
-        scratch_shapes=[pltpu.SemaphoreType.DMA((8 * n,)), pltpu.SemaphoreType.DMA((8 * n,))],
-        compiler_params=pltpu.CompilerParams(collective_id=cid, has_side_effects=True, vmem_limit_bytes=VMEM_LIMIT),
-        name=f"halo{cid}",
-    )(*us)
-    return [tuple(res[3 * k:3 * k + 3]) for k in range(n)]
+    return start, finish
 
 
 def _peers(nh, nw):
@@ -183,43 +147,7 @@
     return sum(jnp.dot(x, same[...], preferred_element_type=F32) for x in (lo, mid, hi)) / cnt
 
 
-def _allsum_kernel(nh, nw, cnt, part_ref, par_ref, out_ref, mine, buf, same, lsem, send, recv):
-    me, peers = _peers(nh, nw)
-    local = pltpu.make_async_copy(part_ref, mine, lsem)
-    local.start()
-    _fill_same(same)
-    local.wait()
-    _meet(peers)
-    m = _group_means(_sum_devices(me, peers, mine, buf, send, recv), same, cnt)
-    mean = m[0:1]
-    row = lax.broadcasted_iota(jnp.int32, m.shape, 0)
-    out_ref[...] = jnp.where(row == 0, mean, jnp.where(row == 1, lax.rsqrt(m[1:2] - mean * mean + EPS), par_ref[...]))
-
-
-def _allsum(nh, nw, cnt, cid, part, par):
-    c = part.shape[-1]
-    n = nh * nw
-    return pl.pallas_call(
-        functools.partial(_allsum_kernel, nh, nw, cnt), out_shape=jax.ShapeDtypeStruct((8, c), F32),
-        in_specs=[ANY, VM], out_specs=VM,
-        scratch_shapes=[pltpu.VMEM((8, c), F32), pltpu.VMEM((n - 1, 8, c), F32), pltpu.VMEM((c, c), BF16), pltpu.SemaphoreType.DMA,
-                        pltpu.SemaphoreType.DMA((n - 1,)), pltpu.SemaphoreType.DMA((n - 1,))],
-        compiler_params=pltpu.CompilerParams(collective_id=cid, has_side_effects=True, vmem_limit_bytes=VMEM_LIMIT),
-        name=f"allsum{cid}",
-    )(part, par)
-
-
-def _load_patches(u_ref, rows_ref, p, sems):
-    th, c = u_ref.shape[0], u_ref.shape[2]
-    cps = [pltpu.make_async_copy(u_ref, p.at[1:th + 1, :, c:2 * c], sems.at[0]),
-           pltpu.make_async_copy(rows_ref.at[0], p.at[0, :, c:2 * c], sems.at[1]),
-           pltpu.make_async_copy(rows_ref.at[1], p.at[th + 1, :, c:2 * c], sems.at[2])]
-    for cp in cps:
-        cp.start()
-    return cps
-
-
-def _shift_patches(p, cl_ref, cr_ref, first=0):
+def _shift_patches(p, cl_ref, cr_ref, r0=0):
     n, tw, c3 = p.shape
     c = c3 // 3
     ck = 128
@@ -228,84 +156,95 @@
         idx = lax.broadcasted_iota(jnp.int32, (tw, ck), 0)
         for k in range(c // ck):
             f = p[r, :, c + k * ck:c + (k + 1) * ck].astype(F32)
-            lo = cl_ref[r, :, k * ck:(k + 1) * ck]
-            hi = cr_ref[r, :, k * ck:(k + 1) * ck]
+            lo = cl_ref[r0 + r, :, k * ck:(k + 1) * ck]
+            hi = cr_ref[r0 + r, :, k * ck:(k + 1) * ck]
             p[r, :, k * ck:(k + 1) * ck] = jnp.where(idx == 0, lo, pltpu.roll(f, 1, 0)).astype(BF16)
             p[r, :, 2 * c + k * ck:2 * c + (k + 1) * ck] = jnp.where(idx == tw - 1, hi, pltpu.roll(f, tw - 1, 0)).astype(BF16)
         return 0
 
-    lax.fori_loop(first, n, row, 0)
+    lax.fori_loop(0, n, row, 0)
 
 
 def _transposed(v):
     return v.reshape(v.shape[0] * v.shape[1], v.shape[2]).T
 
 
-def _conv_kernel(rb, epilogue, u_ref, rows_ref, cl_ref, cr_ref, w_ref, v_ref, vt_ref, *refs):
-    outs = refs[:-4]
-    p, wb, psem, wsem = refs[-4:]
-    c = u_ref.shape[2]
+def _put_rows(p, ref):
+    th, c = p.shape[0] - 2, ref.shape[2]
+    for k in range(2):
+        p[k * (th + 1), :, c:2 * c] = ref[k]
+
+
+def _conv_kernel(nh, nw, cnt, x_ref, x0_ref, x1_ref, g_ref, g0_ref, g1_ref, w_ref, par_ref, gb_ref, gt_ref, a_ref, st_ref, *refs):
+    handed, (p, wb, *halo), (sacc, sbuf, same, psem, wsem, hsend, hrecv, ssend, srecv) = refs[:6], refs[6:14], refs[14:]
     i = pl.program_id(0)
+    th, tw, c = x_ref.shape
+    me, peers = _peers(nh, nw)
+    last = th // 2
 
     @pl.when(i == 0)
     def _():
-        cps = _load_patches(u_ref, rows_ref, p, psem)
+        xc = pltpu.make_async_copy(x_ref, p.at[1:th + 1, :, c:2 * c], psem)
         wc = pltpu.make_async_copy(w_ref, wb, wsem)
+        xc.start()
         wc.start()
-        for cp in cps:
-            cp.wait()
-        _shift_patches(p, cl_ref, cr_ref)
+        start, finish = _exchange(nh, nw, [(x_ref, x0_ref, x1_ref, *halo[:3]), (g_ref, g0_ref, g1_ref, *halo[3:])], hsend, hrecv)
+        _meet(peers)
+        start()
+        _fill_same(same)
+        sacc[...] = jnp.zeros_like(sacc)
+        finish()
+        for dst, src in zip(handed, halo):
+            dst[...] = src[...]
+        xc.wait()
+        _put_rows(p, halo[0])
+        _shift_patches(p, halo[1], halo[2])
         wc.wait()
 
-    vt_ref[...] = _transposed(v_ref[...])
-    tw = p.shape[1]
-    acc = None
-    for a in range(3):
-        lhs = p[pl.ds(i * rb + a, rb)].reshape(rb * tw, 3 * c)
-        d = jnp.dot(lhs, wb[a], preferred_element_type=F32)
-        acc = d if acc is None else acc + d
-    epilogue(i, acc, (), outs)
-
-
-def _conv(name, epilogue, u, halo, w, v, outs, out_specs, rb=2):
-    th, tw, c = u.shape
-    full = _whole(th + 2, 1, c, pipeline_mode=pl.Buffered(1))
+    @pl.when(i < last)
+    def _():
+        gt_ref[...] = _transposed(gb_ref[...])
+        acc = None
+        for a in range(3):
+            d = jnp.dot(p[pl.ds(i * 2 + a, 2)].reshape(2 * tw, 3 * c), wb[a], preferred_element_type=F32)
+            acc = d if acc is None else acc + d
+        a16 = acc.astype(BF16)
+        a_ref[...] = a16.reshape(a_ref.shape)
+        v = a16.astype(F32)
+        row = lax.broadcasted_iota(jnp.int32, sacc.shape, 0)
+        sacc[...] += jnp.where(row == 0, v.sum(0, keepdims=True), jnp.where(row == 1, (v * v).sum(0, keepdims=True), 0.0))
+
+    @pl.when(i == last)
+    def _():
+        m = _group_means(_sum_devices(me, peers, sacc, sbuf, ssend, srecv), same, cnt)
+        mean = m[0:1]
+        row = lax.broadcasted_iota(jnp.int32, m.shape, 0)
+        st_ref[...] = jnp.where(row == 0, mean, jnp.where(row == 1, lax.rsqrt(m[1:2] - mean * mean + EPS), par_ref[...]))
+
+
+def _conv(nh, nw, cnt, x, xe, g, ge, w, par):
+    th, tw, c = x.shape
+    n, last = nh * nw - 1, th // 2 - 1
     wshape = (3, 3 * c, c)
+    one = _whole(8, c)
+    dma = pltpu.SemaphoreType.DMA
+    halo = [(2, tw, c), (th + 2, 1, c), (th + 2, 1, c)] * 2
+    types = [BF16, F32, F32] * 2
+    blk = pl.BlockSpec((2, tw, c), lambda i: (jnp.minimum(i, last), 0, 0))
     return pl.pallas_call(
-        functools.partial(_conv_kernel, rb, epilogue),
-        grid=(th // rb,), out_shape=[jax.ShapeDtypeStruct((c, th * tw), BF16)] + outs, in_specs=[ANY, ANY, full, full, ANY, out_specs[0]],
-        out_specs=[pl.BlockSpec((c, rb * tw), lambda i: (0, i))] + out_specs,
-        scratch_shapes=[pltpu.VMEM((th + 2, tw, 3 * c), BF16), pltpu.VMEM(wshape, BF16), pltpu.SemaphoreType.DMA((3,)), pltpu.SemaphoreType.DMA],
-        compiler_params=pltpu.CompilerParams(dimension_semantics=("arbitrary",), vmem_limit_bytes=VMEM_LIMIT),
-        name=name,
-    )(u, *halo, w.reshape(wshape), v)
-
-
-def _add_sums(i, s0, s1, s_ref):
-    row = lax.broadcasted_iota(jnp.int32, s_ref.shape, 0)
-    s = jnp.where(row == 0, s0, jnp.where(row == 1, s1, 0.0))
-
-    @pl.when(i == 0)
-    def _():
-        s_ref[...] = s
-
-    @pl.when(i > 0)
-    def _():
-        s_ref[...] += s
+        functools.partial(_conv_kernel, nh, nw, cnt), grid=(th // 2 + 1,),
+        out_shape=[jax.ShapeDtypeStruct((c, th * tw), BF16), jax.ShapeDtypeStruct((th, tw, c), BF16), jax.ShapeDtypeStruct((8, c), F32)]
+        + [jax.ShapeDtypeStruct(h, t) for h, t in zip(halo, types)],
+        in_specs=[ANY] * 7 + [one, blk], out_specs=[pl.BlockSpec((c, 2 * tw), lambda i: (0, jnp.minimum(i, last))), blk, one] + [_whole(*h) for h in halo],
+        scratch_shapes=[pltpu.VMEM((th + 2, tw, 3 * c), BF16), pltpu.VMEM(wshape, BF16)] + [pltpu.VMEM(h, t) for h, t in zip(halo, types)]
+        + [pltpu.VMEM((8, c), F32), pltpu.VMEM((n, 8, c), F32), pltpu.VMEM((c, c), BF16), dma, dma, dma((16,)), dma((16,)), dma((n,)), dma((n,))],
+        compiler_params=pltpu.CompilerParams(dimension_semantics=("arbitrary",), vmem_limit_bytes=VMEM_LIMIT, collective_id=1, has_side_effects=True),
+        name="conv1",
+    )(x, *xe, g, *ge, w.reshape(wshape), par, g)
 
 
 def _ep_residual(acc, r_ref, o_ref):
     o_ref[...] = (acc + r_ref[...].astype(F32).reshape(acc.shape)).astype(BF16).reshape(o_ref.shape)
-
-
-def _ep_conv1(i, acc, extra, outs):
-    a_ref, s_ref = outs
-    a16 = acc.astype(BF16)
-    a_ref[...] = a16.reshape(a_ref.shape)
-    a = a16.astype(F32)
-    s0 = a.sum(0, keepdims=True)
-    s1 = (a * a).sum(0, keepdims=True)
-    _add_sums(i, s0, s1, s_ref)
 
 
 def _params(st_ref):
@@ -327,13 +266,15 @@
 
 
 def _plan(nt, nb):
-    starts = [0, nt, nt + nb, nt + 2 * nb, 2 * nt + 2 * nb, 2 * nt + 3 * nb, 2 * nt + 4 * nb]
+    starts = [0]
+    for n in (nt, nb, nb, nt, nb, nb):
+        starts.append(starts[-1] + n)
     late = [*range(2, 9), *range(10, 15, 2), *range(16, 25)]
     return starts, [*range(2, 10), 11, 13, 16, 17, 20, 24, 26] + [starts[3] + s for s in late], 15
 
 
 def _main_kernel(nh, nw, cnt, z_ref, z0_ref, z1_ref, g_ref, gt_ref, grows, gcl, gcr, x_ref, xrows, xcl, xcr, w1_ref, w2_ref, st_ref, xb_ref, gb_ref, ab_ref,
-                 y_ref, dx_ref, t_ref, dn_ref, da_ref, dw_ref,
+                 y_ref, dx_ref, t_ref, dn_ref, da_ref, dw_ref, hrows, hcl, hcr,
                  p, vt, wb, dsend, hown, recv0, recv1, recv2, zrows, zcl, zcr, arows, acl, acr, e0, e1, dnb, dab, sacc, sbuf, same,
                  psem, wsem, vsem, send, recv, lsem, zsend, zrecv, asend, arecv, ssend, srecv, dsem):
     i = pl.program_id(0)
@@ -448,8 +389,8 @@
         when_chunk(j - 2 * lag, lambda t: start(s3(t) + keep(t)))
         when_chunk(j - 5 * lag, t6)
 
-    _, z_start, z_finish = _exchange(nh, nw, [(z_ref, z0_ref, z1_ref, zrows, zcl, zcr)], zsend, zrecv)
-    _, a_start, a_finish = _exchange(nh, nw, [(da_ref, e0, e1, arows, acl, acr)], asend, arecv)
+    z_start, z_finish = _exchange(nh, nw, [(z_ref, z0_ref, z1_ref, zrows, zcl, zcr)], zsend, zrecv)
+    a_start, a_finish = _exchange(nh, nw, [(da_ref, e0, e1, arows, acl, acr)], asend, arecv)
 
     def wcp(ref):
         return pltpu.make_async_copy(ref, wb, wsem)
@@ -459,10 +400,6 @@
 
     def given(ref):
         return [pltpu.make_async_copy(ref.at[k], p.at[k * (th + 1), :, c:2 * c], psem.at[k]) for k in range(2)]
-
-    def put_rows(ref):
-        for k in range(2):
-            p[k * (th + 1), :, c:2 * c] = ref[k]
 
     def run(cps):
         start(cps)
@@ -490,10 +427,11 @@
     @at(1)
     def _():
         z_finish()
-        put_rows(zrows)
+        _put_rows(p, zrows)
 
     @at(3)
     def _():
+        run([pltpu.make_async_copy(src, dst, psem.at[k]) for k, (src, dst) in enumerate(zip((zrows, zcl, zcr), (hrows, hcl, hcr)))])
         _shift_patches(p, zcl, zcr)
 
     @at(s_z)
@@ -538,7 +476,7 @@
         start([middle(da_ref)])
         a_finish()
         middle(da_ref).wait()
-        put_rows(arows)
+        _put_rows(p, arows)
         _shift_patches(p, acl, acr)
         wcp(w1_ref).wait()
 
@@ -546,7 +484,7 @@
     def _():
         cps = [middle(z_ref), wcp(w2_ref)]
         start(cps)
-        put_rows(zrows)
+        _put_rows(p, zrows)
         for cp in cps:
             cp.wait()
         _shift_patches(p, zcl, zcr)
@@ -640,7 +578,7 @@
     def _():
         _ep_residual(conv(i - s_x, True), gb_ref, dx_ref)
 
-    @pl.when(i >= s_y)
+    @within(s_y, s_y + nb // 2)
     def _():
         _ep_residual(conv(i - s_y, False), xb_ref, y_ref)
 
@@ -652,8 +590,8 @@
     full = _whole(th + 2, 1, c, pipeline_mode=pl.Buffered(1))
     one = _whole(8, c)
 
-    def blocks(first, passes=1):
-        return pl.BlockSpec((2, tw, c), lambda i: (lax.rem(jnp.minimum(jnp.maximum(i - first, 0), passes * nb - 1), nb), 0, 0))
+    def blocks(first, count=nb):
+        return pl.BlockSpec((2, tw, c), lambda i: (lax.rem(jnp.minimum(jnp.maximum(i - first, 0), count - 1), nb), 0, 0))
 
     dma = pltpu.SemaphoreType.DMA
     img16, img32 = jax.ShapeDtypeStruct((th, tw, c), BF16), jax.ShapeDtypeStruct((th, tw, c), F32)
@@ -661,9 +599,10 @@
     n = nh * nw - 1
     return pl.pallas_call(
         functools.partial(_main_kernel, nh, nw, cnt), grid=(end,),
-        out_shape=[img16, img16, jax.ShapeDtypeStruct((8, c), F32), img32, img16, jax.ShapeDtypeStruct((2 * nt * c, c), F32)],
-        in_specs=[ANY] * 6 + [full, full, ANY, ANY, full, full, ANY, ANY, one, blocks(s_y), blocks(s_x), blocks(s_z, 2)],
-        out_specs=[blocks(s_y), blocks(s_x), one, ANY, ANY, ANY],
+        out_shape=[jax.ShapeDtypeStruct((nb, tw, c), BF16), img16, jax.ShapeDtypeStruct((8, c), F32), img32, img16, jax.ShapeDtypeStruct((2 * nt * c, c), F32)]
+        + [jax.ShapeDtypeStruct(h.shape, h.dtype) for h in gh],
+        in_specs=[ANY] * 6 + [full, full, ANY, ANY, full, full, ANY, ANY, one, blocks(s_y, nb // 2), blocks(s_x), blocks(s_z, 2 * nb)],
+        out_specs=[blocks(s_y, nb // 2), blocks(s_x), one] + [ANY] * 6,
         scratch_shapes=[pltpu.VMEM((th + 2, tw, 3 * c), BF16), pltpu.VMEM((c, th * tw), BF16), pltpu.VMEM((nt, c, c), BF16),
                         pltpu.VMEM((2, half, c), F32), pltpu.VMEM((nt, half, c), F32), pltpu.VMEM((2, half, c), F32),
                         pltpu.VMEM((nt, 2, c // 8, c), F32), pltpu.VMEM((nt, 2, c // 16, c), F32),
@@ -675,10 +614,74 @@
     )(z, z0, z1, g, gt, *gh, x, *xh, w1.reshape(nt, c, c), w2.reshape(nt, c, c), st, x, g, a)
 
 
-def _finish_kernel(*refs):
-    n = len(refs) // 2
-    for src, dst in zip(refs[:n], refs[n:]):
+def _finish_kernel(z_ref, rows_ref, cl_ref, cr_ref, w_ref, xb_ref, y0_ref, dx0_ref, d1_ref, d2_ref, y_ref, dx_ref, dw1_ref, dw2_ref,
+                   p, wb, yb, psem, wsem, ysem, csem):
+    i = pl.program_id(0)
+    steps = pl.num_programs(0)
+    th, tw, c = z_ref.shape
+    r0 = th // 2
+    n = th - r0 + 1
+
+    def yout(k):
+        return pltpu.make_async_copy(yb.at[lax.rem(k, 2)], y_ref.at[r0 + k], ysem.at[lax.rem(k, 2)])
+
+    ycopy = pltpu.make_async_copy(y0_ref.at[0], y_ref.at[i], csem)
+    ycopy.start()
+
+    @pl.when(i == 0)
+    def _():
+        cps = [pltpu.make_async_copy(z_ref.at[r0 - 1:], p.at[:n, :, c:2 * c], psem.at[0]),
+               pltpu.make_async_copy(rows_ref.at[1], p.at[n, :, c:2 * c], psem.at[1])]
+        wc = pltpu.make_async_copy(w_ref, wb, wsem)
+        for cp in cps + [wc]:
+            cp.start()
+        for cp in cps:
+            cp.wait()
+        _shift_patches(p, cl_ref, cr_ref, r0)
+        wc.wait()
+
+    @pl.when(i > 1)
+    def _():
+        yout(i - 2).wait()
+
+    for src, dst in ((dx0_ref, dx_ref), (d1_ref, dw1_ref), (d2_ref, dw2_ref)):
         dst[...] = src[...]
+    acc = None
+    for a in range(3):
+        d = jnp.dot(p[i + a], wb[a], preferred_element_type=F32)
+        acc = d if acc is None else acc + d
+    yb[lax.rem(i, 2)] = (acc + xb_ref[0].astype(F32)).astype(BF16)
+    yout(i).start()
+    ycopy.wait()
+
+    @pl.when(i == steps - 1)
+    def _():
+        yout(i - 1).wait()
+        yout(i).wait()
+
+
+def _finish(z, zh, w, x, y0, dx0, d):
+    th, tw, c = x.shape
+    steps = th // 2
+    rows = d.shape[0] // th
+    wshape = (3, 3 * c, c)
+    dma = pltpu.SemaphoreType.DMA
+    full = _whole(th + 2, 1, c)
+
+    def part(k):
+        return pl.BlockSpec((rows, c), lambda i: (i + k, 0))
+
+    def img(n, k=0):
+        return pl.BlockSpec((n, tw, c), lambda i: (i + k, 0, 0))
+
+    wout = jax.ShapeDtypeStruct((d.shape[0] // 2, c), F32)
+    iout = jax.ShapeDtypeStruct((th, tw, c), BF16)
+    return pl.pallas_call(
+        _finish_kernel, grid=(steps,), out_shape=[iout, iout, wout, wout],
+        in_specs=[ANY, ANY, full, full, ANY, img(1, steps), img(1), img(2), part(steps), part(0)], out_specs=[ANY, img(2), part(0), part(0)],
+        scratch_shapes=[pltpu.VMEM((steps + 2, tw, 3 * c), BF16), pltpu.VMEM(wshape, BF16), pltpu.VMEM((2, tw, c), BF16), dma((2,)), dma, dma((2,)), dma],
+        compiler_params=pltpu.CompilerParams(dimension_semantics=("arbitrary",), vmem_limit_bytes=VMEM_LIMIT), name="finish",
+    )(z, *zh, w.reshape(wshape), x, y0, dx0, d, d)
 
 
 def solution(mesh):
@@ -694,27 +697,19 @@
         blk = pl.BlockSpec((rb, tw, c), lambda i: (i, 0, 0))
         small = _whole(8, c)
         img16 = jax.ShapeDtypeStruct((th, tw, c), BF16)
-        img32 = jax.ShapeDtypeStruct((th, tw, c), F32)
-        sums = jax.ShapeDtypeStruct((8, c), F32)
         par = jnp.concatenate([jnp.zeros((2, c), F32), gamma[None], beta[None], jnp.zeros((4, c), F32)])
 
         edge = jax.ShapeDtypeStruct((th, 1, c), F32)
         eblk = pl.BlockSpec((rb, 1, c), lambda i: (i, 0, 0))
 
-        def with_edges(u):
-            return u, u[:, 0:1, :].astype(F32), u[:, tw - 1:, :].astype(F32)
-
-        xh, gh = _halo(nh, nw, 0, *with_edges(x), *with_edges(g))
-        gt, a, s = _conv("conv1", _ep_conv1, x, xh, w1, g, [img16, sums], [blk, small])
-        st = _allsum(nh, nw, cnt, 1, s, par)
+        def edges(u):
+            return u[:, 0:1, :].astype(F32), u[:, tw - 1:, :].astype(F32)
+
+        gt, a, st, *halos = _conv(nh, nw, cnt, x, edges(x), g, edges(g), w1, par)
+        xh, gh = halos[:3], halos[3:]
         z, *ze = pl.pallas_call(_z_kernel, grid=(th // rb,), out_shape=[img16, edge, edge], in_specs=[blk, small], out_specs=[blk, eblk, eblk], name="act")(a, st)
-        y, dx, t, _, _, d = _main(nh, nw, cnt, z, *ze, g, gt, gh, x, xh, w1, w2, st, a)
-        rows = d.shape[0] // th
-        halves = [pl.BlockSpec((rows, c), lambda i, k=k: (i + k, 0)) for k in (th // 2, 0)]
-        own = pl.BlockSpec((rows, c), lambda i: (i, 0))
-        wout = jax.ShapeDtypeStruct((d.shape[0] // 2, c), F32)
-        y, dx, dw1, dw2 = pl.pallas_call(_finish_kernel, grid=(th // rb,), out_shape=[img16, img16, wout, wout], in_specs=[blk, blk] + halves,
-                                         out_specs=[blk, blk, own, own], name="finish")(y, dx, d, d)
+        y, dx, t, _, _, d, *zh = _main(nh, nw, cnt, z, *ze, g, gt, gh, x, xh, w1, w2, st, a)
+        y, dx, dw1, dw2 = _finish(z, zh, w2, x, y, dx, d)
         return y[None], dx[None], dw1.reshape(w1.shape), dw2.reshape(w2.shape), t[0], t[1]
 
     return jax.shard_map(body, mesh=mesh3, in_specs=(tile, P(), P(), P(), P(), tile), out_specs=(tile, tile, P(), P(), P(), P()), check_vma=False)

time: 403 us -> 396 us (0.983)
  Pallas kernels: 397 us -> 389 us
    pallas_call x1, Pallas kernels: 291 us -> 275 us  [_main(): pl.pallas_call(functools.partial(_main_kernel, nh, nw, cnt), grid=(end,),...]
    pallas_call x4 -> x2, Pallas kernels: 96.3 us -> 105 us  [the longest x1 64.6 us: _conv(): pl.pallas_call(functools.partial(_conv_kernel, nh, nw, cnt), grid=(th //...]
where the time goes in v8:
time: 396 us; the launch traced here: 395 us
  Pallas kernels  389 us (98%)
    pallas_call x1, Pallas kernels, _main(): pl.pallas_call(functools.partial(_main_kernel, nh, nw, cnt), grid=(end,),...  275 us
    pallas_call x1, Pallas kernels, _conv(): pl.pallas_call(functools.partial(_conv_kernel, nh, nw, cnt), grid=(th //...  64.6 us
    pallas_call x1, Pallas kernels, _finish(): pl.pallas_call(_finish_kernel, grid=(steps,), out_shape=[iout, iout, wout...  40.1 us
    pallas_call x1, Pallas kernels, body(): pl.pallas_call(_z_kernel, grid=(th // rb,), out_shape=[img16, edge, edge]...  9.29 us

profile of v8, /device:TPU:0, one launch (start us, length us, event | category | flops | bytes accessed | tf_op | source)
XLA Modules:
  0.0 395.0 jit_solution(17037517664293469048)
XLA Ops:
  0.6 0.1 pad.3.clone
  0.7 0.7 broadcast_in_dim.19
  1.4 0.7 broadcast_in_dim.20
  2.1 0.7 maximum_maximum_fusion.par_ref
  2.8 1.9 slice_convert_fusion
  4.7 64.6 %conv1.1 = (bf16[640,4096]{1,0:T(8,128)(2,1)}, bf16[16,256,640]{2,1,0:T(8,128)(2,1)}, f32[8,640]{1,0:T(8,128)}, bf16[2,256,640]{2,1,0:T(8,128)(2,1)}, f32[18,1,6...) custom-call(bf16[16,256,640]{2,1,0:T(8,128)(2,1)} %bitcast.11, ...), custom_call_target="tpu_custom_call" | custom-call | tf_op jit(solution)/shard_map/conv1/pallas_call | solution.py:234
  69.3 9.3 %act.1 = (bf16[16,256,640]{2,1,0:T(8,128)(2,1)}, f32[16,1,640]{2,1,0:T(1,128)}, f32[16,1,640]{2,1,0:T(1,128)}) custom-call(bf16[16,256,640]{2,1,0:T(8,128)(2,1)} %get-tuple-element.29.a_ref.ab_ref, f32[8,640]{1,0:T(8,128)} %get-tuple-element.30.st_ref), custom_call_target="tpu_custom_call" | custom-call | tf_op jit(solution)/shard_map/act/pallas_call | solution.py:710
  78.6 274.9 %main.1 = (bf16[8,256,640]{2,1,0:T(8,128)(2,1)}, bf16[16,256,640]{2,1,0:T(8,128)(2,1)}, f32[8,640]{1,0:T(8,128)}, f32[16,256,640]{2,1,0:T(8,128)}, bf16[16,256,6...) custom-call(bf16[16,256,640]{2,1,0:T(8,128)(2,1)} %get-tuple-element, ...), custom_call_target="tpu_custom_call" | custom-call | tf_op jit(solution)/shard_map/main/pallas_call | solution.py:600
  353.5 40.1 %finish.1 = (bf16[16,256,640]{2,1,0:T(8,128)(2,1)}, bf16[16,256,640]{2,1,0:T(8,128)(2,1)}, f32[5760,640]{1,0:T(8,128)}, f32[5760,640]{1,0:T(8,128)}) custom-call(bf16[16,256,640]{2,1,0:T(8,128)(2,1)} %get-tuple-element.31.z_ref, bf16[2,256,640]{2,1,0:T(8,128)(2,1)} %get-tuple-element.41.rows_ref, f32[18,1,640]{2,1,0:T(1,128)} %get-tuple-element.42.cl_ref, ...), custom_call_target="tpu_custom_call" | custom-call | tf_op jit(solution)/shard_map/finish/pallas_call | solution.py:679
  393.6 1.4 slice_reduce_fusion
  (3 shorter events, 0.0 us)

commit v9 on v8

--- a/solution.py
+++ b/solution.py
@@ -16,6 +16,7 @@
 VMEM_LIMIT = 67043328
 ANY = pl.BlockSpec(memory_space=pl.ANY)
 VM = pl.BlockSpec(memory_space=pltpu.VMEM)
+LAST = 4
 GELU_C = 0.7978845608028654
 GELU_A = 0.044715
 
@@ -40,12 +41,11 @@
     return 0.5 * (1.0 + t) + 0.5 * n * (1.0 - t * t) * (GELU_C * (1.0 + 3.0 * GELU_A * n2))
 
 
-def _exchange(nh, nw, arrays, send, recv):
-    th, tw, c = arrays[0][0].shape
+def _exchange(nh, nw, u, first, last, rows, cl, cr, send, recv):
+    th = u.shape[0]
     w = lax.axis_index("w")
     h = lax.axis_index("x") * 2 + lax.axis_index("c")
     dirs = [(dh, dw) for dh in (-1, 0, 1) for dw in (-1, 0, 1) if (dh, dw) != (0, 0)]
-    sends = [(k, i, dh, dw) for k in range(len(arrays)) for i, (dh, dw) in enumerate(dirs)]
 
     def dev(dh, dw):
         hh = h + dh
@@ -57,8 +57,7 @@
             ok = cond if ok is None else jnp.logical_and(ok, cond)
         return ok
 
-    def landing(k, dh, dw):
-        rows, cl, cr = arrays[k][3:]
+    def landing(dh, dw):
         side = cr if dw < 0 else cl
         if dw == 0:
             return rows, 1 if dh < 0 else 0
@@ -66,35 +65,34 @@
             return side, slice(1, th + 1)
         return side, th + 1 if dh < 0 else 0
 
-    def copy(k, i, dh, dw):
-        u, first, last = arrays[k][:3]
+    def copy(i, dh, dw):
         r = 0 if dh < 0 else th - 1
         edge = first if dw < 0 else last
         src = u.at[r] if dw == 0 else edge if dh == 0 else edge.at[r]
-        ref, at = landing(k, dh, dw)
-        return pltpu.make_async_remote_copy(src_ref=src, dst_ref=ref.at[at], send_sem=send.at[k * 8 + i], recv_sem=recv.at[k * 8 + i],
+        ref, at = landing(dh, dw)
+        return pltpu.make_async_remote_copy(src_ref=src, dst_ref=ref.at[at], send_sem=send.at[i], recv_sem=recv.at[i],
                                             device_id=dev(dh, dw), device_id_type=MESH)
 
     def start():
-        for k, i, dh, dw in sends:
+        for i, (dh, dw) in enumerate(dirs):
             @pl.when(has(dh, dw))
-            def _(k=k, i=i, dh=dh, dw=dw):
-                copy(k, i, dh, dw).start()
+            def _(i=i, dh=dh, dw=dw):
+                copy(i, dh, dw).start()
 
     def finish():
-        for k, i, dh, dw in sends:
+        for i, (dh, dw) in enumerate(dirs):
             @pl.when(jnp.logical_not(has(-dh, -dw)))
-            def _(k=k, dh=dh, dw=dw):
-                ref, at = landing(k, dh, dw)
+            def _(dh=dh, dw=dw):
+                ref, at = landing(dh, dw)
                 ref[at] = jnp.zeros(ref.at[at].shape, ref.dtype)
 
             @pl.when(has(dh, dw))
-            def _(k=k, i=i, dh=dh, dw=dw):
-                copy(k, i, dh, dw).wait_send()
+            def _(i=i, dh=dh, dw=dw):
+                copy(i, dh, dw).wait_send()
 
             @pl.when(has(-dh, -dw))
-            def _(k=k, i=i, dh=dh, dw=dw):
-                copy(k, i, dh, dw).wait_recv()
+            def _(i=i, dh=dh, dw=dw):
+                copy(i, dh, dw).wait_recv()
 
     return start, finish
 
@@ -181,6 +179,8 @@
     th, tw, c = x_ref.shape
     me, peers = _peers(nh, nw)
     last = th // 2
+    x_start, x_finish = _exchange(nh, nw, x_ref, x0_ref, x1_ref, *halo[:3], hsend.at[0], hrecv.at[0])
+    g_start, g_finish = _exchange(nh, nw, g_ref, g0_ref, g1_ref, *halo[3:], hsend.at[1], hrecv.at[1])
 
     @pl.when(i == 0)
     def _():
@@ -188,14 +188,12 @@
         wc = pltpu.make_async_copy(w_ref, wb, wsem)
         xc.start()
         wc.start()
-        start, finish = _exchange(nh, nw, [(x_ref, x0_ref, x1_ref, *halo[:3]), (g_ref, g0_ref, g1_ref, *halo[3:])], hsend, hrecv)
         _meet(peers)
-        start()
+        x_start()
+        g_start()
         _fill_same(same)
         sacc[...] = jnp.zeros_like(sacc)
-        finish()
-        for dst, src in zip(handed, halo):
-            dst[...] = src[...]
+        x_finish()
         xc.wait()
         _put_rows(p, halo[0])
         _shift_patches(p, halo[1], halo[2])
@@ -216,6 +214,9 @@
 
     @pl.when(i == last)
     def _():
+        g_finish()
+        for dst, src in zip(handed, halo):
+            dst[...] = src[...]
         m = _group_means(_sum_devices(me, peers, sacc, sbuf, ssend, srecv), same, cnt)
         mean = m[0:1]
         row = lax.broadcasted_iota(jnp.int32, m.shape, 0)
@@ -237,7 +238,7 @@
         + [jax.ShapeDtypeStruct(h, t) for h, t in zip(halo, types)],
         in_specs=[ANY] * 7 + [one, blk], out_specs=[pl.BlockSpec((c, 2 * tw), lambda i: (0, jnp.minimum(i, last))), blk, one] + [_whole(*h) for h in halo],
         scratch_shapes=[pltpu.VMEM((th + 2, tw, 3 * c), BF16), pltpu.VMEM(wshape, BF16)] + [pltpu.VMEM(h, t) for h, t in zip(halo, types)]
-        + [pltpu.VMEM((8, c), F32), pltpu.VMEM((n, 8, c), F32), pltpu.VMEM((c, c), BF16), dma, dma, dma((16,)), dma((16,)), dma((n,)), dma((n,))],
+        + [pltpu.VMEM((8, c), F32), pltpu.VMEM((n, 8, c), F32), pltpu.VMEM((c, c), BF16), dma, dma, dma((2, 8)), dma((2, 8)), dma((n,)), dma((n,))],
         compiler_params=pltpu.CompilerParams(dimension_semantics=("arbitrary",), vmem_limit_bytes=VMEM_LIMIT, collective_id=1, has_side_effects=True),
         name="conv1",
     )(x, *xe, g, *ge, w.reshape(wshape), par, g)
@@ -270,7 +271,7 @@
     for n in (nt, nb, nb, nt, nb, nb):
         starts.append(starts[-1] + n)
     late = [*range(2, 9), *range(10, 15, 2), *range(16, 25)]
-    return starts, [*range(2, 10), 11, 13, 16, 17, 20, 24, 26] + [starts[3] + s for s in late], 15
+    return starts, [*range(2, 11), *range(12, 17), 18, 20, 23, 25] + [starts[3] + s for s in late], 18
 
 
 def _main_kernel(nh, nw, cnt, z_ref, z0_ref, z1_ref, g_ref, gt_ref, grows, gcl, gcr, x_ref, xrows, xcl, xcr, w1_ref, w2_ref, st_ref, xb_ref, gb_ref, ab_ref,
@@ -338,13 +339,13 @@
         for cp in cps:
             cp.start()
 
-    def when_chunk(t, f):
-        one = jnp.logical_and(t >= 0, t < nt)
-        two = jnp.logical_and(t >= second, t < second + nt)
-
-        @pl.when(jnp.logical_or(one, two))
-        def _():
-            f(t)
+    def when_chunk(j, stages, f):
+        for first, lag in ((0, 3), (second, 2)):
+            t = j - stages * lag
+
+            @pl.when(jnp.logical_and(t >= first, t < first + nt))
+            def _(t=t):
+                f(t)
 
     def tick(j):
         def t2(t):
@@ -379,18 +380,15 @@
             for cp in s4(t) + s5(t):
                 cp.wait_send()
 
-        lag = 2
-        when_chunk(j, lambda t: start(s1(t)))
-        when_chunk(j - lag, t2)
-        when_chunk(j - 2 * lag, t3)
-        when_chunk(j - 3 * lag, t4)
-        when_chunk(j - 4 * lag, t5)
-        when_chunk(j - lag, lambda t: start(s2(t)))
-        when_chunk(j - 2 * lag, lambda t: start(s3(t) + keep(t)))
-        when_chunk(j - 5 * lag, t6)
-
-    z_start, z_finish = _exchange(nh, nw, [(z_ref, z0_ref, z1_ref, zrows, zcl, zcr)], zsend, zrecv)
-    a_start, a_finish = _exchange(nh, nw, [(da_ref, e0, e1, arows, acl, acr)], asend, arecv)
+        when_chunk(j, 0, lambda t: start(s1(t)))
+        for stages, f in enumerate((t2, t3, t4, t5)):
+            when_chunk(j, stages + 1, f)
+        when_chunk(j, 1, lambda t: start(s2(t)))
+        when_chunk(j, 2, lambda t: start(s3(t) + keep(t)))
+        when_chunk(j, 5, t6)
+
+    z_start, z_finish = _exchange(nh, nw, z_ref, z0_ref, z1_ref, zrows, zcl, zcr, zsend, zrecv)
+    a_start, a_finish = _exchange(nh, nw, da_ref, e0, e1, arows, acl, acr, asend, arecv)
 
     def wcp(ref):
         return pltpu.make_async_copy(ref, wb, wsem)
@@ -578,7 +576,7 @@
     def _():
         _ep_residual(conv(i - s_x, True), gb_ref, dx_ref)
 
-    @within(s_y, s_y + nb // 2)
+    @within(s_y, s_y + (th - LAST) // 2)
     def _():
         _ep_residual(conv(i - s_y, False), xb_ref, y_ref)
 
@@ -599,10 +597,10 @@
     n = nh * nw - 1
     return pl.pallas_call(
         functools.partial(_main_kernel, nh, nw, cnt), grid=(end,),
-        out_shape=[jax.ShapeDtypeStruct((nb, tw, c), BF16), img16, jax.ShapeDtypeStruct((8, c), F32), img32, img16, jax.ShapeDtypeStruct((2 * nt * c, c), F32)]
+        out_shape=[jax.ShapeDtypeStruct((th - LAST, tw, c), BF16), img16, jax.ShapeDtypeStruct((8, c), F32), img32, img16, jax.ShapeDtypeStruct((2 * nt * c, c), F32)]
         + [jax.ShapeDtypeStruct(h.shape, h.dtype) for h in gh],
-        in_specs=[ANY] * 6 + [full, full, ANY, ANY, full, full, ANY, ANY, one, blocks(s_y, nb // 2), blocks(s_x), blocks(s_z, 2 * nb)],
-        out_specs=[blocks(s_y, nb // 2), blocks(s_x), one] + [ANY] * 6,
+        in_specs=[ANY] * 6 + [full, full, ANY, ANY, full, full, ANY, ANY, one, blocks(s_y, (th - LAST) // 2), blocks(s_x), blocks(s_z, 2 * nb)],
+        out_specs=[blocks(s_y, (th - LAST) // 2), blocks(s_x), one] + [ANY] * 6,
         scratch_shapes=[pltpu.VMEM((th + 2, tw, 3 * c), BF16), pltpu.VMEM((c, th * tw), BF16), pltpu.VMEM((nt, c, c), BF16),
                         pltpu.VMEM((2, half, c), F32), pltpu.VMEM((nt, half, c), F32), pltpu.VMEM((2, half, c), F32),
                         pltpu.VMEM((nt, 2, c // 8, c), F32), pltpu.VMEM((nt, 2, c // 16, c), F32),
@@ -619,45 +617,57 @@
     i = pl.program_id(0)
     steps = pl.num_programs(0)
     th, tw, c = z_ref.shape
-    r0 = th // 2
-    n = th - r0 + 1
+    r0 = th - LAST
+    wait = steps - LAST
+    n = y0_ref.shape[0]
+    cps = [pltpu.make_async_copy(z_ref.at[r0 - 1:], p.at[:LAST + 1, :, c:2 * c], psem.at[0]),
+           pltpu.make_async_copy(rows_ref.at[1], p.at[LAST + 1, :, c:2 * c], psem.at[1]), pltpu.make_async_copy(w_ref, wb, wsem)]
+    ycopy = pltpu.make_async_copy(y0_ref, y_ref.at[pl.ds(i * n, n)], csem)
 
     def yout(k):
         return pltpu.make_async_copy(yb.at[lax.rem(k, 2)], y_ref.at[r0 + k], ysem.at[lax.rem(k, 2)])
 
-    ycopy = pltpu.make_async_copy(y0_ref.at[0], y_ref.at[i], csem)
-    ycopy.start()
-
     @pl.when(i == 0)
     def _():
-        cps = [pltpu.make_async_copy(z_ref.at[r0 - 1:], p.at[:n, :, c:2 * c], psem.at[0]),
-               pltpu.make_async_copy(rows_ref.at[1], p.at[n, :, c:2 * c], psem.at[1])]
-        wc = pltpu.make_async_copy(w_ref, wb, wsem)
-        for cp in cps + [wc]:
+        for cp in cps:
             cp.start()
+
+    @pl.when(i == wait)
+    def _():
         for cp in cps:
             cp.wait()
         _shift_patches(p, cl_ref, cr_ref, r0)
-        wc.wait()
-
-    @pl.when(i > 1)
-    def _():
-        yout(i - 2).wait()
+
+    @pl.when(i < wait)
+    def _():
+        ycopy.start()
 
     for src, dst in ((dx0_ref, dx_ref), (d1_ref, dw1_ref), (d2_ref, dw2_ref)):
         dst[...] = src[...]
-    acc = None
-    for a in range(3):
-        d = jnp.dot(p[i + a], wb[a], preferred_element_type=F32)
-        acc = d if acc is None else acc + d
-    yb[lax.rem(i, 2)] = (acc + xb_ref[0].astype(F32)).astype(BF16)
-    yout(i).start()
-    ycopy.wait()
+
+    @pl.when(i < wait)
+    def _():
+        ycopy.wait()
+
+    @pl.when(i >= wait)
+    def _():
+        k = i - wait
+
+        @pl.when(k > 1)
+        def _():
+            yout(k - 2).wait()
+
+        acc = None
+        for a in range(3):
+            d = jnp.dot(p[k + a], wb[a], preferred_element_type=F32)
+            acc = d if acc is None else acc + d
+        yb[lax.rem(k, 2)] = (acc + xb_ref[0].astype(F32)).astype(BF16)
+        yout(k).start()
 
     @pl.when(i == steps - 1)
     def _():
-        yout(i - 1).wait()
-        yout(i).wait()
+        yout(LAST - 2).wait()
+        yout(LAST - 1).wait()
 
 
 def _finish(z, zh, w, x, y0, dx0, d):
@@ -671,15 +681,18 @@
     def part(k):
         return pl.BlockSpec((rows, c), lambda i: (i + k, 0))
 
-    def img(n, k=0):
-        return pl.BlockSpec((n, tw, c), lambda i: (i + k, 0, 0))
+    def img(n, at=lambda i: i):
+        return pl.BlockSpec((n, tw, c), lambda i: (at(i), 0, 0))
+
+    wait = steps - LAST
+    y0_spec, x_spec = img((th - LAST) // wait, lambda i: jnp.minimum(i, wait - 1)), img(1, lambda i: th - LAST + jnp.maximum(i - wait, 0))
 
     wout = jax.ShapeDtypeStruct((d.shape[0] // 2, c), F32)
     iout = jax.ShapeDtypeStruct((th, tw, c), BF16)
     return pl.pallas_call(
         _finish_kernel, grid=(steps,), out_shape=[iout, iout, wout, wout],
-        in_specs=[ANY, ANY, full, full, ANY, img(1, steps), img(1), img(2), part(steps), part(0)], out_specs=[ANY, img(2), part(0), part(0)],
-        scratch_shapes=[pltpu.VMEM((steps + 2, tw, 3 * c), BF16), pltpu.VMEM(wshape, BF16), pltpu.VMEM((2, tw, c), BF16), dma((2,)), dma, dma((2,)), dma],
+        in_specs=[ANY, ANY, full, full, ANY, x_spec, y0_spec, img(2), part(steps), part(0)], out_specs=[ANY, img(2), part(0), part(0)],
+        scratch_shapes=[pltpu.VMEM((LAST + 2, tw, 3 * c), BF16), pltpu.VMEM(wshape, BF16), pltpu.VMEM((2, tw, c), BF16), dma((2,)), dma, dma((2,)), dma],
         compiler_params=pltpu.CompilerParams(dimension_semantics=("arbitrary",), vmem_limit_bytes=VMEM_LIMIT), name="finish",
     )(z, *zh, w.reshape(wshape), x, y0, dx0, d, d)
 

time: 396 us -> 398 us (level)
    pallas_call x1, Pallas kernels: 275 us -> 285 us  [_main(): pl.pallas_call(functools.partial(_main_kernel, nh, nw, cnt), grid=(end,),...]
    pallas_call x1, Pallas kernels: 40.1 us -> 35.7 us  [_finish(): pl.pallas_call(_finish_kernel, grid=(steps,), out_shape=[iout, iout, wout...]
where the time goes in v9:
time: 398 us; the launch traced here: 397 us
  Pallas kernels  391 us (98%)
    pallas_call x1, Pallas kernels, _main(): pl.pallas_call(functools.partial(_main_kernel, nh, nw, cnt), grid=(end,),...  285 us
    pallas_call x1, Pallas kernels, _conv(): pl.pallas_call(functools.partial(_conv_kernel, nh, nw, cnt), grid=(th //...  61.1 us
    pallas_call x1, Pallas kernels, _finish(): pl.pallas_call(_finish_kernel, grid=(steps,), out_shape=[iout, iout, wout...  35.7 us
    pallas_call x1, Pallas kernels, body(): pl.pallas_call(_z_kernel, grid=(th // rb,), out_shape=[img16, edge, edge]...  9.29 us

profile of v9, /device:TPU:0, one launch (start us, length us, event | category | flops | bytes accessed | tf_op | source)
XLA Modules:
  0.0 397.2 jit_solution(9710432191452103720)
XLA Ops:
  0.6 0.1 pad.3.clone
  0.7 0.7 broadcast_in_dim.19
  1.4 0.7 broadcast_in_dim.20
  2.1 0.7 maximum_maximum_fusion.par_ref
  2.8 1.9 slice_convert_fusion
  4.7 61.1 %conv1.1 = (bf16[640,4096]{1,0:T(8,128)(2,1)}, bf16[16,256,640]{2,1,0:T(8,128)(2,1)}, f32[8,640]{1,0:T(8,128)}, bf16[2,256,640]{2,1,0:T(8,128)(2,1)}, f32[18,1,6...) custom-call(bf16[16,256,640]{2,1,0:T(8,128)(2,1)} %bitcast.11, ...), custom_call_target="tpu_custom_call" | custom-call | tf_op jit(solution)/shard_map/conv1/pallas_call | solution.py:235
  65.8 9.3 %act.1 = (bf16[16,256,640]{2,1,0:T(8,128)(2,1)}, f32[16,1,640]{2,1,0:T(1,128)}, f32[16,1,640]{2,1,0:T(1,128)}) custom-call(bf16[16,256,640]{2,1,0:T(8,128)(2,1)} %get-tuple-element.29.a_ref.ab_ref, f32[8,640]{1,0:T(8,128)} %get-tuple-element.30.st_ref), custom_call_target="tpu_custom_call" | custom-call | tf_op jit(solution)/shard_map/act/pallas_call | solution.py:723
  75.1 284.9 %main.1 = (bf16[12,256,640]{2,1,0:T(8,128)(2,1)}, bf16[16,256,640]{2,1,0:T(8,128)(2,1)}, f32[8,640]{1,0:T(8,128)}, f32[16,256,640]{2,1,0:T(8,128)}, bf16[16,256,...) custom-call(bf16[16,256,640]{2,1,0:T(8,128)(2,1)} %get-tuple-element, ...), custom_call_target="tpu_custom_call" | custom-call | tf_op jit(solution)/shard_map/main/pallas_call | solution.py:598
  360.0 35.7 %finish.1 = (bf16[16,256,640]{2,1,0:T(8,128)(2,1)}, bf16[16,256,640]{2,1,0:T(8,128)(2,1)}, f32[5760,640]{1,0:T(8,128)}, f32[5760,640]{1,0:T(8,128)}) custom-call(bf16[16,256,640]{2,1,0:T(8,128)(2,1)} %get-tuple-element.31.z_ref, bf16[2,256,640]{2,1,0:T(8,128)(2,1)} %get-tuple-element.41.rows_ref, f32[18,1,640]{2,1,0:T(1,128)} %get-tuple-element.42.cl_ref, ...), custom_call_target="tpu_custom_call" | custom-call | tf_op jit(solution)/shard_map/finish/pallas_call | solution.py:692
  395.7 1.4 slice_reduce_fusion
  (3 shorter events, 0.0 us)

commit v10 on v9

--- a/solution.py
+++ b/solution.py
@@ -16,7 +16,7 @@
 VMEM_LIMIT = 67043328
 ANY = pl.BlockSpec(memory_space=pl.ANY)
 VM = pl.BlockSpec(memory_space=pltpu.VMEM)
-LAST = 4
+LAST = 8
 GELU_C = 0.7978845608028654
 GELU_A = 0.044715
 
@@ -455,7 +455,7 @@
     def _():
         for k in range(2):
             dn_out(nb - 2 + k).wait()
-        start([dn_in(0), middle(x_ref), wcp(w1_ref)] + given(xrows))
+        start([dn_in(0), dn_in(1), middle(x_ref), wcp(w1_ref)] + given(xrows))
         total = _sum_devices(me, peers, sacc, sbuf, ssend, srecv)
         u = _group_means(total * _params(st_ref)[2], same, cnt)
         row = lax.broadcasted_iota(jnp.int32, total.shape, 0)
@@ -554,10 +554,6 @@
     def _():
         k = i - s_a
 
-        @pl.when(k + 1 < nb)
-        def _():
-            dn_in(k + 1).start()
-
         @pl.when(k > 1)
         def _():
             da_out(k - 2).wait()
@@ -568,6 +564,11 @@
         xhat = (ab_ref[...].astype(F32) - mean) * rstd
         da = (rstd * (dnb[lax.rem(k, 2)] * gamma - u1 - xhat * u0)).astype(BF16)
         dab[lax.rem(k, 2)] = da
+
+        @pl.when(k + 2 < nb)
+        def _():
+            dn_in(k + 2).start()
+
         _edges(da.astype(F32), e0.at[pl.ds(2 * k, 2)], e1.at[pl.ds(2 * k, 2)])
         vt[:, pl.ds(pl.multiple_of(2 * k * tw, 2 * tw), 2 * tw)] = _transposed(da)
         da_out(k).start()
@@ -618,62 +619,50 @@
     steps = pl.num_programs(0)
     th, tw, c = z_ref.shape
     r0 = th - LAST
-    wait = steps - LAST
-    n = y0_ref.shape[0]
-    cps = [pltpu.make_async_copy(z_ref.at[r0 - 1:], p.at[:LAST + 1, :, c:2 * c], psem.at[0]),
-           pltpu.make_async_copy(rows_ref.at[1], p.at[LAST + 1, :, c:2 * c], psem.at[1]), pltpu.make_async_copy(w_ref, wb, wsem)]
-    ycopy = pltpu.make_async_copy(y0_ref, y_ref.at[pl.ds(i * n, n)], csem)
+    n = LAST + 1
 
     def yout(k):
         return pltpu.make_async_copy(yb.at[lax.rem(k, 2)], y_ref.at[r0 + k], ysem.at[lax.rem(k, 2)])
 
+    ycopy = pltpu.make_async_copy(y0_ref.at[0], y_ref.at[i], csem)
+    ycopy.start()
+
     @pl.when(i == 0)
     def _():
-        for cp in cps:
+        cps = [pltpu.make_async_copy(z_ref.at[r0 - 1:], p.at[:n, :, c:2 * c], psem.at[0]),
+               pltpu.make_async_copy(rows_ref.at[1], p.at[n, :, c:2 * c], psem.at[1])]
+        wc = pltpu.make_async_copy(w_ref, wb, wsem)
+        for cp in cps + [wc]:
             cp.start()
-
-    @pl.when(i == wait)
-    def _():
         for cp in cps:
             cp.wait()
         _shift_patches(p, cl_ref, cr_ref, r0)
-
-    @pl.when(i < wait)
-    def _():
-        ycopy.start()
+        wc.wait()
+
+    @pl.when(i > 1)
+    def _():
+        yout(i - 2).wait()
 
     for src, dst in ((dx0_ref, dx_ref), (d1_ref, dw1_ref), (d2_ref, dw2_ref)):
         dst[...] = src[...]
-
-    @pl.when(i < wait)
-    def _():
-        ycopy.wait()
-
-    @pl.when(i >= wait)
-    def _():
-        k = i - wait
-
-        @pl.when(k > 1)
-        def _():
-            yout(k - 2).wait()
-
-        acc = None
-        for a in range(3):
-            d = jnp.dot(p[k + a], wb[a], preferred_element_type=F32)
-            acc = d if acc is None else acc + d
-        yb[lax.rem(k, 2)] = (acc + xb_ref[0].astype(F32)).astype(BF16)
-        yout(k).start()
+    acc = None
+    for a in range(3):
+        d = jnp.dot(p[i + a], wb[a], preferred_element_type=F32)
+        acc = d if acc is None else acc + d
+    yb[lax.rem(i, 2)] = (acc + xb_ref[0].astype(F32)).astype(BF16)
+    yout(i).start()
+    ycopy.wait()
 
     @pl.when(i == steps - 1)
     def _():
-        yout(LAST - 2).wait()
-        yout(LAST - 1).wait()
+        yout(i - 1).wait()
+        yout(i).wait()
 
 
 def _finish(z, zh, w, x, y0, dx0, d):
     th, tw, c = x.shape
-    steps = th // 2
-    rows = d.shape[0] // th
+    steps = LAST
+    rows = d.shape[0] // 2 // steps
     wshape = (3, 3 * c, c)
     dma = pltpu.SemaphoreType.DMA
     full = _whole(th + 2, 1, c)
@@ -681,18 +670,15 @@
     def part(k):
         return pl.BlockSpec((rows, c), lambda i: (i + k, 0))
 
-    def img(n, at=lambda i: i):
-        return pl.BlockSpec((n, tw, c), lambda i: (at(i), 0, 0))
-
-    wait = steps - LAST
-    y0_spec, x_spec = img((th - LAST) // wait, lambda i: jnp.minimum(i, wait - 1)), img(1, lambda i: th - LAST + jnp.maximum(i - wait, 0))
+    def img(n, k=0):
+        return pl.BlockSpec((n, tw, c), lambda i: (i + k, 0, 0))
 
     wout = jax.ShapeDtypeStruct((d.shape[0] // 2, c), F32)
     iout = jax.ShapeDtypeStruct((th, tw, c), BF16)
     return pl.pallas_call(
         _finish_kernel, grid=(steps,), out_shape=[iout, iout, wout, wout],
-        in_specs=[ANY, ANY, full, full, ANY, x_spec, y0_spec, img(2), part(steps), part(0)], out_specs=[ANY, img(2), part(0), part(0)],
-        scratch_shapes=[pltpu.VMEM((LAST + 2, tw, 3 * c), BF16), pltpu.VMEM(wshape, BF16), pltpu.VMEM((2, tw, c), BF16), dma((2,)), dma, dma((2,)), dma],
+        in_specs=[ANY, ANY, full, full, ANY, img(1, steps), img(1), img(2), part(steps), part(0)], out_specs=[ANY, img(2), part(0), part(0)],
+        scratch_shapes=[pltpu.VMEM((steps + 2, tw, 3 * c), BF16), pltpu.VMEM(wshape, BF16), pltpu.VMEM((2, tw, c), BF16), dma((2,)), dma, dma((2,)), dma],
         compiler_params=pltpu.CompilerParams(dimension_semantics=("arbitrary",), vmem_limit_bytes=VMEM_LIMIT), name="finish",
     )(z, *zh, w.reshape(wshape), x, y0, dx0, d, d)
 

time: 398 us -> 394 us (0.990)
  Pallas kernels: 391 us -> 387 us
    pallas_call x1, Pallas kernels: 285 us -> 277 us  [_main(): pl.pallas_call(functools.partial(_main_kernel, nh, nw, cnt), grid=(end,),...]
    pallas_call x1, Pallas kernels: 35.7 us -> 40 us  [_finish(): pl.pallas_call(_finish_kernel, grid=(steps,), out_shape=[iout, iout, wout...]
where the time goes in v10:
time: 394 us; the launch traced here: 393 us
  Pallas kernels  387 us (98%)
    pallas_call x1, Pallas kernels, _main(): pl.pallas_call(functools.partial(_main_kernel, nh, nw, cnt), grid=(end,),...  277 us
    pallas_call x1, Pallas kernels, _conv(): pl.pallas_call(functools.partial(_conv_kernel, nh, nw, cnt), grid=(th //...  61.1 us
    pallas_call x1, Pallas kernels, _finish(): pl.pallas_call(_finish_kernel, grid=(steps,), out_shape=[iout, iout, wout...  40 us
    pallas_call x1, Pallas kernels, body(): pl.pallas_call(_z_kernel, grid=(th // rb,), out_shape=[img16, edge, edge]...  9.29 us

profile of v10, /device:TPU:0, one launch (start us, length us, event | category | flops | bytes accessed | tf_op | source)
XLA Modules:
  0.0 393.3 jit_solution(2900669075847366294)
XLA Ops:
  0.6 0.1 pad.3.clone
  0.7 0.7 broadcast_in_dim.19
  1.4 0.7 broadcast_in_dim.20
  2.1 0.7 maximum_maximum_fusion.par_ref
  2.8 1.9 slice_convert_fusion
  4.7 61.1 %conv1.1 = (bf16[640,4096]{1,0:T(8,128)(2,1)}, bf16[16,256,640]{2,1,0:T(8,128)(2,1)}, f32[8,640]{1,0:T(8,128)}, bf16[2,256,640]{2,1,0:T(8,128)(2,1)}, f32[18,1,6...) custom-call(bf16[16,256,640]{2,1,0:T(8,128)(2,1)} %bitcast.11, ...), custom_call_target="tpu_custom_call" | custom-call | tf_op jit(solution)/shard_map/conv1/pallas_call | solution.py:235
  65.8 9.3 %act.1 = (bf16[16,256,640]{2,1,0:T(8,128)(2,1)}, f32[16,1,640]{2,1,0:T(1,128)}, f32[16,1,640]{2,1,0:T(1,128)}) custom-call(bf16[16,256,640]{2,1,0:T(8,128)(2,1)} %get-tuple-element.29.a_ref.ab_ref, f32[8,640]{1,0:T(8,128)} %get-tuple-element.30.st_ref), custom_call_target="tpu_custom_call" | custom-call | tf_op jit(solution)/shard_map/act/pallas_call | solution.py:709
  75.1 276.7 %main.1 = (bf16[8,256,640]{2,1,0:T(8,128)(2,1)}, bf16[16,256,640]{2,1,0:T(8,128)(2,1)}, f32[8,640]{1,0:T(8,128)}, f32[16,256,640]{2,1,0:T(8,128)}, bf16[16,256,6...) custom-call(bf16[16,256,640]{2,1,0:T(8,128)(2,1)} %get-tuple-element, ...), custom_call_target="tpu_custom_call" | custom-call | tf_op jit(solution)/shard_map/main/pallas_call | solution.py:599
  351.9 40.0 %finish.1 = (bf16[16,256,640]{2,1,0:T(8,128)(2,1)}, bf16[16,256,640]{2,1,0:T(8,128)(2,1)}, f32[5760,640]{1,0:T(8,128)}, f32[5760,640]{1,0:T(8,128)}) custom-call(bf16[16,256,640]{2,1,0:T(8,128)(2,1)} %get-tuple-element.31.z_ref, bf16[2,256,640]{2,1,0:T(8,128)(2,1)} %get-tuple-element.41.rows_ref, f32[18,1,640]{2,1,0:T(1,128)} %get-tuple-element.42.cl_ref, ...), custom_call_target="tpu_custom_call" | custom-call | tf_op jit(solution)/shard_map/finish/pallas_call | solution.py:678
  391.9 1.4 slice_reduce_fusion
  (3 shorter events, 0.0 us)

commit v11 on v10

--- a/solution.py
+++ b/solution.py
@@ -271,7 +271,7 @@
     for n in (nt, nb, nb, nt, nb, nb):
         starts.append(starts[-1] + n)
     late = [*range(2, 9), *range(10, 15, 2), *range(16, 25)]
-    return starts, [*range(2, 11), *range(12, 17), 18, 20, 23, 25] + [starts[3] + s for s in late], 18
+    return starts, [*range(2, 10), 11, 13, 16, 17, 20, 24, 26] + [starts[3] + s for s in late], 15
 
 
 def _main_kernel(nh, nw, cnt, z_ref, z0_ref, z1_ref, g_ref, gt_ref, grows, gcl, gcr, x_ref, xrows, xcl, xcr, w1_ref, w2_ref, st_ref, xb_ref, gb_ref, ab_ref,
@@ -340,7 +340,7 @@
             cp.start()
 
     def when_chunk(j, stages, f):
-        for first, lag in ((0, 3), (second, 2)):
+        for first, lag in ((0, 2), (second, 2)):
             t = j - stages * lag
 
             @pl.when(jnp.logical_and(t >= first, t < first + nt))

time: 394 us -> 392 us (level)
  no operation moved by 1% of the time
where the time goes in v11:
time: 392 us
  Pallas kernels  385 us (98%)
    pallas_call x1, Pallas kernels, _main(): pl.pallas_call(functools.partial(_main_kernel, nh, nw, cnt), grid=(end,),...  275 us
    pallas_call x1, Pallas kernels, _conv(): pl.pallas_call(functools.partial(_conv_kernel, nh, nw, cnt), grid=(th //...  61.1 us
    pallas_call x1, Pallas kernels, _finish(): pl.pallas_call(_finish_kernel, grid=(steps,), out_shape=[iout, iout, wout...  40 us
    pallas_call x1, Pallas kernels, body(): pl.pallas_call(_z_kernel, grid=(th // rb,), out_shape=[img16, edge, edge]...  9.29 us

profile of v11, /device:TPU:0, one launch (start us, length us, event | category | flops | bytes accessed | tf_op | source)
XLA Modules:
  0.0 391.6 jit_solution(17292885919540393540)
XLA Ops:
  0.6 0.1 pad.3.clone
  0.7 0.7 broadcast_in_dim.19
  1.4 0.7 broadcast_in_dim.20
  2.1 0.7 maximum_maximum_fusion.par_ref
  2.8 1.9 slice_convert_fusion
  4.7 61.1 %conv1.1 = (bf16[640,4096]{1,0:T(8,128)(2,1)}, bf16[16,256,640]{2,1,0:T(8,128)(2,1)}, f32[8,640]{1,0:T(8,128)}, bf16[2,256,640]{2,1,0:T(8,128)(2,1)}, f32[18,1,6...) custom-call(bf16[16,256,640]{2,1,0:T(8,128)(2,1)} %bitcast.11, ...), custom_call_target="tpu_custom_call" | custom-call | tf_op jit(solution)/shard_map/conv1/pallas_call | solution.py:235
  65.8 9.3 %act.1 = (bf16[16,256,640]{2,1,0:T(8,128)(2,1)}, f32[16,1,640]{2,1,0:T(1,128)}, f32[16,1,640]{2,1,0:T(1,128)}) custom-call(bf16[16,256,640]{2,1,0:T(8,128)(2,1)} %get-tuple-element.29.a_ref.ab_ref, f32[8,640]{1,0:T(8,128)} %get-tuple-element.30.st_ref), custom_call_target="tpu_custom_call" | custom-call | tf_op jit(solution)/shard_map/act/pallas_call | solution.py:709
  75.1 275.0 %main.1 = (bf16[8,256,640]{2,1,0:T(8,128)(2,1)}, bf16[16,256,640]{2,1,0:T(8,128)(2,1)}, f32[8,640]{1,0:T(8,128)}, f32[16,256,640]{2,1,0:T(8,128)}, bf16[16,256,6...) custom-call(bf16[16,256,640]{2,1,0:T(8,128)(2,1)} %get-tuple-element, ...), custom_call_target="tpu_custom_call" | custom-call | tf_op jit(solution)/shard_map/main/pallas_call | solution.py:599
  350.1 40.0 %finish.1 = (bf16[16,256,640]{2,1,0:T(8,128)(2,1)}, bf16[16,256,640]{2,1,0:T(8,128)(2,1)}, f32[5760,640]{1,0:T(8,128)}, f32[5760,640]{1,0:T(8,128)}) custom-call(bf16[16,256,640]{2,1,0:T(8,128)(2,1)} %get-tuple-element.31.z_ref, bf16[2,256,640]{2,1,0:T(8,128)(2,1)} %get-tuple-element.41.rows_ref, f32[18,1,640]{2,1,0:T(1,128)} %get-tuple-element.42.cl_ref, ...), custom_call_target="tpu_custom_call" | custom-call | tf_op jit(solution)/shard_map/finish/pallas_call | solution.py:678
  390.1 1.4 slice_reduce_fusion
  (3 shorter events, 0.0 us)
